TPU v7x, 128 devices: a whole 4x4x4 slice. The times are simulated.
128 devices in a mesh: group: 16 (over x, z_lo, core), head: 8 (over y, z_hi).
Axes of the slice: x: 4, y: 4, z: 4 (z_hi: 2, z_lo: 2; z = z_hi * 2 + z_lo), core: 2. Of those that a mesh axis runs over, the one named last changes fastest.
Arguments:
- hidden_in: bfloat16 [256, 2560], P('group'), may hold values from -6 to 6
- ssm_state: float32 [256, 80, 64, 128], P('group', 'head'), may hold values from -6 to 6
- conv_x_state: bfloat16 [256, 3, 5120], P('group', None, 'head'), may hold values from -6 to 6
- conv_bc_state: bfloat16 [256, 3, 256], P('group'), may hold values from -6 to 6
- token_ids: int32 [256], P('group'), may hold values from 0 to 25599
- ref_logits: bfloat16 [256, 25600], P('group', 'head'), may hold values from -15 to 350
- in_z: bfloat16 [2560, 5120], P('group', 'head'), may hold values from -0.125 to 0.125
- in_x: bfloat16 [2560, 5120], P('group', 'head'), may hold values from -0.125 to 0.125
- in_bc: bfloat16 [2560, 256], P('group'), may hold values from -0.125 to 0.125
- in_dt: bfloat16 [2560, 80], P('group', 'head'), may hold values from -0.125 to 0.125
- out_t: bfloat16 [2560, 5120], P('group', 'head'), may hold values from -0.078125 to 0.078125
- lm_head: bfloat16 [25600, 2560], P('head', 'group'), may hold values from -6 to 6
- conv_wx: float32 [4, 5120], P(None, 'head'), may hold values from -3 to 3
- conv_bx: float32 [5120], P('head'), may hold values from -1.5 to 1.5
- conv_wbc: float32 [4, 256], replicated, may hold values from -3 to 3
- conv_bbc: float32 [256], replicated, may hold values from -1.5 to 1.5
- dt_bias: float32 [80], P('head'), may hold values from -4 to -1
- a_log: float32 [80], P('head'), may hold values from 0 to 2.77
- skip_gain: float32 [80], P('head'), may hold values from 0.5 to 1.5
- norm_in: float32 [2560], replicated, may hold values from 0.5 to 1.5
- norm_gain: float32 [5120], P('head'), may hold values from 0.5 to 1.5
- final_gain: float32 [2560], replicated, may hold values from 0.5 to 1.5
Outputs:
- new_state: float32 [256, 80, 64, 128], P('group', 'head')
- divergence: float32 [256], P('group')
- token_logprob: float32 [256], P('group')
- roll_z: bfloat16 [2560, 5120], P(None, 'head')
- roll_x: bfloat16 [2560, 5120], P(None, 'head')
- roll_bc: bfloat16 [2560, 256], replicated
- roll_dt: bfloat16 [2560, 80], P(None, 'head')
- roll_out: bfloat16 [2560, 5120], P(None, 'head')
All inputs are finite; a program needn't handle non-finite values.
Results may differ from a plain program's by a relative error of at most 0.0102.
Values may be sent and summed in bfloat16 or wider, within the bound.
No kernel may reach another device: no remote copies, remote signals or barrier semaphores. Data moves between devices by JAX's collectives and lax.ppermute only.
A program may use at most 128 MiB of HBM per device.

v0:
```python
import jax
import jax.numpy as jnp
from jax import lax
from jax.sharding import PartitionSpec as P

P_SIZE = 64


EPSILON = 1e-05


def sent_together(arrays, axis, dim, along):
    both = jnp.concatenate(arrays, axis=along)
    result, at, done = (lax.all_gather(both, axis, axis=dim, tiled=True), 0, [])
    for a in arrays:
        done.append(lax.slice_in_dim(result, at, at + a.shape[along], axis=along))
        at += a.shape[along]
    return tuple(done)


def from_everyone(array, axis):
    peers = lax.axis_size(axis)
    return lax.all_to_all(
        jnp.broadcast_to(array[None], (peers, *array.shape)), axis, 0, 0, tiled=True
    )


def taken_together(array, axis):
    everything = from_everyone(array, axis)
    return jnp.sum(everything, axis=0)


def collected_together(array, axis):
    leaves = jax.tree.leaves(array)
    sequence = sorted(range(len(leaves)), key=lambda k: -leaves[k].size)
    width = (1, *leaves[sequence[0]].shape)[-1]
    lines = [
        jnp.pad(leaves[k].reshape(-1), (0, -leaves[k].size % width)).reshape(-1, width)
        for k in sequence
    ]
    both, at, found = (from_everyone(jnp.concatenate(lines), axis), 0, {})
    for k, line in zip(sequence, lines):
        piece = both[:, at : at + len(line)].reshape(len(both), -1)
        found[k] = piece[:, : leaves[k].size].reshape(-1, *leaves[k].shape)
        at += len(line)
    numbers = iter(range(len(leaves)))
    return jax.tree.map(lambda _: found[next(numbers)], array)


def folded_in_pairs(pieces, combine):
    while len(jax.tree.leaves(pieces)[0]) > 1:
        pieces = jax.vmap(combine)(
            *(jax.tree.map(lambda part: part[side::2], pieces) for side in (0, 1))
        )
    return jax.tree.map(lambda part: part[0], pieces)


def combined_all(array, axis, combine):
    pieces = collected_together(array, axis)
    return folded_in_pairs(pieces, combine)


def rms_norm(values, gain):
    return values * lax.rsqrt(jnp.mean(values * values, axis=-1, keepdims=True) + EPSILON) * gain


def causal_conv(history, newest, taps, offset):
    window = jnp.concatenate([history, newest[:, None, :]], axis=1).astype(jnp.float32)
    return jax.nn.silu(jnp.sum(window * taps[None, :, :], axis=1) + offset)


def combine_stats(first, second):
    roll_max = jnp.maximum(first[0], second[0])
    roll_sum = first[1] * jnp.exp(first[0] - roll_max) + second[1] * jnp.exp(second[0] - roll_max)
    ref_max = jnp.maximum(first[2], second[2])
    scale_first = jnp.exp(first[2] - ref_max)
    scale_second = jnp.exp(second[2] - ref_max)
    ref_sum = first[3] * scale_first + second[3] * scale_second
    cross_sum = first[4] * scale_first + second[4] * scale_second
    return (roll_max, roll_sum, ref_max, ref_sum, cross_sum, first[5] + second[5])


def shards(
    hidden_in,
    ssm_state,
    conv_x_state,
    conv_bc_state,
    token_ids,
    ref_logits,
    in_z,
    in_x,
    in_bc,
    in_dt,
    out_t,
    lm_head,
    conv_wx,
    conv_bx,
    conv_wbc,
    conv_bbc,
    dt_bias,
    a_log,
    skip_gain,
    norm_in,
    norm_gain,
    final_gain,
):
    roll_z, roll_x, roll_bc, roll_dt, roll_out = sent_together(
        (in_z, in_x, in_bc, in_dt, out_t), "group", 0, 1
    )
    stream_in = hidden_in.astype(jnp.float32)
    normed = rms_norm(stream_in, norm_in).astype(jnp.bfloat16)
    gate_branch = jnp.dot(normed, roll_z, preferred_element_type=jnp.float32).astype(jnp.bfloat16)
    x_branch = jnp.dot(normed, roll_x, preferred_element_type=jnp.float32).astype(jnp.bfloat16)
    bc_branch = jnp.dot(normed, roll_bc, preferred_element_type=jnp.float32).astype(jnp.bfloat16)
    step_raw = jnp.dot(normed, roll_dt, preferred_element_type=jnp.float32).astype(jnp.bfloat16)
    x_conv = causal_conv(conv_x_state, x_branch, conv_wx, conv_bx)
    bc_conv = causal_conv(conv_bc_state, bc_branch, conv_wbc, conv_bbc)
    state_size = bc_conv.shape[1] // 2
    b_vals = bc_conv[:, :state_size]
    c_vals = bc_conv[:, state_size:]
    step = jax.nn.softplus(step_raw.astype(jnp.float32) + dt_bias)
    decay = jnp.exp(-step * jnp.exp(a_log))
    seq_count = x_conv.shape[0]
    local_heads = a_log.shape[0]
    x_heads = x_conv.reshape(seq_count, local_heads, P_SIZE)
    inflow = (step[:, :, None] * x_heads)[:, :, :, None] * b_vals[:, None, None, :]
    new_state = decay[:, :, None, None] * ssm_state + inflow
    ssm_out = jnp.einsum("shpn,sn->shp", new_state, c_vals)
    ssm_out = (ssm_out + skip_gain[None, :, None] * x_heads).reshape(
        seq_count, local_heads * P_SIZE
    )
    gated = ssm_out * jax.nn.silu(gate_branch.astype(jnp.float32))
    square_total = taken_together(jnp.sum(gated * gated, axis=-1), "head")
    inner_width = gated.shape[1] * lax.axis_size("head")
    gated_out = (
        gated * lax.rsqrt(square_total / inner_width + EPSILON)[:, None] * norm_gain
    ).astype(jnp.bfloat16)
    partial_mix = lax.dot_general(
        gated_out, roll_out, (((1,), (1,)), ((), ())), preferred_element_type=jnp.float32
    )
    mixed = taken_together(partial_mix, "head")
    final_hidden = rms_norm(stream_in + mixed, final_gain).astype(jnp.bfloat16)
    vocab_local = lm_head.shape[0]
    logits = lax.dot_general(
        final_hidden,
        lax.all_gather(lm_head, "group", axis=1, tiled=True),
        (((1,), (1,)), ((), ())),
        preferred_element_type=jnp.float32,
    )
    reference_rows = ref_logits.astype(jnp.float32)
    column_ids = lax.axis_index("head") * vocab_local + lax.broadcasted_iota(
        jnp.int32, (1, vocab_local), 1
    )
    picked_part = jnp.sum(jnp.where(column_ids == token_ids[:, None], logits, 0.0), axis=-1)
    roll_local = jnp.max(logits, axis=-1)
    ref_local = jnp.max(reference_rows, axis=-1)
    roll_sum = jnp.sum(jnp.exp(logits - roll_local[:, None]), axis=-1)
    ref_weights = jnp.exp(reference_rows - ref_local[:, None])
    ref_sum = jnp.sum(ref_weights, axis=-1)
    cross_sum = jnp.sum(ref_weights * (reference_rows - logits), axis=-1)
    roll_max, roll_sum, ref_max, ref_sum, cross_sum, picked = combined_all(
        (roll_local, roll_sum, ref_local, ref_sum, cross_sum, picked_part), "head", combine_stats
    )
    lse_roll = roll_max + jnp.log(roll_sum)
    lse_ref = ref_max + jnp.log(ref_sum)
    divergence = cross_sum / ref_sum - lse_ref + lse_roll
    token_logprob = picked - lse_roll
    return (new_state, divergence, token_logprob, roll_z, roll_x, roll_bc, roll_dt, roll_out)


def solution(mesh):
    return jax.shard_map(
        shards,
        mesh=mesh,
        in_specs=(
            P("group", None),
            P("group", "head", None, None),
            P("group", None, "head"),
            P("group", None, None),
            P("group"),
            P("group", "head"),
            P("group", "head"),
            P("group", "head"),
            P("group", None),
            P("group", "head"),
            P("group", "head"),
            P("head", "group"),
            P(None, "head"),
            P("head"),
            P(),
            P(),
            P("head"),
            P("head"),
            P("head"),
            P(),
            P("head"),
            P(),
        ),
        out_specs=(
            P("group", "head", None, None),
            P("group"),
            P("group"),
            P(None, "head"),
            P(None, "head"),
            P(),
            P(None, "head"),
            P(None, "head"),
        ),
        check_vma=False,
    )
```

profile of v0, /device:TPU:0, one launch (start us, length us, event | category | flops | bytes accessed | tf_op | source)
XLA Modules:
  0.0 219.2 jit_solution(8908940668585763981)
XLA Ops:
  7.2 0.0 all-gather.3.cloned.1.call-start
  7.2 0.8 copy.50
  8.1 2.1 concatenate.12
  10.1 0.0 all-gather.3.cloned.1.call-update
  10.2 0.0 all-gather.5.cloned.1.call-start
  10.2 0.7 all-gather.5.cloned.1.call-update
  10.9 0.5 exp.69
  11.4 0.1 add.148
  11.5 0.1 fusion.9
  11.7 69.3 %all-gather.3.cloned.1.call-done = bf16[2560,2186]{1,0:T(8,128)(2,1)} async-done(((bf16[160,2186]{1,0:T(8,128)(2,1)}), bf16[2560,2186]{1,0:T(8,128)(2,1)}) %all-gather.3.cloned.1.call-update) | async-done | bytes 11192336 | tf_op jit(solution)/shard_map/all_gather | solution.py:14
  81.0 6.3 %fusion.26 = (bf16[2560,640]{1,0:T(8,128)(2,1)S(1)}, bf16[2560,640]{1,0:T(8,128)(2,1)}, bf16[2560,640]{1,0:T(8,128)(2,1)S(1)}) fusion(bf16[2560,2186]{1,0:T(8,128)(2,1)} %all-gather.3.cloned.1.call-done), kind=kLoop, calls=%fused_computation.67 | loop fusion | bytes 19660800 | tf_op jit(solution)/shard_map/slice | solution.py:16
  87.3 0.0 copy-start.10
  87.3 1.7 copy-done.2
  89.0 0.6 fusion.1
  89.6 0.1 reduce_sum.103
  89.7 0.0 copy-start.9
  89.7 1.4 slice.210
  91.1 0.0 copy-start.3
  91.1 0.3 fusion.2
  91.5 0.7 divide_multiply_fusion.1
  92.2 1.6 multiply_exponential_fusion
  93.8 0.1 broadcast_multiply_fusion
  93.9 4.2 %multiply_add_fusion = f32[16,10,64,128]{3,2,1,0:T(8,128)S(1)} fusion(f32[16,10,64,128]{3,2,1,0:T(8,128)} %param.23, f32[16,128]{1,0:T(8,128)S(1)} %get-tuple-element.72, f32[16,10,64]{2,1,0:T(8,128)S(1)} %broadcast_multiply_fusion, f32[16,10]{1,0:T(8,128)S(1)} %get-tuple-element.75), kind=kLoop, calls=%fused_computation | loop fusion | flops 3932160 | bytes 10535552 | tf_op jit(solution)/shard_map/add | solution.py:127
  98.1 0.0 copy-start
  98.1 0.0 copy-start.14
  98.1 2.3 %copy-done = f32[16,10,64,128]{3,2,1,0:T(8,128)} copy-done((f32[16,10,64,128]{3,2,1,0:T(8,128)}, f32[16,10,64,128]{3,2,1,0:T(8,128)S(1)}, u32[]{:S(2)}) %copy-start) | copy-done | bytes 5242904
  100.5 2.1 fusion.30
  102.6 0.7 bitcast_add_fusion
  103.3 1.0 reshape.143
  104.3 0.7 multiply_reduce_fusion.3
  105.0 14.1 %all_to_all.16 = f32[8,1,16]{2,1,0:T(1,128)S(1)} all-to-all(f32[8,1,16]{2,1,0:T(1,128)S(1)} %broadcast_in_dim.15), channel_id=1, replica_groups=mesh['group'=16,'head'=8] {'head'}, dimensions={0} | all-to-all | bytes 1024 | tf_op jit(solution)/shard_map/all_to_all | solution.py:23
  119.2 0.0 copy-start.5
  119.2 3.0 %fusion.15 = f32[16,2560]{1,0:T(8,128)S(1)} fusion(bf16[2560,640]{1,0:T(8,128)(2,1)} %get-tuple-element.63, f32[16,640]{1,0:T(8,128)S(1)} %get-tuple-element.78, f32[640]{0:T(1024)S(1)} %copy-done.11, f32[16]{0:T(128)S(1)} %add_rsqrt_fusion.1), kind=kOutput, calls=%fused_computation.38 | convolution fusion | flops 52459520 | bytes 3484224 | tf_op jit(solution)/shard_map/dot_general | solution.py:138
  122.2 1.2 broadcast_in_dim.16
  123.5 3.6 %all-to-all-start.1 = ((f32[8,16,2560]{2,1,0:T(8,128)}), f32[8,16,2560]{2,1,0:T(8,128)S(1)}, u32[]{:S(2)}, u32[]{:S(2)}) async-start(f32[8,16,2560]{2,1,0:T(8,128)} %broadcast_in_dim.16), calls=%async_computation.1 | async-start | bytes 2621440 | tf_op jit(solution)/shard_map/all_to_all | solution.py:23
  127.1 0.1 reduce_max.28
  127.2 21.8 %all-to-all-done.1 = f32[8,16,2560]{2,1,0:T(8,128)S(1)} async-done(((f32[8,16,2560]{2,1,0:T(8,128)}), f32[8,16,2560]{2,1,0:T(8,128)S(1)}, u32[]{:S(2)}, u32[]{:S(2)}) %all-to-all-start.1) | async-done | bytes 1310752 | tf_op jit(solution)/shard_map/all_to_all | solution.py:23
  149.1 0.1 reduce_sum.107
  149.1 0.1 multiply_reduce_fusion
  149.3 38.0 %all-gather.5.cloned.1.call-done = bf16[3200,2560]{0,1:T(8,128)(2,1)} async-done(((bf16[3200,160]{0,1:T(8,128)(2,1)}), bf16[3200,2560]{0,1:T(8,128)(2,1)}) %all-gather.5.cloned.1.call-update) | async-done | bytes 16384016 | tf_op jit(solution)/shard_map/all_gather | solution.py:146
  187.3 8.0 %fusion.29 = (f32[16]{0:T(128)S(1)}, f32[16,3200]{1,0:T(8,128)S(1)}) fusion(bf16[3200,2560]{0,1:T(8,128)(2,1)} %all-gather.5.cloned.1.call-done, f32[16,2560]{1,0:T(8,128)S(1)} %reduce_sum.107, bf16[16,2560]{1,0:T(8,128)(2,1)S(1)} %copy-done.4, f32[2560]{0:T(1024)S(1)} %copy-done.8, f32[16]{0:T(128)S(1)} %add_rsqrt_fusion), kind=kOutput, calls=%fused_computation.70 | convolution fusion | flops 262399984 | bytes 16844928 | tf_op jit(solution)/shard_map/dot_general | solution.py:144
  195.4 0.3 select_reduce_fusion
  195.7 0.6 broadcast_in_dim.18
  196.3 6.6 %all-to-all-start.2 = ((f32[8,6,16]{2,1,0:T(8,128)}), f32[8,6,16]{2,1,0:T(8,128)S(1)}, u32[]{:S(2)}, u32[]{:S(2)}) async-start(f32[8,6,16]{2,1,0:T(8,128)} %broadcast_in_dim.18), calls=%async_computation.2 | async-start | bytes 65536 | tf_op jit(solution)/shard_map/all_to_all | solution.py:23
  202.9 0.9 copy.58
  203.8 6.8 %all-to-all-done.2 = f32[8,6,16]{2,1,0:T(8,128)S(1)} async-done(((f32[8,6,16]{2,1,0:T(8,128)}), f32[8,6,16]{2,1,0:T(8,128)S(1)}, u32[]{:S(2)}, u32[]{:S(2)}) %all-to-all-start.2) | async-done | bytes 3104 | tf_op jit(solution)/shard_map/all_to_all | solution.py:23
  211.3 0.5 subtract_bitcast_fusion
  211.9 0.5 add_bitcast_fusion
  (72 shorter events, 0.8 us)
Async XLA Ops:
  7.2 3.7 %copy-start.16 = (f32[10]{0:T(128)S(1)}, f32[10]{0:T(128)}, u32[]{:S(2)}) copy-start(f32[10]{0:T(128)} %param.39) | copy-start | bytes 124
  7.2 4.3 %copy-start.12 = (f32[640]{0:T(1024)S(1)}, f32[640]{0:T(1024)}, u32[]{:S(2)}) copy-start(f32[640]{0:T(1024)} %param.35) | copy-start | bytes 7684
  7.2 4.3 %copy-start.4 = (bf16[16,2560]{1,0:T(8,128)(2,1)S(1)}, bf16[16,2560]{1,0:T(8,128)(2,1)}, u32[]{:S(2)}) copy-start(bf16[16,2560]{1,0:T(8,128)(2,1)} %param.22) | copy-start | bytes 245764
  7.2 73.8 %all-gather.3.cloned.1.call-start = ((), (), s32[]{:S(2)}) async-start(), calls=%async_computation.3 | async-start | bytes 12533760 | tf_op jit(solution)/shard_map/all_gather | solution.py:14
  10.2 177.2 %all-gather.5.cloned.1.call-start = ((), (), s32[]{:S(2)}) async-start(), calls=%async_computation.4 | async-start | bytes 17408000 | tf_op jit(solution)/shard_map/all_gather | solution.py:146
  11.7 77.3 %copy-start.6 = (f32[2560]{0:T(1024)S(1)}, f32[2560]{0:T(1024)}, u32[]{:S(2)}) copy-start(f32[2560]{0:T(1024)} %param.41) | copy-start | bytes 30724
  87.3 1.7 copy-start.2
  87.3 17.1 %copy-start.1 = (bf16[2560,640]{1,0:T(8,128)(2,1)}, bf16[2560,640]{1,0:T(8,128)(2,1)S(1)}, u32[]{:S(2)}) copy-start(bf16[2560,640]{1,0:T(8,128)(2,1)S(1)} %get-tuple-element.62) | copy-start | bytes 9830404
  87.3 2.3 %copy-start.7 = (bf16[16,3,640]{2,0,1:T(8,128)(2,1)S(1)}, bf16[16,3,640]{2,0,1:T(8,128)(2,1)}, u32[]{:S(2)}) copy-start(bf16[16,3,640]{2,0,1:T(8,128)(2,1)} %param.24) | copy-start | bytes 184324
  87.3 2.3 %copy-start.10 = (f32[4,640]{1,0:T(4,128)S(1)}, f32[4,640]{1,0:T(4,128)}, u32[]{:S(2)}) copy-start(f32[4,640]{1,0:T(4,128)} %param.34) | copy-start | bytes 30724
  89.7 1.8 copy-start.9
  89.7 1.8 copy-start.13
  91.1 7.0 %copy-start.3 = (bf16[2560,256]{1,0:T(8,128)(2,1)}, bf16[2560,256]{1,0:T(8,128)(2,1)S(1)}, u32[]{:S(2)}) copy-start(bf16[2560,256]{1,0:T(8,128)(2,1)S(1)} %slice.210) | copy-start | bytes 3932164
  98.1 2.4 %copy-start = (f32[16,10,64,128]{3,2,1,0:T(8,128)}, f32[16,10,64,128]{3,2,1,0:T(8,128)S(1)}, u32[]{:S(2)}) copy-start(f32[16,10,64,128]{3,2,1,0:T(8,128)S(1)} %multiply_add_fusion) | copy-start | bytes 15728644
  98.1 4.5 %copy-start.14 = (f32[10]{0:T(128)S(1)}, f32[10]{0:T(128)}, u32[]{:S(2)}) copy-start(f32[10]{0:T(128)} %param.40) | copy-start | bytes 124
  102.6 16.6 %copy-start.11 = (f32[640]{0:T(1024)S(1)}, f32[640]{0:T(1024)}, u32[]{:S(2)}) copy-start(f32[640]{0:T(1024)} %param.42) | copy-start | bytes 7684
  119.2 7.8 %copy-start.5 = (bf16[16,3200]{1,0:T(8,128)(2,1)S(1)}, bf16[16,3200]{1,0:T(8,128)(2,1)}, u32[]{:S(2)}) copy-start(bf16[16,3200]{1,0:T(8,128)(2,1)} %param.27) | copy-start | bytes 307204
  122.2 65.1 %copy-start.8 = (f32[2560]{0:T(1024)S(1)}, f32[2560]{0:T(1024)}, u32[]{:S(2)}) copy-start(f32[2560]{0:T(1024)} %param.43) | copy-start | bytes 30724
  123.5 25.6 %all-to-all-start.1 = ((f32[8,16,2560]{2,1,0:T(8,128)}), f32[8,16,2560]{2,1,0:T(8,128)S(1)}, u32[]{:S(2)}, u32[]{:S(2)}) async-start(f32[8,16,2560]{2,1,0:T(8,128)} %broadcast_in_dim.16), calls=%async_computation.1 | async-start | bytes 2621440 | tf_op jit(solution)/shard_map/all_to_all | solution.py:23
  149.3 46.1 %copy-start.15 = (s32[16]{0:T(128)S(1)}, s32[16]{0:T(128)}, u32[]{:S(2)}) copy-start(s32[16]{0:T(128)} %param.26) | copy-start | bytes 196
  149.3 53.6 %slice-start = ((bf16[2560,2186]{1,0:T(8,128)(2,1)}), bf16[2560,10]{1,0:T(8,128)(2,1)S(1)}, s32[]{:S(2)}) async-start(bf16[2560,2186]{1,0:T(8,128)(2,1)} %all-gather.3.cloned.1.call-done), calls=%async_computation.5 | async-start | bytes 1310720 | tf_op jit(solution)/shard_map/slice | solution.py:16
  196.3 14.3 %all-to-all-start.2 = ((f32[8,6,16]{2,1,0:T(8,128)}), f32[8,6,16]{2,1,0:T(8,128)S(1)}, u32[]{:S(2)}, u32[]{:S(2)}) async-start(f32[8,6,16]{2,1,0:T(8,128)} %broadcast_in_dim.18), calls=%async_computation.2 | async-start | bytes 65536 | tf_op jit(solution)/shard_map/all_to_all | solution.py:23
Sparse Core Ops, SparseCore 0:
  10.3 70.6 all-gather.2
  82.7 104.5 all-gather.4
where the time goes:
time: 220 us; the launch traced here: 219 us
  waiting for transfers between devices  137 us (62%)
  local copies, waits for them, and re-layouts  19.7 us (9%)
  matrix products  16.4 us (7%)
  between operations  14.3 us (6%)
  blocking collectives  14.1 us (6%)
  starting transfers between devices  10.2 us (5%)
  other arithmetic  7.78 us (4%)
    all_gather x1, waiting for transfers between devices, sent_together(): result, at, done = (lax.all_gather(both, axis, axis=dim, tiled=True), 0, [])  69.3 us
    all_gather x1, waiting for transfers between devices, shards(): lax.all_gather(lm_head, 'group', axis=1, tiled=True)  38 us
    all_to_all x2, waiting for transfers between devices, from_everyone(): lax.all_to_all(jnp.broadcast_to(array[None], (peers, *array.shape)), axis...  28.6 us
    all_to_all x1, blocking collectives, from_everyone(): lax.all_to_all(jnp.broadcast_to(array[None], (peers, *array.shape)), axis...  14.1 us
    all_to_all x2, starting transfers between devices, from_everyone(): lax.all_to_all(jnp.broadcast_to(array[None], (peers, *array.shape)), axis...  10.2 us
    dot_general x1, matrix products, shards(): lax.dot_general(final_hidden, lax.all_gather(lm_head, 'group', axis=1, ti...  8.03 us
    slice x4, local copies, waits for them, and re-layouts, sent_together(): done.append(lax.slice_in_dim(result, at, at + a.shape[along], axis=along))  7.68 us
    unnamed x36, local copies, waits for them, and re-layouts  5.83 us
  transfers between devices with their start and end apart: 4, of which 4 were waited for; matrix products, arithmetic and copies ran while one was open for 12% of the time, Pallas kernels for 0%

commit v1 on v0

v1 whole, which is shorter than its diff:
```python
import jax
import jax.numpy as jnp
from jax import lax
from jax.sharding import Mesh
from jax.sharding import PartitionSpec as P

P_SIZE = 64
EPSILON = 1e-05
CHIPS = ("x", "z")
GROUP = ("x", "z", "core")
F32 = jnp.float32
BF16 = jnp.bfloat16


def from_partner(array):
    return lax.ppermute(array, "core", [(0, 1), (1, 0)])


def exchange(blocks, axis):
    return lax.all_to_all(blocks, axis, 0, 0, tiled=True)


def from_everyone(array, axis):
    peers = lax.axis_size(axis)
    return exchange(jnp.broadcast_to(array[None], (peers, *array.shape)), axis)


def two_parts(values):
    high = lax.reduce_precision(values, 8, 7)
    return high.astype(BF16), (values - high).astype(BF16)


def with_scalars(array, scalars):
    high, low = two_parts(scalars)
    spare = -(array.shape[-1] + 2) % 128
    tail = jnp.stack([high, low] + [jnp.zeros_like(high)] * spare, axis=-1)
    return jnp.concatenate([array, tail], axis=-1)


def conv_branch(history, newest, taps, offset):
    total = newest * taps[3] + offset
    for k in range(3):
        total = total + history[:, k, :].astype(F32) * taps[k]
    return jax.nn.silu(total)


def shards(
    hidden_in,
    ssm_state,
    conv_x_state,
    conv_bc_state,
    token_ids,
    ref_logits,
    in_z,
    in_x,
    in_bc,
    in_dt,
    out_t,
    lm_head,
    conv_wx,
    conv_bx,
    conv_wbc,
    conv_bbc,
    dt_bias,
    a_log,
    skip_gain,
    norm_in,
    norm_gain,
    final_gain,
):
    chips = lax.axis_size(CHIPS)
    first_core = lax.axis_index("core") == 0
    seqs, width = hidden_in.shape
    rows, inner = in_z.shape
    heads = a_log.shape[0]
    state_size = in_bc.shape[1] // 2
    class_seqs = chips * seqs

    dt_padded = jnp.pad(in_dt, ((0, 0), (0, -heads % 128)))
    own = jnp.concatenate([in_z, in_x, in_bc, dt_padded, out_t], axis=1)
    in_cols = own.shape[1] - inner
    gathered = lax.all_gather(own, GROUP, axis=0, tiled=True)
    roll_z = gathered[:, :inner]
    roll_x = gathered[:, inner : 2 * inner]
    roll_bc = gathered[:, 2 * inner : 2 * inner + 2 * state_size]
    dt_at = 2 * inner + 2 * state_size
    roll_dt = gathered[:, dt_at : dt_at + heads]
    roll_out = gathered[:, in_cols:]
    other = from_partner(own)
    lm_other = from_partner(lm_head)

    def own_first(array):
        left, right = array[:, :rows], array[:, rows:]
        return jnp.where(first_core, left, right), jnp.where(first_core, right, left)

    stream_in = hidden_in.astype(F32)
    scale = lax.rsqrt(jnp.mean(stream_in * stream_in, axis=-1, keepdims=True) + EPSILON)
    normed = (stream_in * scale * norm_in).astype(BF16)
    both = jnp.concatenate(
        [normed.reshape(seqs, chips, -1), hidden_in.reshape(seqs, chips, -1)], axis=-1
    ).transpose(1, 0, 2)
    both = exchange(both, CHIPS).reshape(class_seqs, -1)
    normed_own, normed_other = own_first(both[:, : 2 * rows])
    hidden_own, hidden_other = own_first(both[:, 2 * rows :])

    partial_in = jnp.dot(normed_own, own[:, :in_cols], preferred_element_type=F32) + jnp.dot(
        normed_other, other[:, :in_cols], preferred_element_type=F32
    )
    partial_in = exchange(partial_in.astype(BF16).reshape(chips, seqs, in_cols), CHIPS)
    branches = jnp.sum(partial_in.astype(F32), axis=0)
    gate = branches[:, :inner]
    x_conv = conv_branch(conv_x_state, branches[:, inner : 2 * inner], conv_wx, conv_bx)
    bc_conv = conv_branch(conv_bc_state, branches[:, 2 * inner : dt_at], conv_wbc, conv_bbc)
    b_vals, c_vals = bc_conv[:, :state_size], bc_conv[:, state_size:]
    step = jax.nn.softplus(branches[:, dt_at : dt_at + heads] + dt_bias)
    decay = jnp.exp(-step * jnp.exp(a_log))
    x_heads = x_conv.reshape(seqs, heads, P_SIZE)
    inflow = (step[:, :, None] * x_heads)[:, :, :, None] * b_vals[:, None, None, :]
    new_state = decay[:, :, None, None] * ssm_state + inflow
    carried = jnp.einsum("shpn,sn->shp", ssm_state, c_vals)
    overlap = jnp.sum(b_vals * c_vals, axis=-1)
    direct = step * overlap[:, None] + skip_gain
    ssm_out = (decay[:, :, None] * carried + direct[:, :, None] * x_heads).reshape(seqs, inner)
    gated = (ssm_out * jax.nn.silu(gate)).astype(BF16)

    gated = from_everyone(gated, CHIPS).reshape(class_seqs, inner).astype(F32)
    squares = jnp.sum(gated * gated, axis=-1)
    gained = (gated * norm_gain).astype(BF16)
    across = (((1,), (1,)), ((), ()))
    mix_own = lax.dot_general(gained, out_t, across, preferred_element_type=F32)
    mix_other = lax.dot_general(gained, other[:, in_cols:], across, preferred_element_type=F32)
    mix = jnp.concatenate([mix_own.astype(BF16), mix_other.astype(BF16)], axis=-1)
    mix = jnp.sum(from_everyone(with_scalars(mix, squares), "head").astype(F32), axis=0)
    square_total = mix[:, 2 * rows] + mix[:, 2 * rows + 1]
    mix_scale = lax.rsqrt(square_total / (inner * lax.axis_size("head")) + EPSILON)[:, None]
    stream_own = hidden_own.astype(F32) + mix_scale * mix[:, :rows]
    stream_other = hidden_other.astype(F32) + mix_scale * mix[:, rows : 2 * rows]

    group_at = lax.axis_index(GROUP)
    gain_own = lax.dynamic_slice_in_dim(final_gain, group_at * rows, rows)
    gain_other = lax.dynamic_slice_in_dim(final_gain, (group_at ^ 1) * rows, rows)
    squares = jnp.sum(stream_own * stream_own, axis=-1) + jnp.sum(stream_other * stream_other, axis=-1)
    partial_logits = lax.dot_general(
        (stream_own * gain_own).astype(BF16), lm_head, across, preferred_element_type=F32
    ) + lax.dot_general(
        (stream_other * gain_other).astype(BF16), lm_other, across, preferred_element_type=F32
    )
    vocab_local = lm_head.shape[0]
    sent = with_scalars(partial_logits.astype(BF16), squares).reshape(chips, seqs, -1)
    summed = jnp.sum(exchange(sent, CHIPS).astype(F32), axis=0)
    final_square = summed[:, vocab_local] + summed[:, vocab_local + 1]
    logits = summed[:, :vocab_local] * lax.rsqrt(final_square / width + EPSILON)[:, None]

    reference_rows = ref_logits.astype(F32)
    columns = lax.axis_index("head") * vocab_local + lax.broadcasted_iota(jnp.int32, (1, vocab_local), 1)
    picked = jnp.sum(jnp.where(columns == token_ids[:, None], logits, 0.0), axis=-1)
    roll_max = jnp.max(logits, axis=-1)
    ref_max = jnp.max(reference_rows, axis=-1)
    roll_sum = jnp.sum(jnp.exp(logits - roll_max[:, None]), axis=-1)
    ref_weights = jnp.exp(reference_rows - ref_max[:, None])
    ref_sum = jnp.sum(ref_weights, axis=-1)
    cross_sum = jnp.sum(ref_weights * (reference_rows - logits), axis=-1)
    zero = jnp.zeros_like(picked)
    stats = jnp.stack([roll_max, roll_sum, ref_max, ref_sum, cross_sum, picked, zero, zero])
    stats = from_everyone(stats, "head")
    roll_top = jnp.max(stats[:, 0], axis=0)
    ref_top = jnp.max(stats[:, 2], axis=0)
    roll_total = jnp.sum(stats[:, 1] * jnp.exp(stats[:, 0] - roll_top), axis=0)
    ref_scale = jnp.exp(stats[:, 2] - ref_top)
    ref_total = jnp.sum(stats[:, 3] * ref_scale, axis=0)
    cross_total = jnp.sum(stats[:, 4] * ref_scale, axis=0)
    lse_roll = roll_top + jnp.log(roll_total)
    lse_ref = ref_top + jnp.log(ref_total)
    divergence = cross_total / ref_total - lse_ref + lse_roll
    token_logprob = jnp.sum(stats[:, 5], axis=0) - lse_roll
    return (new_state, divergence, token_logprob, roll_z, roll_x, roll_bc, roll_dt, roll_out)


def solution(mesh):
    group, head = mesh.devices.shape
    fine = Mesh(mesh.devices.reshape(group // 4, 2, 2, head), ("x", "z", "core", "head"))
    return jax.shard_map(
        shards,
        mesh=fine,
        in_specs=(
            P(GROUP, None),
            P(GROUP, "head", None, None),
            P(GROUP, None, "head"),
            P(GROUP, None, None),
            P(GROUP),
            P(GROUP, "head"),
            P(GROUP, "head"),
            P(GROUP, "head"),
            P(GROUP, None),
            P(GROUP, "head"),
            P(GROUP, "head"),
            P("head", GROUP),
            P(None, "head"),
            P("head"),
            P(),
            P(),
            P("head"),
            P("head"),
            P("head"),
            P(),
            P("head"),
            P(),
        ),
        out_specs=(
            P(GROUP, "head", None, None),
            P(GROUP),
            P(GROUP),
            P(None, "head"),
            P(None, "head"),
            P(),
            P(None, "head"),
            P(None, "head"),
        ),
        check_vma=False,
    )
```

time: 220 us -> 144 us (0.65)
  waiting for transfers between devices: 137 us -> 45.9 us
  starting transfers between devices: 10.2 us -> 28.4 us
  matrix products: 16.4 us -> 7.55 us
  local copies, waits for them, and re-layouts: 19.7 us -> 24.3 us
  other arithmetic: 7.78 us -> 11.6 us
  blocking collectives: 14.1 us -> 11.2 us
    all_gather x2 -> x1, waiting for transfers between devices: 107 us -> 0.01 us  [shards(): gathered = lax.all_gather(own, GROUP, axis=0, tiled=True)]
    all_to_all x2 -> x5, starting transfers between devices: 10.2 us -> 28.2 us  [exchange(): return lax.all_to_all(blocks, axis, 0, 0, tiled=True)]
    all_to_all x2 -> x5, waiting for transfers between devices: 28.6 us -> 45.8 us  [exchange(): return lax.all_to_all(blocks, axis, 0, 0, tiled=True)]
    dot_general x7, matrix products: 16.4 us -> 7.55 us  [the longest x1 4.73 us: shards(): carried = jnp.einsum('shpn,sn->shp', ssm_state, c_vals)]
    all_to_all x1, blocking collectives: 14.1 us -> 11.2 us  [exchange(): return lax.all_to_all(blocks, axis, 0, 0, tiled=True)]
    slice x30 -> x5, local copies, waits for them, and re-layouts: 8.25 us -> 10.8 us  [the longest x1 7.16 us: shards(): roll_out = gathered[:, in_cols:]]
    unnamed x36 -> x44, local copies, waits for them, and re-layouts: 5.83 us -> 6.38 us
  transfers between devices with their start and end apart: 4 -> 8, of which waited for: 4 -> 5; matrix products, arithmetic and copies ran while one was open for 12% -> 18% of each run, Pallas kernels for 0% -> 0%
where the time goes in v1:
time: 144 us
  waiting for transfers between devices  45.9 us (32%)
  starting transfers between devices  28.4 us (20%)
  local copies, waits for them, and re-layouts  24.3 us (17%)
  between operations  14.6 us (10%)
  other arithmetic  11.6 us (8%)
  blocking collectives  11.2 us (8%)
  matrix products  7.55 us (5%)
    all_to_all x5, waiting for transfers between devices, exchange(): return lax.all_to_all(blocks, axis, 0, 0, tiled=True)  45.8 us
    all_to_all x5, starting transfers between devices, exchange(): return lax.all_to_all(blocks, axis, 0, 0, tiled=True)  28.2 us
    all_to_all x1, blocking collectives, exchange(): return lax.all_to_all(blocks, axis, 0, 0, tiled=True)  11.2 us
    slice x1, local copies, waits for them, and re-layouts, shards(): roll_out = gathered[:, in_cols:]  7.16 us
    unnamed x44, local copies, waits for them, and re-layouts  6.38 us
    add x1, other arithmetic, shards(): new_state = decay[:, :, None, None] * ssm_state + inflow  6.01 us
    dot_general x1, matrix products, shards(): carried = jnp.einsum('shpn,sn->shp', ssm_state, c_vals)  4.73 us
  transfers between devices with their start and end apart: 8, of which 5 were waited for; matrix products, arithmetic and copies ran while one was open for 18% of the time, Pallas kernels for 0%

profile of v1, /device:TPU:0, one launch (start us, length us, event | category | flops | bytes accessed | tf_op | source)
XLA Modules:
  0.0 143.5 jit_solution(17616599092487550039)
XLA Ops:
  7.2 0.9 copy.59
  8.2 0.9 constant_dynamic-update-slice_fusion.4
  9.1 1.0 constant_dynamic-update-slice_fusion.3
  10.1 0.9 constant_dynamic-update-slice_fusion.2
  11.0 1.0 constant_dynamic-update-slice_fusion
  12.0 0.9 copy-done
  13.0 1.0 fusion.17
  14.0 1.0 fusion.19
  15.0 1.0 reshape.186
  16.3 0.7 copy.58
  17.0 5.8 %all-to-all-start = ((bf16[8,16,640]{2,1,0:T(8,128)(2,1)}), bf16[8,16,640]{2,1,0:T(8,128)(2,1)S(1)}, u32[]{:S(2)}, u32[]{:S(2)}) async-start(bf16[8,16,640]{2,1,0:T(8,128)(2,1)} %copy.58), calls=%async_computation | async-start | bytes 327680 | tf_op jit(solution)/shard_map/all_to_all | solution.py:20
  22.8 8.0 %all-to-all-done = bf16[8,16,640]{2,1,0:T(8,128)(2,1)S(1)} async-done(((bf16[8,16,640]{2,1,0:T(8,128)(2,1)}), bf16[8,16,640]{2,1,0:T(8,128)(2,1)S(1)}, u32[]{:S(2)}, u32[]{:S(2)}) %all-to-all-start) | async-done | bytes 163872 | tf_op jit(solution)/shard_map/all_to_all | solution.py:20
  30.8 0.3 fusion.3
  31.1 1.1 fusion.1
  32.2 3.5 %all-to-all-start.1 = ((bf16[8,16,1664]{2,1,0:T(8,128)(2,1)}), bf16[8,16,1664]{2,1,0:T(8,128)(2,1)S(1)}, u32[]{:S(2)}, u32[]{:S(2)}) async-start(bf16[8,16,1664]{2,1,0:T(8,128)(2,1)} %bitcast.2), calls=%async_computation.1 | async-start | bytes 851968 | tf_op jit(solution)/shard_map/all_to_all | solution.py:20
  35.8 13.2 %all-to-all-done.1 = bf16[8,16,1664]{2,1,0:T(8,128)(2,1)S(1)} async-done(((bf16[8,16,1664]{2,1,0:T(8,128)(2,1)}), bf16[8,16,1664]{2,1,0:T(8,128)(2,1)S(1)}, u32[]{:S(2)}, u32[]{:S(2)}) %all-to-all-start.1) | async-done | bytes 426016 | tf_op jit(solution)/shard_map/all_to_all | solution.py:20
  49.4 4.7 %fusion.61 = f32[16,1,10,64]{3,1,2,0:T(1,128)S(1)} fusion(f32[16,128,1,1]{1,2,3,0:T(1,128)S(1)} %bitcast.77, f32[16,10,64,128]{3,2,1,0:T(8,128)} %param.23), kind=kOutput, calls=%fused_computation.130 | convolution fusion | flops 2621440 | bytes 5292032 | tf_op jit(solution)/shard_map/shpn,sn->shp/dot_general | solution.py:120
  54.2 0.2 fusion.23
  54.5 11.2 %all_to_all.30 = bf16[8,16,640]{2,1,0:T(8,128)(2,1)S(1)} all-to-all(bf16[8,16,640]{2,1,0:T(8,128)(2,1)S(1)} %broadcast_in_dim.9), channel_id=1, replica_groups=mesh['x'=4,'z'=2,'core'=2,'head'=8] {'x','z'}, dimensions={0} | all-to-all | bytes 327680 | tf_op jit(solution)/shard_map/all_to_all | solution.py:20
  65.9 0.2 convolution_convert_fusion.1
  66.2 0.2 convolution_convert_fusion
  66.7 1.0 broadcast_in_dim.10
  67.6 8.4 %all-to-all-start.3 = ((bf16[8,128,384]{2,1,0:T(8,128)(2,1)}), bf16[8,128,384]{2,1,0:T(8,128)(2,1)S(1)}, u32[]{:S(2)}, u32[]{:S(2)}) async-start(bf16[8,128,384]{2,1,0:T(8,128)(2,1)} %broadcast_in_dim.10), calls=%async_computation.3 | async-start | bytes 1572864 | tf_op jit(solution)/shard_map/all_to_all | solution.py:20
  76.1 0.9 fusion.59
  77.0 12.5 %all-to-all-done.3 = bf16[8,128,384]{2,1,0:T(8,128)(2,1)S(1)} async-done(((bf16[8,128,384]{2,1,0:T(8,128)(2,1)}), bf16[8,128,384]{2,1,0:T(8,128)(2,1)S(1)}, u32[]{:S(2)}, u32[]{:S(2)}) %all-to-all-start.3) | async-done | bytes 786464 | tf_op jit(solution)/shard_map/all_to_all | solution.py:20
  89.6 0.2 fusion.28
  89.8 0.2 multiply_reduce_fusion.1
  90.1 0.1 copy.62
  90.4 0.5 fusion.24
  90.9 0.5 fusion
  91.5 1.1 concatenate.42
  92.6 3.6 %all-to-all-start.4 = ((bf16[8,16,3328]{2,1,0:T(8,128)(2,1)}), bf16[8,16,3328]{2,1,0:T(8,128)(2,1)S(1)}, u32[]{:S(2)}, u32[]{:S(2)}) async-start(bf16[8,16,3328]{2,1,0:T(8,128)(2,1)} %concatenate.42), calls=%async_computation.4 | async-start | bytes 1703936 | tf_op jit(solution)/shard_map/all_to_all | solution.py:20
  96.2 0.1 reduce_max.46
  96.3 10.6 %all-to-all-done.4 = bf16[8,16,3328]{2,1,0:T(8,128)(2,1)S(1)} async-done(((bf16[8,16,3328]{2,1,0:T(8,128)(2,1)}), bf16[8,16,3328]{2,1,0:T(8,128)(2,1)S(1)}, u32[]{:S(2)}, u32[]{:S(2)}) %all-to-all-start.4) | async-done | bytes 852000 | tf_op jit(solution)/shard_map/all_to_all | solution.py:20
  107.0 0.2 fusion.52
  107.2 0.2 fusion.20
  107.5 0.3 select_reduce_fusion
  107.8 0.7 reshape.207
  108.5 7.0 %all-to-all-start.5 = ((f32[8,1,128]{2,1,0:T(1,128)}), f32[8,1,128]{2,1,0:T(1,128)S(1)}, u32[]{:S(2)}, u32[]{:S(2)}) async-start(f32[8,1,128]{2,1,0:T(1,128)} %reshape.207), calls=%async_computation.5 | async-start | bytes 8192 | tf_op jit(solution)/shard_map/all_to_all | solution.py:20
  115.5 6.0 %multiply_add_fusion = f32[16,10,64,128]{3,2,1,0:T(8,128)} fusion(f32[16,10,64,128]{3,2,1,0:T(8,128)} %param.23, f32[16,128]{1,0:T(8,128)S(1)} %get-tuple-element.77, f32[16,10,64]{2,1,0:T(8,128)S(1)} %get-tuple-element.66, f32[16,10]{1,0:T(8,128)S(1)} %multiply_exponential_fusion), kind=kLoop, calls=%fused_computation | loop fusion | flops 3932160 | bytes 10535552 | tf_op jit(solution)/shard_map/add | solution.py:119
  121.5 1.6 %all-to-all-done.5 = f32[8,1,128]{2,1,0:T(1,128)S(1)} async-done(((f32[8,1,128]{2,1,0:T(1,128)}), f32[8,1,128]{2,1,0:T(1,128)S(1)}, u32[]{:S(2)}, u32[]{:S(2)}) %all-to-all-start.5) | async-done | bytes 4128 | tf_op jit(solution)/shard_map/all_to_all | solution.py:20
  123.1 0.5 broadcast.107
  123.6 0.7 reduce.17
  124.5 0.5 fusion.56
  125.0 1.1 slice.214
  126.1 0.9 copy.68
  127.1 2.5 %slice.213 = bf16[2560,256]{1,0:T(8,128)(2,1)} slice(bf16[2560,2304]{1,0:T(8,128)(2,1)} %all-gather.2.cloned.1.call-done), slice={[0:2560], [1280:1536]} | slice | bytes 2621440 | tf_op jit(solution)/shard_map/slice | solution.py:85
  129.5 7.2 %fusion.57 = (bf16[2560,640]{1,0:T(8,128)(2,1)}, bf16[2560,640]{1,0:T(8,128)(2,1)}, bf16[2560,640]{1,0:T(8,128)(2,1)}) fusion(bf16[2560,2304]{1,0:T(8,128)(2,1)} %all-gather.2.cloned.1.call-done), kind=kLoop, calls=%fused_computation.126 | loop fusion | bytes 19660800 | tf_op jit(solution)/shard_map/slice | solution.py:88
  (92 shorter events, 2.4 us)
Async XLA Ops:
  7.2 23.6 %copy-start.4 = (bf16[160,640]{1,0:T(8,128)(2,1)S(1)}, bf16[160,640]{1,0:T(8,128)(2,1)}, u32[]{:S(2)}) copy-start(bf16[160,640]{1,0:T(8,128)(2,1)} %param.28) | copy-start | bytes 614404
  7.2 23.6 %copy-start.5 = (bf16[160,640]{1,0:T(8,128)(2,1)S(1)}, bf16[160,640]{1,0:T(8,128)(2,1)}, u32[]{:S(2)}) copy-start(bf16[160,640]{1,0:T(8,128)(2,1)} %param.29) | copy-start | bytes 614404
  7.2 23.6 %copy-start.6 = (bf16[160,256]{1,0:T(8,128)(2,1)S(1)}, bf16[160,256]{1,0:T(8,128)(2,1)}, u32[]{:S(2)}) copy-start(bf16[160,256]{1,0:T(8,128)(2,1)} %param.30) | copy-start | bytes 245764
  7.2 117.8 %all-gather.2.cloned.1.call-start = ((), (), s32[]{:S(2)}) async-start(), calls=%async_computation.6 | async-start | bytes 12533760 | tf_op jit(solution)/shard_map/all_gather | solution.py:82
  12.0 0.9 copy-start
  12.9 22.8 %copy-start.17 = (f32[10]{0:T(128)S(1)}, f32[10]{0:T(128)}, u32[]{:S(2)}) copy-start(f32[10]{0:T(128)} %param.39) | copy-start | bytes 124
  12.9 22.8 %copy-start.9 = (f32[4,640]{1,0:T(4,128)S(1)}, f32[4,640]{1,0:T(4,128)}, u32[]{:S(2)}) copy-start(f32[4,640]{1,0:T(4,128)} %param.34) | copy-start | bytes 30724
  12.9 22.9 %copy-start.11 = (f32[4,256]{1,0:T(4,128)S(1)}, f32[4,256]{1,0:T(4,128)}, u32[]{:S(2)}) copy-start(f32[4,256]{1,0:T(4,128)} %param.36) | copy-start | bytes 12292
  12.9 18.2 %collective-permute-start = (bf16[160,2304]{1,0:T(8,128)(2,1)}, bf16[160,2304]{1,0:T(8,128)(2,1)S(1)}, u32[]{:S(2)}, u32[]{:S(2)}) collective-permute-start(bf16[160,2304]{1,0:T(8,128)(2,1)} %copy-done), channel_id=1, source_target_pairs={{0,8},{8,0},{1,9},{9,1},{2,10},{10,2},{3,11},{11,3},{4,12},{12,4},... | collective-permute-start | bytes 2211848 | tf_op jit(solution)/shard_map/ppermute | solution.py:16
  16.2 32.9 %copy-start.7 = (bf16[16,3,640]{2,0,1:T(8,128)(2,1)S(1)}, bf16[16,3,640]{2,0,1:T(8,128)(2,1)}, u32[]{:S(2)}) copy-start(bf16[16,3,640]{2,0,1:T(8,128)(2,1)} %param.24) | copy-start | bytes 184324
  16.2 32.9 %copy-start.10 = (f32[640]{0:T(1024)S(1)}, f32[640]{0:T(1024)}, u32[]{:S(2)}) copy-start(f32[640]{0:T(1024)} %param.35) | copy-start | bytes 7684
  16.3 32.9 %copy-start.8 = (bf16[16,3,256]{2,0,1:T(8,128)(2,1)S(1)}, bf16[16,3,256]{2,0,1:T(8,128)(2,1)}, u32[]{:S(2)}) copy-start(bf16[16,3,256]{2,0,1:T(8,128)(2,1)} %param.25) | copy-start | bytes 73732
  16.3 32.9 %copy-start.13 = (f32[256]{0:T(256)S(1)}, f32[256]{0:T(256)}, u32[]{:S(2)}) copy-start(f32[256]{0:T(256)} %param.37) | copy-start | bytes 3076
  16.3 33.0 %copy-start.15 = (f32[10]{0:T(128)S(1)}, f32[10]{0:T(128)}, u32[]{:S(2)}) copy-start(f32[10]{0:T(128)} %param.40) | copy-start | bytes 124
  16.3 33.0 %copy-start.16 = (f32[10]{0:T(128)S(1)}, f32[10]{0:T(128)}, u32[]{:S(2)}) copy-start(f32[10]{0:T(128)} %param.38) | copy-start | bytes 124
  17.0 13.7 %all-to-all-start = ((bf16[8,16,640]{2,1,0:T(8,128)(2,1)}), bf16[8,16,640]{2,1,0:T(8,128)(2,1)S(1)}, u32[]{:S(2)}, u32[]{:S(2)}) async-start(bf16[8,16,640]{2,1,0:T(8,128)(2,1)} %copy.58), calls=%async_computation | async-start | bytes 327680 | tf_op jit(solution)/shard_map/all_to_all | solution.py:20
  32.2 16.7 %all-to-all-start.1 = ((bf16[8,16,1664]{2,1,0:T(8,128)(2,1)}), bf16[8,16,1664]{2,1,0:T(8,128)(2,1)S(1)}, u32[]{:S(2)}, u32[]{:S(2)}) async-start(bf16[8,16,1664]{2,1,0:T(8,128)(2,1)} %bitcast.2), calls=%async_computation.1 | async-start | bytes 851968 | tf_op jit(solution)/shard_map/all_to_all | solution.py:20
  49.4 16.4 %copy-start.12 = (f32[640]{0:T(1024)S(1)}, f32[640]{0:T(1024)}, u32[]{:S(2)}) copy-start(f32[640]{0:T(1024)} %param.42) | copy-start | bytes 7684
  49.4 16.5 %copy-start.2 = (bf16[160,640]{1,0:T(8,128)(2,1)S(1)}, bf16[160,640]{1,0:T(8,128)(2,1)}, u32[]{:S(2)}) copy-start(bf16[160,640]{1,0:T(8,128)(2,1)} %param.32) | copy-start | bytes 614404
  54.2 21.8 %copy-start.1 = (bf16[3200,160]{0,1:T(8,128)(2,1)S(1)}, bf16[3200,160]{0,1:T(8,128)(2,1)}, u32[]{:S(2)}) copy-start(bf16[3200,160]{0,1:T(8,128)(2,1)} %param.33) | copy-start | bytes 3072004
  67.6 21.9 %all-to-all-start.3 = ((bf16[8,128,384]{2,1,0:T(8,128)(2,1)}), bf16[8,128,384]{2,1,0:T(8,128)(2,1)S(1)}, u32[]{:S(2)}, u32[]{:S(2)}) async-start(bf16[8,128,384]{2,1,0:T(8,128)(2,1)} %broadcast_in_dim.10), calls=%async_computation.3 | async-start | bytes 1572864 | tf_op jit(solution)/shard_map/all_to_all | solution.py:20
  76.0 14.9 %collective-permute-start.1 = (bf16[3200,160]{0,1:T(8,128)(2,1)S(1)}, bf16[3200,160]{0,1:T(8,128)(2,1)S(1)}, u32[]{:S(2)}, u32[]{:S(2)}) collective-permute-start(bf16[3200,160]{0,1:T(8,128)(2,1)S(1)} %copy-done.1), channel_id=1, source_target_pairs={{0,8},{8,0},{1,9},{9,1},{2,10},{10,2},{3,11},{11,3},{4,12},{12,4},... | collective-permute-start | bytes 3072008 | tf_op jit(solution)/shard_map/ppermute | solution.py:16
  90.9 5.3 %copy-start.3 = (bf16[16,3200]{1,0:T(8,128)(2,1)S(1)}, bf16[16,3200]{1,0:T(8,128)(2,1)}, u32[]{:S(2)}) copy-start(bf16[16,3200]{1,0:T(8,128)(2,1)} %param.27) | copy-start | bytes 307204
  91.4 16.1 %copy-start.14 = (s32[16]{0:T(128)S(1)}, s32[16]{0:T(128)}, u32[]{:S(2)}) copy-start(s32[16]{0:T(128)} %param.26) | copy-start | bytes 196
  92.6 14.3 %all-to-all-start.4 = ((bf16[8,16,3328]{2,1,0:T(8,128)(2,1)}), bf16[8,16,3328]{2,1,0:T(8,128)(2,1)S(1)}, u32[]{:S(2)}, u32[]{:S(2)}) async-start(bf16[8,16,3328]{2,1,0:T(8,128)(2,1)} %concatenate.42), calls=%async_computation.4 | async-start | bytes 1703936 | tf_op jit(solution)/shard_map/all_to_all | solution.py:20
  108.5 14.6 %all-to-all-start.5 = ((f32[8,1,128]{2,1,0:T(1,128)}), f32[8,1,128]{2,1,0:T(1,128)S(1)}, u32[]{:S(2)}, u32[]{:S(2)}) async-start(f32[8,1,128]{2,1,0:T(1,128)} %reshape.207), calls=%async_computation.5 | async-start | bytes 8192 | tf_op jit(solution)/shard_map/all_to_all | solution.py:20
Sparse Core Ops, SparseCore 0:
  13.0 96.0 all-gather.1

commit v2 on v1

v2 whole, which is shorter than its diff:
```python
import functools

import jax
import jax.numpy as jnp
from jax import lax
from jax.experimental import pallas as pl
from jax.experimental.pallas import tpu as pltpu
from jax.sharding import Mesh
from jax.sharding import PartitionSpec as P

P_SIZE = 64
EPSILON = 1e-05
CHIPS = ("x", "z")
GROUP = ("x", "z", "core")
F32 = jnp.float32
BF16 = jnp.bfloat16


def from_partner(array):
    return lax.ppermute(array, "core", [(0, 1), (1, 0)])


def from_opposite(array):
    return lax.ppermute(array, "z", [(0, 1), (1, 0)])


def along_ring(array, sign):
    ring = lax.axis_size("x")
    pairs = [
        (2 * x + core, 2 * ((x + (sign if core == 0 else -sign)) % ring) + core)
        for x in range(ring)
        for core in range(2)
    ]
    return lax.ppermute(array, ("x", "core"), pairs)


def joined_kernel(in_z, in_x, in_bc, in_dt, out_t, own):
    at = 0
    for part in (in_z, in_x, in_bc):
        own[:, at : at + part.shape[1]] = part[...]
        at += part.shape[1]
    own[:, at : at + 128] = jnp.zeros((own.shape[0], 128), own.dtype)
    own[:, at : at + in_dt.shape[1]] = in_dt[...]
    own[:, at + 128 :] = out_t[...]


def joined(in_z, in_x, in_bc, in_dt, out_t):
    rows, inner = in_z.shape
    whole = 3 * inner + in_bc.shape[1] + 128
    return pl.pallas_call(
        joined_kernel,
        out_shape=jax.ShapeDtypeStruct((rows, whole), in_z.dtype),
        cost_estimate=pl.CostEstimate(flops=2000000, bytes_accessed=2 * 2 * rows * whole, transcendentals=0),
    )(in_z, in_x, in_bc, in_dt, out_t)


def blocks_kernel(hidden, gain, out, scale):
    values = hidden[...].astype(F32)
    mean = jnp.mean(values * values, axis=-1, keepdims=True)
    scale[...] = jnp.broadcast_to(lax.rsqrt(mean + EPSILON), scale.shape)
    gained = (values * gain[...]).astype(out.dtype)
    wide = out.shape[2] // 2
    for k in range(out.shape[0]):
        out[k, :, :wide] = gained[:, k * wide : (k + 1) * wide]
        out[k, :, wide:] = hidden[:, k * wide : (k + 1) * wide]


def hidden_blocks(hidden, gain, chips):
    seqs, width = hidden.shape
    return pl.pallas_call(
        blocks_kernel,
        out_shape=(
            jax.ShapeDtypeStruct((chips, seqs, 2 * width // chips), hidden.dtype),
            jax.ShapeDtypeStruct((seqs, 128), F32),
        ),
        cost_estimate=pl.CostEstimate(flops=1000000, bytes_accessed=300000, transcendentals=0),
    )(hidden, gain.reshape(1, width))


def placed_kernel(tags, widths, *refs):
    count = len(tags)
    pieces = refs[:count]
    outs, (held, in_sems, out_sems) = refs[-len(widths) - 3 : -3], refs[-3:]
    rows = pieces[0].shape[0]
    x, z, core = (lax.axis_index(name) for name in ("x", "z", "core"))
    reads = [pltpu.make_async_copy(pieces[i], held.at[i], in_sems.at[i]) for i in range(count)]
    for read in reads:
        read.start()
    writes = []
    for i, (turn, over, swap) in enumerate(tags):
        source_core = lax.rem(core + swap, 2)
        back = lax.rem(4 - turn + turn * 2 * source_core, 4)
        source = lax.rem(x + back, 4) * 4 + lax.rem(z + over, 2) * 2 + source_core
        at = pl.multiple_of(source * rows, rows)
        reads[i].wait()
        col = 0
        for j, wide in enumerate(widths):
            write = pltpu.make_async_copy(
                held.at[i, :, pl.ds(col, wide)],
                outs[j].at[pl.ds(at, rows), :],
                out_sems.at[i, j],
            )
            write.start()
            writes.append(write)
            col += wide
    for write in writes:
        write.wait()


def placed(pieces, devices, widths, earlier=()):
    tags, arrays = list(pieces), list(pieces.values())
    rows, whole = arrays[0].shape
    count = len(tags)
    anywhere = pl.BlockSpec(memory_space=pl.ANY)
    return pl.pallas_call(
        functools.partial(placed_kernel, tags, widths),
        out_shape=tuple(jax.ShapeDtypeStruct((rows * devices, wide), arrays[0].dtype) for wide in widths),
        in_specs=[anywhere] * (count + len(earlier)),
        out_specs=tuple(anywhere for _ in widths),
        scratch_shapes=[
            pltpu.VMEM((count, rows, whole), arrays[0].dtype),
            pltpu.SemaphoreType.DMA((count,)),
            pltpu.SemaphoreType.DMA((count, len(widths))),
        ],
        input_output_aliases={count + j: j for j in range(len(earlier))},
        compiler_params=pltpu.CompilerParams(vmem_limit_bytes=12 * 2**20),
        cost_estimate=pl.CostEstimate(flops=10000000, bytes_accessed=4 * count * rows * whole, transcendentals=0),
    )(*arrays, *earlier)


def exchange(blocks, axis):
    return lax.all_to_all(blocks, axis, 0, 0, tiled=True)


def from_everyone(array, axis):
    peers = lax.axis_size(axis)
    return exchange(jnp.broadcast_to(array[None], (peers, *array.shape)), axis)


def two_parts(values):
    high = lax.reduce_precision(values, 8, 7)
    return high.astype(BF16), (values - high).astype(BF16)


def with_scalars(array, scalars):
    high, low = two_parts(scalars)
    spare = -(array.shape[-1] + 2) % 128
    tail = jnp.stack([high, low] + [jnp.zeros_like(high)] * spare, axis=-1)
    return jnp.concatenate([array, tail], axis=-1)


def column(index, values, lanes):
    return jnp.where(lax.broadcasted_iota(jnp.int32, (values.shape[0], lanes), 1) == index, values, 0.0)


def logits_kernel(inner_total, mixed, both, gains, lm_own, lm_other, out):
    rows = lm_own.shape[0]
    vocab = lm_own.shape[1]
    core = lax.axis_index("core")
    at = lax.axis_index("x") * 4 + lax.axis_index("z") * 2 + core
    total = mixed[0].astype(F32)
    for k in range(1, mixed.shape[0]):
        total = total + mixed[k].astype(F32)
    square = total[:, 2 * rows : 2 * rows + 1] + total[:, 2 * rows + 1 : 2 * rows + 2]
    scale = lax.rsqrt(square / inner_total + EPSILON)
    left = both[:, 2 * rows : 3 * rows].astype(F32)
    right = both[:, 3 * rows : 4 * rows].astype(F32)
    stream_own = jnp.where(core == 0, left, right) + scale * total[:, :rows]
    stream_other = jnp.where(core == 0, right, left) + scale * total[:, rows : 2 * rows]
    squares = jnp.sum(stream_own * stream_own, axis=-1, keepdims=True) + jnp.sum(
        stream_other * stream_other, axis=-1, keepdims=True
    )
    final_own = (stream_own * gains[pl.ds(at, 1), :]).astype(BF16)
    final_other = (stream_other * gains[pl.ds(at + 1 - 2 * core, 1), :]).astype(BF16)
    wide = 640
    for start in range(0, vocab, wide):
        part = jnp.dot(final_own, lm_own[:, start : start + wide], preferred_element_type=F32)
        part = part + jnp.dot(final_other, lm_other[:, start : start + wide], preferred_element_type=F32)
        out[:, start : start + wide] = part.astype(BF16)
    high = squares.astype(BF16).astype(F32)
    out[:, vocab:] = (column(0, high, 128) + column(1, squares - high, 128)).astype(BF16)


def partial_logits(mixed, both, gains, lm_own, lm_other, inner_total):
    _, vocab = lm_own.shape
    return pl.pallas_call(
        functools.partial(logits_kernel, inner_total),
        out_shape=jax.ShapeDtypeStruct((both.shape[0], vocab + 128), BF16),
        compiler_params=pltpu.CompilerParams(vmem_limit_bytes=24 * 2**20),
        cost_estimate=pl.CostEstimate(flops=300000000, bytes_accessed=4000000, transcendentals=0),
    )(mixed, both, gains, lm_own, lm_other)


def stats_kernel(width, parts, reference, tokens, out):
    vocab = reference.shape[1]
    total = parts[0].astype(F32)
    for k in range(1, parts.shape[0]):
        total = total + parts[k].astype(F32)
    square = total[:, vocab : vocab + 1] + total[:, vocab + 1 : vocab + 2]
    logits = total[:, :vocab] * lax.rsqrt(square / width + EPSILON)
    rows = reference[...].astype(F32)
    columns = lax.axis_index("head") * vocab + lax.broadcasted_iota(jnp.int32, logits.shape, 1)
    picked = jnp.sum(jnp.where(columns == tokens[...], logits, 0.0), axis=-1, keepdims=True)
    roll_max = jnp.max(logits, axis=-1, keepdims=True)
    ref_max = jnp.max(rows, axis=-1, keepdims=True)
    roll_sum = jnp.sum(jnp.exp(logits - roll_max), axis=-1, keepdims=True)
    weights = jnp.exp(rows - ref_max)
    ref_sum = jnp.sum(weights, axis=-1, keepdims=True)
    cross = jnp.sum(weights * (rows - logits), axis=-1, keepdims=True)
    found = column(0, roll_max, 128)
    for index, values in enumerate((roll_sum, ref_max, ref_sum, cross, picked), 1):
        found = found + column(index, values, 128)
    turned = found.T[:8]
    for k in range(out.shape[0]):
        out[k, :, : turned.shape[1]] = turned
        out[k, :, turned.shape[1] :] = jnp.zeros((8, 128 - turned.shape[1]), F32)


def head_stats(parts, reference, tokens, width, peers):
    return pl.pallas_call(
        functools.partial(stats_kernel, width),
        out_shape=jax.ShapeDtypeStruct((peers, 8, 128), F32),
        compiler_params=pltpu.CompilerParams(vmem_limit_bytes=16 * 2**20),
        cost_estimate=pl.CostEstimate(flops=3000000, bytes_accessed=1000000, transcendentals=100000),
    )(parts, reference, tokens)


def combine_kernel(stats, divergence, logprob):
    rows = [[stats[k, j : j + 1, :] for j in range(6)] for k in range(stats.shape[0])]
    roll_top, ref_top = rows[0][0], rows[0][2]
    for row in rows[1:]:
        roll_top, ref_top = jnp.maximum(roll_top, row[0]), jnp.maximum(ref_top, row[2])
    roll_total = sum(row[1] * jnp.exp(row[0] - roll_top) for row in rows)
    scales = [jnp.exp(row[2] - ref_top) for row in rows]
    ref_total = sum(row[3] * scale for row, scale in zip(rows, scales))
    cross_total = sum(row[4] * scale for row, scale in zip(rows, scales))
    lse_roll = roll_top + jnp.log(roll_total)
    lse_ref = ref_top + jnp.log(ref_total)
    count = divergence.shape[1]
    divergence[...] = (cross_total / ref_total - lse_ref + lse_roll)[:, :count]
    logprob[...] = (sum(row[5] for row in rows) - lse_roll)[:, :count]


def combined(stats, seqs):
    return pl.pallas_call(
        combine_kernel,
        out_shape=(jax.ShapeDtypeStruct((1, seqs), F32),) * 2,
        cost_estimate=pl.CostEstimate(flops=100000, bytes_accessed=40000, transcendentals=0),
    )(stats)


def conv_branch(history, newest, taps, offset):
    total = newest * taps[3] + offset
    for k in range(3):
        total = total + history[:, k, :].astype(F32) * taps[k]
    return jax.nn.silu(total)


def shards(
    hidden_in,
    ssm_state,
    conv_x_state,
    conv_bc_state,
    token_ids,
    ref_logits,
    in_z,
    in_x,
    in_bc,
    in_dt,
    out_t,
    lm_head,
    conv_wx,
    conv_bx,
    conv_wbc,
    conv_bbc,
    dt_bias,
    a_log,
    skip_gain,
    norm_in,
    norm_gain,
    final_gain,
):
    chips = lax.axis_size(CHIPS)
    first_core = lax.axis_index("core") == 0
    seqs, width = hidden_in.shape
    rows, inner = in_z.shape
    heads = a_log.shape[0]
    state_size = in_bc.shape[1] // 2
    class_seqs = chips * seqs

    hidden_sent, scale = hidden_blocks(hidden_in, norm_in, chips)
    own = joined(in_z, in_x, in_bc, in_dt, out_t)
    in_cols = own.shape[1] - inner
    dt_at = 2 * inner + 2 * state_size
    other = from_partner(own)
    ahead = along_ring(own, 1)
    behind = along_ring(own, -1)
    over = from_opposite(own)
    lm_other = from_partner(lm_head)
    far = along_ring(ahead, 1)
    ahead_z = along_ring(over, 1)
    behind_z = along_ring(over, -1)
    far_z = along_ring(ahead_z, 1)
    pieces = {(0, 0, 0): own, (0, 0, 1): other}
    for at, piece in (
        ((0, 1), over),
        ((1, 0), ahead),
        ((3, 0), behind),
        ((1, 1), ahead_z),
        ((3, 1), behind_z),
        ((2, 0), far),
        ((2, 1), far_z),
    ):
        pieces.update({(*at, 0): piece, (*at, 1): from_partner(piece)})
    widths = (inner, inner, 2 * state_size, 128, inner)
    first, second = list(pieces)[:8], list(pieces)[8:]
    devices = 2 * chips
    rolled = placed({tag: pieces[tag] for tag in first}, devices, widths)
    rolled = placed({tag: pieces[tag] for tag in second}, devices, widths, rolled)
    roll_z, roll_x, roll_bc, dt_wide, roll_out = rolled
    roll_dt = dt_wide[:, :heads]

    def own_first(array):
        left, right = array[:, :rows], array[:, rows:]
        return jnp.where(first_core, left, right), jnp.where(first_core, right, left)

    both = exchange(hidden_sent, CHIPS)
    both = both.reshape(class_seqs, -1)
    normed_own, normed_other = own_first(both[:, : 2 * rows])

    partial_in = jnp.dot(normed_own, own[:, :in_cols], preferred_element_type=F32) + jnp.dot(
        normed_other, other[:, :in_cols], preferred_element_type=F32
    )
    partial_in = partial_in.astype(BF16).reshape(chips, seqs, in_cols)
    partial_in = exchange(partial_in, CHIPS)
    branches = jnp.sum(partial_in.astype(F32), axis=0) * scale[:, :1]
    gate = branches[:, :inner]
    x_conv = conv_branch(conv_x_state, branches[:, inner : 2 * inner], conv_wx, conv_bx)
    bc_conv = conv_branch(conv_bc_state, branches[:, 2 * inner : dt_at], conv_wbc, conv_bbc)
    b_vals, c_vals = bc_conv[:, :state_size], bc_conv[:, state_size:]
    step = jax.nn.softplus(branches[:, dt_at : dt_at + heads] + dt_bias)
    decay = jnp.exp(-step * jnp.exp(a_log))
    x_heads = x_conv.reshape(seqs, heads, P_SIZE)
    inflow = (step[:, :, None] * x_heads)[:, :, :, None] * b_vals[:, None, None, :]
    new_state = decay[:, :, None, None] * ssm_state + inflow
    carried = jnp.einsum("shpn,sn->shp", ssm_state, c_vals)
    overlap = jnp.sum(b_vals * c_vals, axis=-1)
    direct = step * overlap[:, None] + skip_gain
    ssm_out = (decay[:, :, None] * carried + direct[:, :, None] * x_heads).reshape(seqs, inner)
    gated = (ssm_out * jax.nn.silu(gate)).astype(BF16)

    gated = from_everyone(gated, CHIPS)
    gated = gated.reshape(class_seqs, inner).astype(F32)
    squares = jnp.sum(gated * gated, axis=-1)
    gained = (gated * norm_gain).astype(BF16)
    across = (((1,), (1,)), ((), ()))
    mix_own = lax.dot_general(gained, out_t, across, preferred_element_type=F32)
    mix_other = lax.dot_general(gained, other[:, in_cols:], across, preferred_element_type=F32)
    mix = jnp.concatenate([mix_own.astype(BF16), mix_other.astype(BF16)], axis=-1)
    mix = with_scalars(mix, squares)
    mix = from_everyone(mix, "head")

    sent = partial_logits(
        mix, both, final_gain.reshape(-1, rows), lm_head.T, lm_other.T, inner * lax.axis_size("head")
    )
    parts = exchange(sent.reshape(chips, seqs, -1), CHIPS)
    stats = head_stats(parts, ref_logits, token_ids[:, None], width, lax.axis_size("head"))
    stats = exchange(stats, "head")
    divergence, token_logprob = combined(stats, seqs)
    divergence, token_logprob = divergence[0], token_logprob[0]
    return (new_state, divergence, token_logprob, roll_z, roll_x, roll_bc, roll_dt, roll_out)


def solution(mesh):
    group, head = mesh.devices.shape
    fine = Mesh(mesh.devices.reshape(group // 4, 2, 2, head), ("x", "z", "core", "head"))
    return jax.shard_map(
        shards,
        mesh=fine,
        in_specs=(
            P(GROUP, None),
            P(GROUP, "head", None, None),
            P(GROUP, None, "head"),
            P(GROUP, None, None),
            P(GROUP),
            P(GROUP, "head"),
            P(GROUP, "head"),
            P(GROUP, "head"),
            P(GROUP, None),
            P(GROUP, "head"),
            P(GROUP, "head"),
            P("head", GROUP),
            P(None, "head"),
            P("head"),
            P(),
            P(),
            P("head"),
            P("head"),
            P("head"),
            P(),
            P("head"),
            P(),
        ),
        out_specs=(
            P(GROUP, "head", None, None),
            P(GROUP),
            P(GROUP),
            P(None, "head"),
            P(None, "head"),
            P(),
            P(None, "head"),
            P(None, "head"),
        ),
        check_vma=False,
    )
```

time: 144 us -> 142 us (0.986)
  Pallas kernels: 0 us -> 19.9 us
  local copies, waits for them, and re-layouts: 24.3 us -> 8.42 us
  starting transfers between devices: 28.4 us -> 43.7 us
  between operations: 14.6 us -> 1.03 us
  blocking collectives: 11.2 us -> 0 us
  waiting for transfers between devices: 45.9 us -> 52.7 us
  other arithmetic: 11.6 us -> 7.44 us
    ppermute x0 -> x7, waiting for transfers between devices: none -> 29.1 us  [the longest x6 29.1 us: along_ring(): return lax.ppermute(array, ('x', 'core'), pairs)]
    all_to_all x5 -> x6, waiting for transfers between devices: 45.8 us -> 23.6 us  [exchange(): return lax.all_to_all(blocks, axis, 0, 0, tiled=True)]
    pallas_call x0 -> x7, Pallas kernels: none -> 19.9 us  [the longest x2 10.5 us: placed(): pl.pallas_call(functools.partial(placed_kernel, tags, widths), out_shape=...]
    all_to_all x1 -> x0, blocking collectives: 11.2 us -> none  [exchange(): return lax.all_to_all(blocks, axis, 0, 0, tiled=True)]
    slice x3 -> x1, local copies, waits for them, and re-layouts: 10.7 us -> 0.81 us  [shards(): branches = jnp.sum(partial_in.astype(F32), axis=0) * scale[:, :1]]
    ppermute x0 -> x7, starting transfers between devices: none -> 8.69 us  [the longest x6 6.67 us: along_ring(): return lax.ppermute(array, ('x', 'core'), pairs)]
    all_to_all x5 -> x6, starting transfers between devices: 28.2 us -> 34.2 us  [exchange(): return lax.all_to_all(blocks, axis, 0, 0, tiled=True)]
    unnamed x44 -> x36, local copies, waits for them, and re-layouts: 6.38 us -> 3.98 us
  transfers between devices with their start and end apart: 8 -> 22, of which waited for: 5 -> 9; matrix products, arithmetic and copies ran while one was open for 18% -> 14% of each run, Pallas kernels for 0% -> 9%
where the time goes in v2:
time: 142 us; the launch traced here: 141 us
  waiting for transfers between devices  52.7 us (37%)
  starting transfers between devices  43.7 us (31%)
  Pallas kernels  19.9 us (14%)
  local copies, waits for them, and re-layouts  8.42 us (6%)
  matrix products  7.53 us (5%)
  other arithmetic  7.44 us (5%)
    all_to_all x6, starting transfers between devices, exchange(): return lax.all_to_all(blocks, axis, 0, 0, tiled=True)  34.2 us
    ppermute x6, waiting for transfers between devices, along_ring(): return lax.ppermute(array, ('x', 'core'), pairs)  29.1 us
    all_to_all x6, waiting for transfers between devices, exchange(): return lax.all_to_all(blocks, axis, 0, 0, tiled=True)  23.6 us
    pallas_call x2, Pallas kernels, placed(): pl.pallas_call(functools.partial(placed_kernel, tags, widths), out_shape=...  10.5 us
    ppermute x6, starting transfers between devices, along_ring(): return lax.ppermute(array, ('x', 'core'), pairs)  6.67 us
    add x1, other arithmetic, shards(): new_state = decay[:, :, None, None] * ssm_state + inflow  6.02 us
    dot_general x1, matrix products, shards(): carried = jnp.einsum('shpn,sn->shp', ssm_state, c_vals)  4.61 us
    unnamed x36, local copies, waits for them, and re-layouts  3.98 us
  transfers between devices with their start and end apart: 22, of which 9 were waited for; matrix products, arithmetic and copies ran while one was open for 14% of the time, Pallas kernels for 9%

profile of v2, /device:TPU:0, one launch (start us, length us, event | category | flops | bytes accessed | tf_op | source)
XLA Modules:
  0.0 140.7 jit_solution(6666907770259650035)
XLA Ops:
  0.7 1.5 %copy.43.in_dt = bf16[160,10]{1,0:T(8,128)(2,1)} copy(bf16[160,10]{0,1:T(8,128)(2,1)} %param.31) | data formatting | bytes 6400 | tf_op args[9]
  2.2 2.1 %shard_map.270.refs_0_ = bf16[160,2304]{1,0:T(8,128)(2,1)} custom-call(bf16[160,640]{1,0:T(8,128)(2,1)} %in_z.1, bf16[160,640]{1,0:T(8,128)(2,1)} %in_x.1, bf16[160,256]{1,0:T(8,128)(2,1)} %in_bc.1, bf16[160,10]{1,0:T(8,128)(2,1)} %copy.43.in_dt, bf16[160,640]{1,0:T(8,128)(2,1)} %out_t.1), custom_call_target="tpu_custom_call" | custom-call | flops 2000000 | bytes 1474560 | tf_op jit(solution)/shard_map/pallas_call | solution.py:50
  4.3 1.3 reshape.103.gain
  5.6 1.7 %shard_map.269 = (bf16[8,16,640]{2,1,0:T(8,128)(2,1)}, f32[16,128]{1,0:T(8,128)}) custom-call(bf16[16,2560]{1,0:T(8,128)(2,1)} %hidden.1, f32[1,2560]{1,0:T(1,128)} %reshape.103.gain), custom_call_target="tpu_custom_call" | custom-call | flops 1000000 | bytes 300000 | tf_op jit(solution)/shard_map/pallas_call | solution.py:70
  7.3 5.8 %all-to-all-start = ((bf16[8,16,640]{2,1,0:T(8,128)(2,1)}), bf16[8,16,640]{2,1,0:T(8,128)(2,1)S(1)}, u32[]{:S(2)}, u32[]{:S(2)}) async-start(bf16[8,16,640]{2,1,0:T(8,128)(2,1)} %get-tuple-element.22), calls=%async_computation | async-start | bytes 327680 | tf_op jit(solution)/shard_map/all_to_all | solution.py:132
  13.1 2.0 %collective-permute-start.2 = (bf16[160,2304]{1,0:T(8,128)(2,1)}, bf16[160,2304]{1,0:T(8,128)(2,1)}, u32[]{:S(2)}, u32[]{:S(2)}) collective-permute-start(bf16[160,2304]{1,0:T(8,128)(2,1)} %shard_map.270.refs_0_), channel_id=1, source_target_pairs={{0,16},{16,0},{1,17},{17,1},{2,18},{18,2},{3,19},{19,3},{4,20},{20... | collective-permute-start | bytes 2211848 | tf_op jit(solution)/shard_map/ppermute | solution.py:24
  15.1 4.7 %all-to-all-done = bf16[8,16,640]{2,1,0:T(8,128)(2,1)S(1)} async-done(((bf16[8,16,640]{2,1,0:T(8,128)(2,1)}), bf16[8,16,640]{2,1,0:T(8,128)(2,1)S(1)}, u32[]{:S(2)}, u32[]{:S(2)}) %all-to-all-start) | async-done | bytes 163872 | tf_op jit(solution)/shard_map/all_to_all | solution.py:132
  19.8 1.4 fusion.2
  21.3 1.1 fusion
  22.4 3.5 %all-to-all-start.1 = ((bf16[8,16,1664]{2,1,0:T(8,128)(2,1)}), bf16[8,16,1664]{2,1,0:T(8,128)(2,1)S(1)}, u32[]{:S(2)}, u32[]{:S(2)}) async-start(bf16[8,16,1664]{2,1,0:T(8,128)(2,1)} %bitcast.1), calls=%async_computation.1 | async-start | bytes 851968 | tf_op jit(solution)/shard_map/all_to_all | solution.py:132
  25.9 0.8 slice_reduce_fusion
  26.8 11.5 %all-to-all-done.1 = bf16[8,16,1664]{2,1,0:T(8,128)(2,1)S(1)} async-done(((bf16[8,16,1664]{2,1,0:T(8,128)(2,1)}), bf16[8,16,1664]{2,1,0:T(8,128)(2,1)S(1)}, u32[]{:S(2)}, u32[]{:S(2)}) %all-to-all-start.1) | async-done | bytes 426016 | tf_op jit(solution)/shard_map/all_to_all | solution.py:132
  38.4 0.1 fusion.24
  38.7 4.6 %fusion.26 = f32[16,1,10,64]{3,1,2,0:T(1,128)S(1)} fusion(f32[16,128,1,1]{1,2,3,0:T(1,128)S(1)} %bitcast.52, f32[16,10,64,128]{3,2,1,0:T(8,128)} %param.23), kind=kOutput, calls=%fused_computation.59 | convolution fusion | flops 2621440 | bytes 5292032 | tf_op jit(solution)/shard_map/shpn,sn->shp/dot_general | solution.py:346
  43.4 0.8 fusion.6
  44.4 0.7 broadcast_in_dim.6
  45.0 4.2 %all-to-all-start.2 = ((bf16[8,16,640]{2,1,0:T(8,128)(2,1)}), bf16[8,16,640]{2,1,0:T(8,128)(2,1)S(1)}, u32[]{:S(2)}, u32[]{:S(2)}) async-start(bf16[8,16,640]{2,1,0:T(8,128)(2,1)} %broadcast_in_dim.6), calls=%async_computation.2 | async-start | bytes 327680 | tf_op jit(solution)/shard_map/all_to_all | solution.py:132
  49.3 2.0 %collective-permute-start.7 = (bf16[160,2304]{1,0:T(8,128)(2,1)S(1)}, bf16[160,2304]{1,0:T(8,128)(2,1)}, u32[]{:S(2)}, u32[]{:S(2)}) collective-permute-start(bf16[160,2304]{1,0:T(8,128)(2,1)S(1)} %copy-done), channel_id=1, source_target_pairs={{0,32},{8,104},{32,64},{40,8},{64,96},{72,40},{96,0},{104,72},{1,3... | collective-permute-start | bytes 2211848 | tf_op jit(solution)/shard_map/ppermute | solution.py:34
  51.3 1.3 collective-permute-start.14
  52.6 0.8 collective-permute-start.3
  53.4 2.9 %all-to-all-done.2 = bf16[8,16,640]{2,1,0:T(8,128)(2,1)S(1)} async-done(((bf16[8,16,640]{2,1,0:T(8,128)(2,1)}), bf16[8,16,640]{2,1,0:T(8,128)(2,1)S(1)}, u32[]{:S(2)}, u32[]{:S(2)}) %all-to-all-start.2) | async-done | bytes 163872 | tf_op jit(solution)/shard_map/all_to_all | solution.py:132
  56.4 0.2 convolution_convert_fusion.1
  56.6 0.1 multiply_reduce_fusion
  56.8 0.2 convolution_convert_fusion
  57.1 0.1 concatenate.23
  57.2 0.1 copy.44
  57.3 1.0 broadcast_in_dim.7
  58.2 7.5 %all-to-all-start.3 = ((bf16[8,128,384]{2,1,0:T(8,128)(2,1)}), bf16[8,128,384]{2,1,0:T(8,128)(2,1)S(1)}, u32[]{:S(2)}, u32[]{:S(2)}) async-start(bf16[8,128,384]{2,1,0:T(8,128)(2,1)} %broadcast_in_dim.7), calls=%async_computation.3 | async-start | bytes 1572864 | tf_op jit(solution)/shard_map/all_to_all | solution.py:132
  65.8 4.7 %collective-permute-done.7.refs_4_ = bf16[160,2304]{1,0:T(8,128)(2,1)} collective-permute-done((bf16[160,2304]{1,0:T(8,128)(2,1)S(1)}, bf16[160,2304]{1,0:T(8,128)(2,1)}, u32[]{:S(2)}, u32[]{:S(2)}) %collective-permute-start.7) | collective-permute-done | bytes 737312 | tf_op jit(solution)/shard_map/ppermute | solution.py:34
  70.5 0.3 collective-permute-done.14.refs_6_
  70.8 2.5 %collective-permute-start.5 = (bf16[160,2304]{1,0:T(8,128)(2,1)}, bf16[160,2304]{1,0:T(8,128)(2,1)}, u32[]{:S(2)}, u32[]{:S(2)}) collective-permute-start(bf16[160,2304]{1,0:T(8,128)(2,1)} %collective-permute-done.2.refs_2_), channel_id=1, source_target_pairs={{0,96},{8,40},{32,0},{40,72},{64,32},{72,104},{96,64},{104,8},{1,9... | collective-permute-start | bytes 2211848 | tf_op jit(solution)/shard_map/ppermute | solution.py:34
  73.3 8.7 %collective-permute-done.3.refs_0_ = bf16[160,2304]{1,0:T(8,128)(2,1)} collective-permute-done((bf16[160,2304]{1,0:T(8,128)(2,1)}, bf16[160,2304]{1,0:T(8,128)(2,1)}, u32[]{:S(2)}, u32[]{:S(2)}) %collective-permute-start.3) | collective-permute-done | bytes 737312 | tf_op jit(solution)/shard_map/ppermute | solution.py:34
  82.1 3.1 %shard_map.271 = bf16[128,3328]{1,0:T(8,128)(2,1)} custom-call(bf16[8,128,384]{2,1,0:T(8,128)(2,1)S(1)} %all-to-all-done.3.mixed, bf16[128,640]{1,0:T(8,128)(2,1)S(1)} %bitcast.50, f32[16,160]{1,0:T(8,128)S(1)} %reshape.108.gains, bf16[160,3200]{1,0:T(8,128)(2,1)S(1)} %bitcast.51, bf16[160,3200]{1,0:T(8,128)(2,1)} %bitcast.17.lm_other), custom_call_target="tpu_custom_call" | custom-call | flops 300000000 | bytes 4000000 | tf_op jit(solution)/shard_map/pallas_call | solution.py:186
  85.2 5.7 %all-to-all-start.4 = ((bf16[8,16,3328]{2,1,0:T(8,128)(2,1)}), bf16[8,16,3328]{2,1,0:T(8,128)(2,1)S(1)}, u32[]{:S(2)}, u32[]{:S(2)}) async-start(bf16[8,16,3328]{2,1,0:T(8,128)(2,1)} %bitcast.18), calls=%async_computation.4 | async-start | bytes 1703936 | tf_op jit(solution)/shard_map/all_to_all | solution.py:132
  91.0 0.5 collective-permute-start.4
  91.5 0.3 collective-permute-start.6
  91.8 5.4 %collective-permute-done.8.refs_4_ = bf16[160,2304]{1,0:T(8,128)(2,1)} collective-permute-done((bf16[160,2304]{1,0:T(8,128)(2,1)}, bf16[160,2304]{1,0:T(8,128)(2,1)}, u32[]{:S(2)}, u32[]{:S(2)}) %collective-permute-start.8) | collective-permute-done | bytes 737312 | tf_op jit(solution)/shard_map/ppermute | solution.py:34
  97.2 10.0 %collective-permute-done.10.refs_6_ = bf16[160,2304]{1,0:T(8,128)(2,1)} collective-permute-done((bf16[160,2304]{1,0:T(8,128)(2,1)}, bf16[160,2304]{1,0:T(8,128)(2,1)}, u32[]{:S(2)}, u32[]{:S(2)}) %collective-permute-start.10) | collective-permute-done | bytes 737312 | tf_op jit(solution)/shard_map/ppermute | solution.py:34
  107.3 4.5 %all-to-all-done.4.parts = bf16[8,16,3328]{2,1,0:T(8,128)(2,1)S(1)} async-done(((bf16[8,16,3328]{2,1,0:T(8,128)(2,1)}), bf16[8,16,3328]{2,1,0:T(8,128)(2,1)S(1)}, u32[]{:S(2)}, u32[]{:S(2)}) %all-to-all-start.4) | async-done | bytes 852000 | tf_op jit(solution)/shard_map/all_to_all | solution.py:132
  111.8 0.9 copy-done.2
  112.7 1.1 shard_map.272
  113.8 7.5 %all-to-all-start.5 = ((f32[8,8,128]{2,1,0:T(8,128)}), f32[8,8,128]{2,1,0:T(8,128)S(1)}, u32[]{:S(2)}, u32[]{:S(2)}) async-start(f32[8,8,128]{2,1,0:T(8,128)} %shard_map.272), calls=%async_computation.5 | async-start | bytes 65536 | tf_op jit(solution)/shard_map/all_to_all | solution.py:132
  121.2 6.0 %multiply_add_fusion = f32[16,10,64,128]{3,2,1,0:T(8,128)} fusion(f32[16,10,64,128]{3,2,1,0:T(8,128)} %param.23, f32[16,128]{1,0:T(8,128)S(1)} %get-tuple-element.70, f32[16,10,64]{2,1,0:T(8,128)} %get-tuple-element.67, f32[16,10]{1,0:T(8,128)S(1)} %multiply_exponential_fusion), kind=kLoop, calls=%fused_computation | loop fusion | flops 3932160 | bytes 10535552 | tf_op jit(solution)/shard_map/add | solution.py:345
  127.3 5.1 %shard_map.274 = (bf16[2560,640]{1,0:T(8,128)(2,1)}, bf16[2560,640]{1,0:T(8,128)(2,1)}, bf16[2560,256]{1,0:T(8,128)(2,1)}, bf16[2560,128]{1,0:T(8,128)(2,1)S(1)}, bf16[2560,640]{1,0:T(8,128)(2,1)}) custom-call(bf16[160,2304]{1,0:T(8,128)(2,1)S(1)} %copy-done, bf16[160,2304]{1,0:T(8,128)(2,1)S(1)} %collective-permute-done.refs_1_, ...), custom_call_target="tpu_custom_call" | custom-call | flops 10000000 | bytes 11796480 | tf_op jit(solution)/shard_map/pallas_call | solution.py:115
  132.4 0.6 copy-done.4
  133.0 1.3 shard_map.273
  134.3 5.4 %shard_map.275 = (bf16[2560,640]{1,0:T(8,128)(2,1)}, bf16[2560,640]{1,0:T(8,128)(2,1)}, bf16[2560,256]{1,0:T(8,128)(2,1)}, bf16[2560,128]{1,0:T(8,128)(2,1)S(1)}, bf16[2560,640]{1,0:T(8,128)(2,1)}) custom-call(bf16[160,2304]{1,0:T(8,128)(2,1)} %collective-permute-done.3.refs_0_, ...), custom_call_target="tpu_custom_call", output_to_operand_aliasing={{0}: (8, {}), {1}: (9, {}), {2}: (10, {}), {3}: (11, {}), {... | custom-call | flops 10000000 | bytes 11796480 | tf_op jit(solution)/shard_map/pallas_call | solution.py:115
  139.8 0.9 copy.46
  (76 shorter events, 1.0 us)
Async XLA Ops:
  0.6 26.0 %copy-start.16 = (f32[10]{0:T(128)S(1)}, f32[10]{0:T(128)}, u32[]{:S(2)}) copy-start(f32[10]{0:T(128)} %param.39) | copy-start | bytes 124
  0.6 26.0 %copy-start.8 = (f32[4,640]{1,0:T(4,128)S(1)}, f32[4,640]{1,0:T(4,128)}, u32[]{:S(2)}) copy-start(f32[4,640]{1,0:T(4,128)} %param.34) | copy-start | bytes 30724
  0.7 26.1 %copy-start.10 = (f32[4,256]{1,0:T(4,128)S(1)}, f32[4,256]{1,0:T(4,128)}, u32[]{:S(2)}) copy-start(f32[4,256]{1,0:T(4,128)} %param.36) | copy-start | bytes 12292
  0.7 37.7 %copy-start.6 = (bf16[16,3,256]{2,0,1:T(8,128)(2,1)S(1)}, bf16[16,3,256]{2,0,1:T(8,128)(2,1)}, u32[]{:S(2)}) copy-start(bf16[16,3,256]{2,0,1:T(8,128)(2,1)} %param.25) | copy-start | bytes 73732
  0.7 37.7 %copy-start.12 = (f32[256]{0:T(256)S(1)}, f32[256]{0:T(256)}, u32[]{:S(2)}) copy-start(f32[256]{0:T(256)} %param.37) | copy-start | bytes 3076
  0.7 37.8 %copy-start.5 = (bf16[16,3,640]{2,0,1:T(8,128)(2,1)S(1)}, bf16[16,3,640]{2,0,1:T(8,128)(2,1)}, u32[]{:S(2)}) copy-start(bf16[16,3,640]{2,0,1:T(8,128)(2,1)} %param.24) | copy-start | bytes 184324
  0.7 37.8 %copy-start.9 = (f32[640]{0:T(1024)S(1)}, f32[640]{0:T(1024)}, u32[]{:S(2)}) copy-start(f32[640]{0:T(1024)} %param.35) | copy-start | bytes 7684
  4.3 17.0 %collective-permute-start = (bf16[160,2304]{1,0:T(8,128)(2,1)}, bf16[160,2304]{1,0:T(8,128)(2,1)S(1)}, u32[]{:S(2)}, u32[]{:S(2)}) collective-permute-start(bf16[160,2304]{1,0:T(8,128)(2,1)} %shard_map.270.refs_0_), channel_id=1, source_target_pairs={{0,8},{8,0},{1,9},{9,1},{2,10},{10,2},{3,11},{11,3},{4,12},{12,4},... | collective-permute-start | bytes 2211848 | tf_op jit(solution)/shard_map/ppermute | solution.py:20
  7.3 12.5 %all-to-all-start = ((bf16[8,16,640]{2,1,0:T(8,128)(2,1)}), bf16[8,16,640]{2,1,0:T(8,128)(2,1)S(1)}, u32[]{:S(2)}, u32[]{:S(2)}) async-start(bf16[8,16,640]{2,1,0:T(8,128)(2,1)} %get-tuple-element.22), calls=%async_computation | async-start | bytes 327680 | tf_op jit(solution)/shard_map/all_to_all | solution.py:132
  13.1 39.5 %collective-permute-start.2 = (bf16[160,2304]{1,0:T(8,128)(2,1)}, bf16[160,2304]{1,0:T(8,128)(2,1)}, u32[]{:S(2)}, u32[]{:S(2)}) collective-permute-start(bf16[160,2304]{1,0:T(8,128)(2,1)} %shard_map.270.refs_0_), channel_id=1, source_target_pairs={{0,16},{16,0},{1,17},{17,1},{2,18},{18,2},{3,19},{19,3},{4,20},{20... | collective-permute-start | bytes 2211848 | tf_op jit(solution)/shard_map/ppermute | solution.py:24
  19.8 23.4 %copy-start.13 = (f32[10]{0:T(128)S(1)}, f32[10]{0:T(128)}, u32[]{:S(2)}) copy-start(f32[10]{0:T(128)} %param.40) | copy-start | bytes 124
  19.8 23.4 %copy-start.14 = (f32[10]{0:T(128)S(1)}, f32[10]{0:T(128)}, u32[]{:S(2)}) copy-start(f32[10]{0:T(128)} %param.38) | copy-start | bytes 124
  21.2 28.0 %copy-start = (bf16[160,2304]{1,0:T(8,128)(2,1)S(1)}, bf16[160,2304]{1,0:T(8,128)(2,1)}, u32[]{:S(2)}) copy-start(bf16[160,2304]{1,0:T(8,128)(2,1)} %shard_map.270.refs_0_) | copy-start | bytes 2211844
  21.2 31.3 %copy-start.1 = (bf16[3200,160]{0,1:T(8,128)(2,1)S(1)}, bf16[3200,160]{0,1:T(8,128)(2,1)}, u32[]{:S(2)}) copy-start(bf16[3200,160]{0,1:T(8,128)(2,1)} %param.33) | copy-start | bytes 3072004
  21.3 35.0 %copy-start.11 = (f32[640]{0:T(1024)S(1)}, f32[640]{0:T(1024)}, u32[]{:S(2)}) copy-start(f32[640]{0:T(1024)} %param.42) | copy-start | bytes 7684
  21.3 35.1 %copy-start.3 = (bf16[160,640]{1,0:T(8,128)(2,1)S(1)}, bf16[160,640]{1,0:T(8,128)(2,1)}, u32[]{:S(2)}) copy-start(bf16[160,640]{1,0:T(8,128)(2,1)} %out_t.1) | copy-start | bytes 614404
  22.4 15.8 %all-to-all-start.1 = ((bf16[8,16,1664]{2,1,0:T(8,128)(2,1)}), bf16[8,16,1664]{2,1,0:T(8,128)(2,1)S(1)}, u32[]{:S(2)}, u32[]{:S(2)}) async-start(bf16[8,16,1664]{2,1,0:T(8,128)(2,1)} %bitcast.1), calls=%async_computation.1 | async-start | bytes 851968 | tf_op jit(solution)/shard_map/all_to_all | solution.py:132
  38.7 43.4 %copy-start.7 = (f32[2560]{0:T(1024)S(1)}, f32[2560]{0:T(1024)}, u32[]{:S(2)}) copy-start(f32[2560]{0:T(1024)} %param.43) | copy-start | bytes 30724
  44.3 62.9 %copy-start.15 = (s32[16]{0:T(128)S(1)}, s32[16]{0:T(128)}, u32[]{:S(2)}) copy-start(s32[16]{0:T(128)} %param.26) | copy-start | bytes 196
  45.0 11.3 %all-to-all-start.2 = ((bf16[8,16,640]{2,1,0:T(8,128)(2,1)}), bf16[8,16,640]{2,1,0:T(8,128)(2,1)S(1)}, u32[]{:S(2)}, u32[]{:S(2)}) async-start(bf16[8,16,640]{2,1,0:T(8,128)(2,1)} %broadcast_in_dim.6), calls=%async_computation.2 | async-start | bytes 327680 | tf_op jit(solution)/shard_map/all_to_all | solution.py:132
  49.3 21.2 %collective-permute-start.7 = (bf16[160,2304]{1,0:T(8,128)(2,1)S(1)}, bf16[160,2304]{1,0:T(8,128)(2,1)}, u32[]{:S(2)}, u32[]{:S(2)}) collective-permute-start(bf16[160,2304]{1,0:T(8,128)(2,1)S(1)} %copy-done), channel_id=1, source_target_pairs={{0,32},{8,104},{32,64},{40,8},{64,96},{72,40},{96,0},{104,72},{1,3... | collective-permute-start | bytes 2211848 | tf_op jit(solution)/shard_map/ppermute | solution.py:34
  51.3 19.5 %collective-permute-start.14 = (bf16[160,2304]{1,0:T(8,128)(2,1)S(1)}, bf16[160,2304]{1,0:T(8,128)(2,1)}, u32[]{:S(2)}, u32[]{:S(2)}) collective-permute-start(bf16[160,2304]{1,0:T(8,128)(2,1)S(1)} %copy-done), channel_id=1, source_target_pairs={{0,96},{8,40},{32,0},{40,72},{64,32},{72,104},{96,64},{104,8},{1,9... | collective-permute-start | bytes 2211848 | tf_op jit(solution)/shard_map/ppermute | solution.py:34
  52.6 20.7 %collective-permute-start.1 = (bf16[3200,160]{0,1:T(8,128)(2,1)S(1)}, bf16[3200,160]{0,1:T(8,128)(2,1)}, u32[]{:S(2)}, u32[]{:S(2)}) collective-permute-start(bf16[3200,160]{0,1:T(8,128)(2,1)S(1)} %copy-done.1), channel_id=1, source_target_pairs={{0,8},{8,0},{1,9},{9,1},{2,10},{10,2},{3,11},{11,3},{4,12},{12,4},... | collective-permute-start | bytes 3072008 | tf_op jit(solution)/shard_map/ppermute | solution.py:20
  52.6 29.4 %collective-permute-start.3 = (bf16[160,2304]{1,0:T(8,128)(2,1)}, bf16[160,2304]{1,0:T(8,128)(2,1)}, u32[]{:S(2)}, u32[]{:S(2)}) collective-permute-start(bf16[160,2304]{1,0:T(8,128)(2,1)} %collective-permute-done.2.refs_2_), channel_id=1, source_target_pairs={{0,32},{8,104},{32,64},{40,8},{64,96},{72,40},{96,0},{104,72},{1,3... | collective-permute-start | bytes 2211848 | tf_op jit(solution)/shard_map/ppermute | solution.py:34
  58.2 23.8 %all-to-all-start.3 = ((bf16[8,128,384]{2,1,0:T(8,128)(2,1)}), bf16[8,128,384]{2,1,0:T(8,128)(2,1)S(1)}, u32[]{:S(2)}, u32[]{:S(2)}) async-start(bf16[8,128,384]{2,1,0:T(8,128)(2,1)} %broadcast_in_dim.7), calls=%async_computation.3 | async-start | bytes 1572864 | tf_op jit(solution)/shard_map/all_to_all | solution.py:132
  65.7 25.2 %collective-permute-start.12 = (bf16[160,2304]{1,0:T(8,128)(2,1)}, bf16[160,2304]{1,0:T(8,128)(2,1)}, u32[]{:S(2)}, u32[]{:S(2)}) collective-permute-start(bf16[160,2304]{1,0:T(8,128)(2,1)} %collective-permute-done.2.refs_2_), channel_id=1, source_target_pairs={{0,8},{8,0},{1,9},{9,1},{2,10},{10,2},{3,11},{11,3},{4,12},{12,4},... | collective-permute-start | bytes 2211848 | tf_op jit(solution)/shard_map/ppermute | solution.py:20
  70.4 20.6 %collective-permute-start.13 = (bf16[160,2304]{1,0:T(8,128)(2,1)}, bf16[160,2304]{1,0:T(8,128)(2,1)}, u32[]{:S(2)}, u32[]{:S(2)}) collective-permute-start(bf16[160,2304]{1,0:T(8,128)(2,1)} %collective-permute-done.7.refs_4_), channel_id=1, source_target_pairs={{0,8},{8,0},{1,9},{9,1},{2,10},{10,2},{3,11},{11,3},{4,12},{12,4},... | collective-permute-start | bytes 2211848 | tf_op jit(solution)/shard_map/ppermute | solution.py:20
  70.8 20.7 %collective-permute-start.5 = (bf16[160,2304]{1,0:T(8,128)(2,1)}, bf16[160,2304]{1,0:T(8,128)(2,1)}, u32[]{:S(2)}, u32[]{:S(2)}) collective-permute-start(bf16[160,2304]{1,0:T(8,128)(2,1)} %collective-permute-done.2.refs_2_), channel_id=1, source_target_pairs={{0,96},{8,40},{32,0},{40,72},{64,32},{72,104},{96,64},{104,8},{1,9... | collective-permute-start | bytes 2211848 | tf_op jit(solution)/shard_map/ppermute | solution.py:34
  73.3 23.8 %collective-permute-start.8 = (bf16[160,2304]{1,0:T(8,128)(2,1)}, bf16[160,2304]{1,0:T(8,128)(2,1)}, u32[]{:S(2)}, u32[]{:S(2)}) collective-permute-start(bf16[160,2304]{1,0:T(8,128)(2,1)} %collective-permute-done.7.refs_4_), channel_id=1, source_target_pairs={{0,32},{8,104},{32,64},{40,8},{64,96},{72,40},{96,0},{104,72},{1,3... | collective-permute-start | bytes 2211848 | tf_op jit(solution)/shard_map/ppermute | solution.py:34
  82.0 25.2 %collective-permute-start.10 = (bf16[160,2304]{1,0:T(8,128)(2,1)}, bf16[160,2304]{1,0:T(8,128)(2,1)}, u32[]{:S(2)}, u32[]{:S(2)}) collective-permute-start(bf16[160,2304]{1,0:T(8,128)(2,1)} %collective-permute-done.3.refs_0_), channel_id=1, source_target_pairs={{0,32},{8,104},{32,64},{40,8},{64,96},{72,40},{96,0},{104,72},{1,3... | collective-permute-start | bytes 2211848 | tf_op jit(solution)/shard_map/ppermute | solution.py:34
  85.2 26.6 %all-to-all-start.4 = ((bf16[8,16,3328]{2,1,0:T(8,128)(2,1)}), bf16[8,16,3328]{2,1,0:T(8,128)(2,1)S(1)}, u32[]{:S(2)}, u32[]{:S(2)}) async-start(bf16[8,16,3328]{2,1,0:T(8,128)(2,1)} %bitcast.18), calls=%async_computation.4 | async-start | bytes 1703936 | tf_op jit(solution)/shard_map/all_to_all | solution.py:132
  90.9 36.4 %collective-permute-start.15 = (bf16[160,2304]{1,0:T(8,128)(2,1)}, bf16[160,2304]{1,0:T(8,128)(2,1)S(1)}, u32[]{:S(2)}, u32[]{:S(2)}) collective-permute-start(bf16[160,2304]{1,0:T(8,128)(2,1)} %collective-permute-done.14.refs_6_), channel_id=1, source_target_pairs={{0,8},{8,0},{1,9},{9,1},{2,10},{10,2},{3,11},{11,3},{4,12},{12,4},... | collective-permute-start | bytes 2211848 | tf_op jit(solution)/shard_map/ppermute | solution.py:20
  91.0 43.3 %collective-permute-start.4 = (bf16[160,2304]{1,0:T(8,128)(2,1)}, bf16[160,2304]{1,0:T(8,128)(2,1)}, u32[]{:S(2)}, u32[]{:S(2)}) collective-permute-start(bf16[160,2304]{1,0:T(8,128)(2,1)} %collective-permute-done.3.refs_0_), channel_id=1, source_target_pairs={{0,8},{8,0},{1,9},{9,1},{2,10},{10,2},{3,11},{11,3},{4,12},{12,4},... | collective-permute-start | bytes 2211848 | tf_op jit(solution)/shard_map/ppermute | solution.py:20
  91.5 42.8 %collective-permute-start.6 = (bf16[160,2304]{1,0:T(8,128)(2,1)}, bf16[160,2304]{1,0:T(8,128)(2,1)}, u32[]{:S(2)}, u32[]{:S(2)}) collective-permute-start(bf16[160,2304]{1,0:T(8,128)(2,1)} %collective-permute-done.5.refs_2_), channel_id=1, source_target_pairs={{0,8},{8,0},{1,9},{9,1},{2,10},{10,2},{3,11},{11,3},{4,12},{12,4},... | collective-permute-start | bytes 2211848 | tf_op jit(solution)/shard_map/ppermute | solution.py:20
  97.2 37.2 %collective-permute-start.9 = (bf16[160,2304]{1,0:T(8,128)(2,1)}, bf16[160,2304]{1,0:T(8,128)(2,1)}, u32[]{:S(2)}, u32[]{:S(2)}) collective-permute-start(bf16[160,2304]{1,0:T(8,128)(2,1)} %collective-permute-done.8.refs_4_), channel_id=1, source_target_pairs={{0,8},{8,0},{1,9},{9,1},{2,10},{10,2},{3,11},{11,3},{4,12},{12,4},... | collective-permute-start | bytes 2211848 | tf_op jit(solution)/shard_map/ppermute | solution.py:20
  107.2 27.1 %collective-permute-start.11 = (bf16[160,2304]{1,0:T(8,128)(2,1)}, bf16[160,2304]{1,0:T(8,128)(2,1)}, u32[]{:S(2)}, u32[]{:S(2)}) collective-permute-start(bf16[160,2304]{1,0:T(8,128)(2,1)} %collective-permute-done.10.refs_6_), channel_id=1, source_target_pairs={{0,8},{8,0},{1,9},{9,1},{2,10},{10,2},{3,11},{11,3},{4,12},{12,4},... | collective-permute-start | bytes 2211848 | tf_op jit(solution)/shard_map/ppermute | solution.py:20
  111.8 0.9 copy-start.2
  113.8 18.6 %all-to-all-start.5 = ((f32[8,8,128]{2,1,0:T(8,128)}), f32[8,8,128]{2,1,0:T(8,128)S(1)}, u32[]{:S(2)}, u32[]{:S(2)}) async-start(f32[8,8,128]{2,1,0:T(8,128)} %shard_map.272), calls=%async_computation.5 | async-start | bytes 65536 | tf_op jit(solution)/shard_map/all_to_all | solution.py:132
  132.4 0.6 copy-start.4

commit v3 on v2

--- a/solution.py
+++ b/solution.py
@@ -34,31 +34,41 @@
     return lax.ppermute(array, ("x", "core"), pairs)
 
 
-def joined_kernel(in_z, in_x, in_bc, in_dt, out_t, own):
+def joined_kernel(in_z, in_x, in_bc, in_dt, out_t, own, sent):
     at = 0
     for part in (in_z, in_x, in_bc):
         own[:, at : at + part.shape[1]] = part[...]
+        sent[:, at : at + part.shape[1]] = part[...]
         at += part.shape[1]
-    own[:, at : at + 128] = jnp.zeros((own.shape[0], 128), own.dtype)
-    own[:, at : at + in_dt.shape[1]] = in_dt[...]
+    heads = in_dt.shape[0]
+    rows = lax.broadcasted_iota(jnp.int32, (heads, 128), 0)
+    same = rows == lax.broadcasted_iota(jnp.int32, (heads, 128), 1)
+    turned = lax.dot_general(
+        in_dt[...], same.astype(F32).astype(BF16), (((0,), (0,)), ((), ())), preferred_element_type=F32
+    )
+    own[:, at : at + 128] = turned.astype(own.dtype)
     own[:, at + 128 :] = out_t[...]
+    sent[:, at:] = out_t[...]
 
 
 def joined(in_z, in_x, in_bc, in_dt, out_t):
     rows, inner = in_z.shape
-    whole = 3 * inner + in_bc.shape[1] + 128
+    whole = 3 * inner + in_bc.shape[1]
     return pl.pallas_call(
         joined_kernel,
-        out_shape=jax.ShapeDtypeStruct((rows, whole), in_z.dtype),
+        out_shape=(
+            jax.ShapeDtypeStruct((rows, whole + 128), in_z.dtype),
+            jax.ShapeDtypeStruct((rows, whole), in_z.dtype),
+        ),
         cost_estimate=pl.CostEstimate(flops=2000000, bytes_accessed=2 * 2 * rows * whole, transcendentals=0),
-    )(in_z, in_x, in_bc, in_dt, out_t)
+    )(in_z, in_x, in_bc, in_dt.T, out_t)
 
 
 def blocks_kernel(hidden, gain, out, scale):
     values = hidden[...].astype(F32)
     mean = jnp.mean(values * values, axis=-1, keepdims=True)
     scale[...] = jnp.broadcast_to(lax.rsqrt(mean + EPSILON), scale.shape)
-    gained = (values * gain[...]).astype(out.dtype)
+    gained = (values * gain[...][None, :]).astype(out.dtype)
     wide = out.shape[2] // 2
     for k in range(out.shape[0]):
         out[k, :, :wide] = gained[:, k * wide : (k + 1) * wide]
@@ -74,7 +84,7 @@
             jax.ShapeDtypeStruct((seqs, 128), F32),
         ),
         cost_estimate=pl.CostEstimate(flops=1000000, bytes_accessed=300000, transcendentals=0),
-    )(hidden, gain.reshape(1, width))
+    )(hidden, gain)
 
 
 def placed_kernel(tags, widths, *refs):
@@ -83,7 +93,10 @@
     outs, (held, in_sems, out_sems) = refs[-len(widths) - 3 : -3], refs[-3:]
     rows = pieces[0].shape[0]
     x, z, core = (lax.axis_index(name) for name in ("x", "z", "core"))
-    reads = [pltpu.make_async_copy(pieces[i], held.at[i], in_sems.at[i]) for i in range(count)]
+    reads = [
+        pltpu.make_async_copy(pieces[i], held.at[i, :, pl.ds(0, pieces[i].shape[1])], in_sems.at[i])
+        for i in range(count)
+    ]
     for read in reads:
         read.start()
     writes = []
@@ -95,6 +108,8 @@
         reads[i].wait()
         col = 0
         for j, wide in enumerate(widths):
+            if j == len(widths) - 1:
+                col = pieces[i].shape[1] - wide
             write = pltpu.make_async_copy(
                 held.at[i, :, pl.ds(col, wide)],
                 outs[j].at[pl.ds(at, rows), :],
@@ -109,7 +124,7 @@
 
 def placed(pieces, devices, widths, earlier=()):
     tags, arrays = list(pieces), list(pieces.values())
-    rows, whole = arrays[0].shape
+    rows, whole = arrays[0].shape[0], max(a.shape[1] for a in arrays)
     count = len(tags)
     anywhere = pl.BlockSpec(memory_space=pl.ANY)
     return pl.pallas_call(
@@ -130,23 +145,6 @@
 
 def exchange(blocks, axis):
     return lax.all_to_all(blocks, axis, 0, 0, tiled=True)
-
-
-def from_everyone(array, axis):
-    peers = lax.axis_size(axis)
-    return exchange(jnp.broadcast_to(array[None], (peers, *array.shape)), axis)
-
-
-def two_parts(values):
-    high = lax.reduce_precision(values, 8, 7)
-    return high.astype(BF16), (values - high).astype(BF16)
-
-
-def with_scalars(array, scalars):
-    high, low = two_parts(scalars)
-    spare = -(array.shape[-1] + 2) % 128
-    tail = jnp.stack([high, low] + [jnp.zeros_like(high)] * spare, axis=-1)
-    return jnp.concatenate([array, tail], axis=-1)
 
 
 def column(index, values, lanes):
@@ -245,15 +243,184 @@
     return pl.pallas_call(
         combine_kernel,
         out_shape=(jax.ShapeDtypeStruct((1, seqs), F32),) * 2,
+        compiler_params=pltpu.CompilerParams(vmem_limit_bytes=8 * 2**20),
         cost_estimate=pl.CostEstimate(flops=100000, bytes_accessed=40000, transcendentals=0),
     )(stats)
 
 
-def conv_branch(history, newest, taps, offset):
-    total = newest * taps[3] + offset
-    for k in range(3):
-        total = total + history[:, k, :].astype(F32) * taps[k]
-    return jax.nn.silu(total)
+def input_kernel(both, own, other, out):
+    rows = own.shape[0]
+    core = lax.axis_index("core")
+    left, right = both[:, :rows].astype(F32), both[:, rows : 2 * rows].astype(F32)
+    mine = jnp.where(core == 0, left, right).astype(BF16)
+    others = jnp.where(core == 0, right, left).astype(BF16)
+    wide = out.shape[1] // 2 if out.shape[1] % 256 == 0 else out.shape[1]
+    for start in range(0, out.shape[1], wide):
+        part = jnp.dot(mine, own[:, start : start + wide], preferred_element_type=F32)
+        part = part + jnp.dot(others, other[:, start : start + wide], preferred_element_type=F32)
+        out[:, start : start + wide] = part.astype(BF16)
+
+
+def partial_inputs(both, own, other, cols):
+    return pl.pallas_call(
+        input_kernel,
+        out_shape=jax.ShapeDtypeStruct((both.shape[0], cols), BF16),
+        compiler_params=pltpu.CompilerParams(vmem_limit_bytes=12 * 2**20),
+        cost_estimate=pl.CostEstimate(flops=140000000, bytes_accessed=2000000, transcendentals=0),
+    )(both, own, other)
+
+
+def over_heads(values, heads):
+    left = lax.broadcasted_iota(jnp.int32, (values.shape[0], 128), 1) < P_SIZE
+    tiles = [
+        jnp.where(left, values[:, 2 * t : 2 * t + 1], values[:, 2 * t + 1 : 2 * t + 2]) for t in range(heads // 2)
+    ]
+    return jnp.concatenate(tiles, axis=1)
+
+
+def prepared_kernel(x_state, bc_state, taps_x, off_x, taps_bc, off_bc, dt_bias, a_log, skip, in_dt, other, out, turned):
+    seqs, inner = x_state.shape[1:]
+    wide = inner + bc_state.shape[2]
+    for at, history, taps, offset in ((0, x_state, taps_x, off_x), (inner, bc_state, taps_bc, off_bc)):
+        cols = history.shape[2]
+        total = jnp.broadcast_to(offset[...][None, :], (seqs, cols))
+        for k in range(3):
+            total = total + history[k].astype(F32) * taps[k : k + 1, :]
+        out[:seqs, at : at + cols] = total
+        out[seqs : seqs + 1, at : at + cols] = taps[3:4, :]
+    out[:, wide:] = jnp.zeros((out.shape[0], out.shape[1] - wide), F32)
+    heads = dt_bias.shape[0]
+    out[0:1, wide : wide + heads] = dt_bias[...][None, :]
+    out[1:2, wide : wide + heads] = jnp.exp(a_log[...])[None, :]
+    out[2:3, wide : wide + heads] = skip[...][None, :]
+    turned[...] = jnp.zeros(turned.shape, turned.dtype)
+    half = turned.shape[1] // 2
+    rows = in_dt.shape[1]
+    turned[:heads, :rows] = in_dt[...]
+    turned[:, half : half + rows] = other[...].astype(F32).T[:seqs].astype(turned.dtype)
+
+
+def prepared(x_state, bc_state, taps_x, off_x, taps_bc, off_bc, dt_bias, a_log, skip, in_dt, other, dt_at):
+    seqs, _, inner = x_state.shape
+    rows = in_dt.shape[0]
+    whole = pl.BlockSpec(memory_space=pltpu.VMEM)
+    return pl.pallas_call(
+        prepared_kernel,
+        out_shape=(
+            jax.ShapeDtypeStruct((seqs + 8, inner + bc_state.shape[2] + 128), F32),
+            jax.ShapeDtypeStruct((seqs, 512), BF16),
+        ),
+        grid=(1,),
+        in_specs=[whole] * 10 + [pl.BlockSpec((rows, 128), lambda i: (0, dt_at // 128))],
+        out_specs=(whole, whole),
+        cost_estimate=pl.CostEstimate(flops=1000000, bytes_accessed=300000, transcendentals=0),
+    )(
+        x_state.transpose(1, 0, 2), bc_state.transpose(1, 0, 2), taps_x, off_x, taps_bc, off_bc,
+        dt_bias, a_log, skip, in_dt.T, other,
+    )
+
+
+def mixer_kernel(heads, parts, scale, ready, steps, state, out, inflow, decays, b_out, held, turned, sems):
+    seqs = scale.shape[0]
+    inner = heads * P_SIZE
+    size = state.shape[2]
+    copies = [pltpu.make_async_copy(state.at[s], held.at[s], sems.at[s]) for s in range(seqs)]
+    for copy in copies:
+        copy.start()
+    total = parts[0].astype(F32)
+    for k in range(1, parts.shape[0]):
+        total = total + parts[k].astype(F32)
+    total = total * scale[:, :1]
+    wide = inner + 2 * size
+    conv = ready[:seqs, :wide] + total[:, inner : inner + wide] * ready[seqs : seqs + 1, :wide]
+    conv = conv * jax.nn.sigmoid(conv)
+    x_conv, b_vals, c_vals = conv[:, :inner], conv[:, inner : inner + size], conv[:, inner + size :]
+    lane = lax.broadcasted_iota(jnp.int32, (inner, 128), 1)
+    for s in range(seqs):
+        copies[s].wait()
+        sums = jnp.sum(held[s] * c_vals[s : s + 1, :], axis=-1, keepdims=True)
+        if s == 0:
+            turned[...] = jnp.where(lane == s, sums, 0.0)
+        else:
+            turned[...] = jnp.where(lane == s, sums, turned[...])
+    carried = turned[...].T[:seqs]
+    raw = total[:, inner + wide :] + ready[0:1, wide:]
+    step = jnp.maximum(raw, 0.0) + jnp.log1p(jnp.exp(-jnp.abs(raw)))
+    decay = jnp.exp(-step * ready[1:2, wide:])
+    direct = step * jnp.sum(b_vals * c_vals, axis=-1, keepdims=True) + ready[2:3, wide:]
+    gate = total[:, :inner]
+    mixed = over_heads(decay, heads) * carried + over_heads(direct, heads) * x_conv
+    mixed = (mixed * (gate * jax.nn.sigmoid(gate))).astype(out.dtype)
+    for k in range(out.shape[0]):
+        out[k, :, :inner] = mixed
+        out[k, :, inner:] = steps[...]
+    inflow[...] = over_heads(step, heads) * x_conv
+    decays[...] = decay
+    b_out[...] = b_vals
+
+
+def mixer(parts, scale, ready, steps, state):
+    chips, seqs, _ = parts.shape
+    _, heads, p_size, size = state.shape
+    inner = heads * p_size
+    return pl.pallas_call(
+        functools.partial(mixer_kernel, heads),
+        out_shape=(
+            jax.ShapeDtypeStruct((chips, seqs, inner + steps.shape[1]), BF16),
+            jax.ShapeDtypeStruct((seqs, inner), F32),
+            jax.ShapeDtypeStruct((seqs, 128), F32),
+            jax.ShapeDtypeStruct((seqs, size), F32),
+        ),
+        in_specs=[pl.BlockSpec(memory_space=pltpu.VMEM)] * 4 + [pl.BlockSpec(memory_space=pl.ANY)],
+        scratch_shapes=[
+            pltpu.VMEM((seqs, inner, size), F32),
+            pltpu.VMEM((inner, 128), F32),
+            pltpu.SemaphoreType.DMA((seqs,)),
+        ],
+        compiler_params=pltpu.CompilerParams(vmem_limit_bytes=59 * 2**20),
+        cost_estimate=pl.CostEstimate(flops=10000000, bytes_accessed=6000000, transcendentals=0),
+    )(parts, scale, ready, steps, state.reshape(seqs, inner, size))
+
+
+def mix_kernel(gated, gain, out_own, other, out, steps):
+    rows, inner = out_own.shape
+    heads = steps.shape[0]
+    half = (gated.shape[1] - inner) // 2
+    seqs = gated.shape[0] * rows * 2 // steps.shape[1]
+    core = lax.axis_index("core")
+    for k in range(gated.shape[0] // seqs):
+        mine = gated[k * seqs : (k + 1) * seqs, inner : inner + rows].astype(F32)
+        others = gated[k * seqs : (k + 1) * seqs, inner + half : inner + half + rows].astype(F32)
+        left, right = jnp.where(core == 0, mine, others), jnp.where(core == 0, others, mine)
+        steps[:, 2 * k * rows : (2 * k + 1) * rows] = left[:heads].astype(BF16)
+        steps[:, (2 * k + 1) * rows : (2 * k + 2) * rows] = right[:heads].astype(BF16)
+    values = gated[:, :inner].astype(F32)
+    squares = jnp.sum(values * values, axis=-1, keepdims=True)
+    gained = (values * gain[...][None, :]).astype(BF16)
+    across = (((1,), (1,)), ((), ()))
+    out[0, :, :rows] = lax.dot_general(gained, out_own[...], across, preferred_element_type=F32).astype(BF16)
+    out[0, :, rows : 2 * rows] = lax.dot_general(
+        gained, other[...], across, preferred_element_type=F32
+    ).astype(BF16)
+    spare = out.shape[2] - 2 * rows
+    high = squares.astype(BF16).astype(F32)
+    out[0, :, 2 * rows :] = (column(0, high, spare) + column(1, squares - high, spare)).astype(BF16)
+    whole = out[0]
+    for k in range(1, out.shape[0]):
+        out[k] = whole
+
+
+def partial_mix(gated, gain, out_own, other, peers, heads, width):
+    rows, _ = out_own.shape
+    return pl.pallas_call(
+        mix_kernel,
+        out_shape=(
+            jax.ShapeDtypeStruct((peers, gated.shape[0], 2 * rows + 64), BF16),
+            jax.ShapeDtypeStruct((heads, width), BF16),
+        ),
+        compiler_params=pltpu.CompilerParams(vmem_limit_bytes=12 * 2**20),
+        cost_estimate=pl.CostEstimate(flops=60000000, bytes_accessed=2000000, transcendentals=0),
+    )(gated, gain, out_own, other)
 
 
 def shards(
@@ -281,7 +448,6 @@
     final_gain,
 ):
     chips = lax.axis_size(CHIPS)
-    first_core = lax.axis_index("core") == 0
     seqs, width = hidden_in.shape
     rows, inner = in_z.shape
     heads = a_log.shape[0]
@@ -289,10 +455,10 @@
     class_seqs = chips * seqs
 
     hidden_sent, scale = hidden_blocks(hidden_in, norm_in, chips)
-    own = joined(in_z, in_x, in_bc, in_dt, out_t)
-    in_cols = own.shape[1] - inner
+    full, own = joined(in_z, in_x, in_bc, in_dt, out_t)
+    in_cols = full.shape[1] - inner
     dt_at = 2 * inner + 2 * state_size
-    other = from_partner(own)
+    other = from_partner(full)
     ahead = along_ring(own, 1)
     behind = along_ring(own, -1)
     over = from_opposite(own)
@@ -312,56 +478,39 @@
         ((2, 1), far_z),
     ):
         pieces.update({(*at, 0): piece, (*at, 1): from_partner(piece)})
-    widths = (inner, inner, 2 * state_size, 128, inner)
+    widths = (inner, inner, 2 * state_size, inner)
     first, second = list(pieces)[:8], list(pieces)[8:]
     devices = 2 * chips
     rolled = placed({tag: pieces[tag] for tag in first}, devices, widths)
     rolled = placed({tag: pieces[tag] for tag in second}, devices, widths, rolled)
-    roll_z, roll_x, roll_bc, dt_wide, roll_out = rolled
-    roll_dt = dt_wide[:, :heads]
-
-    def own_first(array):
-        left, right = array[:, :rows], array[:, rows:]
-        return jnp.where(first_core, left, right), jnp.where(first_core, right, left)
+    roll_z, roll_x, roll_bc, roll_out = rolled
 
     both = exchange(hidden_sent, CHIPS)
     both = both.reshape(class_seqs, -1)
-    normed_own, normed_other = own_first(both[:, : 2 * rows])
-
-    partial_in = jnp.dot(normed_own, own[:, :in_cols], preferred_element_type=F32) + jnp.dot(
-        normed_other, other[:, :in_cols], preferred_element_type=F32
-    )
-    partial_in = partial_in.astype(BF16).reshape(chips, seqs, in_cols)
+
+    partial_in = partial_inputs(both, full, other, in_cols).reshape(chips, seqs, in_cols)
     partial_in = exchange(partial_in, CHIPS)
-    branches = jnp.sum(partial_in.astype(F32), axis=0) * scale[:, :1]
-    gate = branches[:, :inner]
-    x_conv = conv_branch(conv_x_state, branches[:, inner : 2 * inner], conv_wx, conv_bx)
-    bc_conv = conv_branch(conv_bc_state, branches[:, 2 * inner : dt_at], conv_wbc, conv_bbc)
-    b_vals, c_vals = bc_conv[:, :state_size], bc_conv[:, state_size:]
-    step = jax.nn.softplus(branches[:, dt_at : dt_at + heads] + dt_bias)
-    decay = jnp.exp(-step * jnp.exp(a_log))
-    x_heads = x_conv.reshape(seqs, heads, P_SIZE)
-    inflow = (step[:, :, None] * x_heads)[:, :, :, None] * b_vals[:, None, None, :]
-    new_state = decay[:, :, None, None] * ssm_state + inflow
-    carried = jnp.einsum("shpn,sn->shp", ssm_state, c_vals)
-    overlap = jnp.sum(b_vals * c_vals, axis=-1)
-    direct = step * overlap[:, None] + skip_gain
-    ssm_out = (decay[:, :, None] * carried + direct[:, :, None] * x_heads).reshape(seqs, inner)
-    gated = (ssm_out * jax.nn.silu(gate)).astype(BF16)
-
-    gated = from_everyone(gated, CHIPS)
-    gated = gated.reshape(class_seqs, inner).astype(F32)
-    squares = jnp.sum(gated * gated, axis=-1)
-    gained = (gated * norm_gain).astype(BF16)
-    across = (((1,), (1,)), ((), ()))
-    mix_own = lax.dot_general(gained, out_t, across, preferred_element_type=F32)
-    mix_other = lax.dot_general(gained, other[:, in_cols:], across, preferred_element_type=F32)
-    mix = jnp.concatenate([mix_own.astype(BF16), mix_other.astype(BF16)], axis=-1)
-    mix = with_scalars(mix, squares)
-    mix = from_everyone(mix, "head")
+    ready, steps = prepared(
+        conv_x_state, conv_bc_state, conv_wx, conv_bx, conv_wbc, conv_bbc, dt_bias, a_log, skip_gain,
+        in_dt, other, dt_at,
+    )
+    gated, inflow, decay, b_vals = mixer(partial_in, scale, ready, steps, ssm_state)
+    new_state = (
+        decay[:, :heads, None, None] * ssm_state
+        + inflow.reshape(seqs, heads, P_SIZE)[:, :, :, None] * b_vals[:, None, None, :]
+    )
+
+    gains = final_gain.reshape(-1, rows)
+
+    gated = exchange(gated, CHIPS)
+    mix, roll_dt = partial_mix(
+        gated.reshape(class_seqs, -1), norm_gain, out_t, other[:, in_cols:], lax.axis_size("head"), heads, width
+    )
+    roll_dt = roll_dt.T
+    mix = exchange(mix, "head")
 
     sent = partial_logits(
-        mix, both, final_gain.reshape(-1, rows), lm_head.T, lm_other.T, inner * lax.axis_size("head")
+        mix, both, gains, lm_head.T, lm_other.T, inner * lax.axis_size("head")
     )
     parts = exchange(sent.reshape(chips, seqs, -1), CHIPS)
     stats = head_stats(parts, ref_logits, token_ids[:, None], width, lax.axis_size("head"))

time: 142 us -> 137 us (0.965)
  blocking collectives: 0 us -> 16.6 us
  waiting for transfers between devices: 52.7 us -> 41.9 us
  Pallas kernels: 19.9 us -> 28.4 us
  matrix products: 7.53 us -> 0 us
  starting transfers between devices: 43.7 us -> 38.3 us
  local copies, waits for them, and re-layouts: 8.42 us -> 3.22 us
    all_to_all x0 -> x1, blocking collectives: none -> 16.6 us  [exchange(): return lax.all_to_all(blocks, axis, 0, 0, tiled=True)]
    pallas_call x1 -> x5, Pallas kernels: 2.12 us -> 12.4 us  [the longest x1 5.73 us: mixer(): pl.pallas_call(functools.partial(mixer_kernel, heads), out_shape=(jax.Sha...]
    all_to_all x6 -> x5, waiting for transfers between devices: 23.6 us -> 14.6 us  [exchange(): return lax.all_to_all(blocks, axis, 0, 0, tiled=True)]
    dot_general x5 -> x0, matrix products: 7.53 us -> none  [the longest x1 4.61 us: shards(): carried = jnp.einsum('shpn,sn->shp', ssm_state, c_vals)]
    all_to_all x6 -> x5, starting transfers between devices: 34.2 us -> 29.6 us  [exchange(): return lax.all_to_all(blocks, axis, 0, 0, tiled=True)]
    ppermute x6, waiting for transfers between devices: 29.1 us -> 27.3 us  [along_ring(): return lax.ppermute(array, ('x', 'core'), pairs)]
    unnamed x36 -> x26, local copies, waits for them, and re-layouts: 3.98 us -> 2.18 us
    broadcast_in_dim x2 -> x0, local copies, waits for them, and re-layouts: 1.64 us -> none  [from_everyone(): return exchange(jnp.broadcast_to(array[None], (peers, *array.shape)), axis)]
  transfers between devices with their start and end apart: 22 -> 21, of which waited for: 9 -> 8; matrix products, arithmetic and copies ran while one was open for 14% -> 5% of each run, Pallas kernels for 9% -> 19%
where the time goes in v3:
time: 137 us; the launch traced here: 135 us
  waiting for transfers between devices  41.9 us (31%)
  starting transfers between devices  38.3 us (28%)
  Pallas kernels  28.4 us (21%)
  blocking collectives  16.6 us (12%)
  other arithmetic  6.08 us (4%)
  local copies, waits for them, and re-layouts  3.22 us (2%)
    all_to_all x5, starting transfers between devices, exchange(): return lax.all_to_all(blocks, axis, 0, 0, tiled=True)  29.6 us
    ppermute x6, waiting for transfers between devices, along_ring(): return lax.ppermute(array, ('x', 'core'), pairs)  27.3 us
    all_to_all x1, blocking collectives, exchange(): return lax.all_to_all(blocks, axis, 0, 0, tiled=True)  16.6 us
    all_to_all x5, waiting for transfers between devices, exchange(): return lax.all_to_all(blocks, axis, 0, 0, tiled=True)  14.6 us
    pallas_call x2, Pallas kernels, placed(): pl.pallas_call(functools.partial(placed_kernel, tags, widths), out_shape=...  9.61 us
    add x1, other arithmetic, shards(): decay[:, :heads, None, None] * ssm_state  6.08 us
    ppermute x6, starting transfers between devices, along_ring(): return lax.ppermute(array, ('x', 'core'), pairs)  5.97 us
    pallas_call x1, Pallas kernels, mixer(): pl.pallas_call(functools.partial(mixer_kernel, heads), out_shape=(jax.Sha...  5.73 us
  transfers between devices with their start and end apart: 21, of which 8 were waited for; matrix products, arithmetic and copies ran while one was open for 5% of the time, Pallas kernels for 19%

profile of v3, /device:TPU:0, one launch (start us, length us, event | category | flops | bytes accessed | tf_op | source)
XLA Modules:
  0.0 135.3 jit_solution(6319533606549570487)
XLA Ops:
  0.6 2.4 %shard_map.270 = (bf16[160,2304]{1,0:T(8,128)(2,1)}, bf16[160,2176]{1,0:T(8,128)(2,1)}) custom-call(bf16[160,640]{1,0:T(8,128)(2,1)} %in_z.1, bf16[160,640]{1,0:T(8,128)(2,1)} %in_x.1, bf16[160,256]{1,0:T(8,128)(2,1)} %in_bc.1, bf16[10,160]{1,0:T(8,128)(2,1)} %bitcast.21, bf16[160,640]{1,0:T(8,128)(2,1)} %out_own.1), custom_call_target="tpu_custom_call" | custom-call | flops 2000000 | bytes 1392640 | tf_op jit(solution)/shard_map/pallas_call | solution.py:57
  3.0 2.0 %collective-permute-start.2 = (bf16[160,2176]{1,0:T(8,128)(2,1)}, bf16[160,2176]{1,0:T(8,128)(2,1)}, u32[]{:S(2)}, u32[]{:S(2)}) collective-permute-start(bf16[160,2176]{1,0:T(8,128)(2,1)} %get-tuple-element.42.refs_0_), channel_id=1, source_target_pairs={{0,16},{16,0},{1,17},{17,1},{2,18},{18,2},{3,19},{19,3},{4,20},{20... | collective-permute-start | bytes 2088968 | tf_op jit(solution)/shard_map/ppermute | solution.py:24
  5.1 1.7 %shard_map.269 = (bf16[8,16,640]{2,1,0:T(8,128)(2,1)}, f32[16,128]{1,0:T(8,128)}) custom-call(bf16[16,2560]{1,0:T(8,128)(2,1)} %hidden.1, f32[2560]{0:T(1024)} %gain.2), custom_call_target="tpu_custom_call" | custom-call | flops 1000000 | bytes 300000 | tf_op jit(solution)/shard_map/pallas_call | solution.py:80
  6.7 16.6 %all_to_all.30 = bf16[8,16,640]{2,1,0:T(8,128)(2,1)S(1)} all-to-all(bf16[8,16,640]{2,1,0:T(8,128)(2,1)} %get-tuple-element.30), channel_id=1, replica_groups=mesh['x'=4,'z'=2,'core'=2,'head'=8] {'x','z'}, dimensions={0} | all-to-all | bytes 327680 | tf_op jit(solution)/shard_map/all_to_all | solution.py:147
  23.3 1.4 %copy-done.4 = bf16[160,2304]{1,0:T(8,128)(2,1)S(1)} copy-done((bf16[160,2304]{1,0:T(8,128)(2,1)S(1)}, bf16[160,2304]{1,0:T(8,128)(2,1)}, u32[]{:S(2)}) %copy-start.4) | copy-done | bytes 737304
  24.7 1.3 shard_map.271
  26.0 5.6 %all-to-all-start.1 = ((bf16[8,16,1664]{2,1,0:T(8,128)(2,1)}), bf16[8,16,1664]{2,1,0:T(8,128)(2,1)S(1)}, u32[]{:S(2)}, u32[]{:S(2)}) async-start(bf16[8,16,1664]{2,1,0:T(8,128)(2,1)} %bitcast.2), calls=%async_computation.1 | async-start | bytes 851968 | tf_op jit(solution)/shard_map/all_to_all | solution.py:147
  31.6 0.0 collective-permute-start.1
  31.6 1.6 %shard_map.272 = (f32[24,1024]{1,0:T(8,128)}, bf16[16,512]{1,0:T(8,128)(2,1)}) custom-call(bf16[3,16,640]{2,1,0:T(8,128)(2,1)} %bitcast.20, bf16[3,16,256]{2,1,0:T(8,128)(2,1)} %bitcast.23, f32[4,640]{1,0:T(4,128)} %taps_x.1, f32[640]{0:T(1024)} %off_x.1, f32[4,256]{1,0:T(4,128)} %taps_bc.1, f32[256]{0:T(256)} %off_bc.1, f32[10]{0:T(128)} %dt_bias.1, ...), custom_call_target="tpu_custom_call" | custom-call | flops 1000000 | bytes 300000 | tf_op jit(solution)/shard_map/pallas_call | solution.py:307
  33.2 6.7 %all-to-all-done.1.parts = bf16[8,16,1664]{2,1,0:T(8,128)(2,1)S(1)} async-done(((bf16[8,16,1664]{2,1,0:T(8,128)(2,1)}), bf16[8,16,1664]{2,1,0:T(8,128)(2,1)S(1)}, u32[]{:S(2)}, u32[]{:S(2)}) %all-to-all-start.1) | async-done | bytes 426016 | tf_op jit(solution)/shard_map/all_to_all | solution.py:147
  40.0 0.8 copy-done.8
  40.7 5.7 %shard_map.273 = (bf16[8,16,1152]{2,1,0:T(8,128)(2,1)}, f32[16,640]{1,0:T(8,128)}, f32[16,128]{1,0:T(8,128)}, f32[16,128]{1,0:T(8,128)}) custom-call(bf16[8,16,1664]{2,1,0:T(8,128)(2,1)} %copy-done.8, f32[16,128]{1,0:T(8,128)} %get-tuple-element.32.scale, f32[24,1024]{1,0:T(8,128)} %get-tuple-element.33.ready, bf16[16,512]{1,0:T(8,128)(2,1)} %get-tuple-element.34.steps, ...), custom_call_target="tpu_custom_call" | custom-call | flops 10000000 | bytes 6000000 | tf_op jit(solution)/shard_map/pallas_call | solution.py:366
  46.5 0.0 copy-start.6
  46.5 3.6 %all-to-all-start.2 = ((bf16[8,16,1152]{2,1,0:T(8,128)(2,1)}), bf16[8,16,1152]{2,1,0:T(8,128)(2,1)S(1)}, u32[]{:S(2)}, u32[]{:S(2)}) async-start(bf16[8,16,1152]{2,1,0:T(8,128)(2,1)} %get-tuple-element.38), calls=%async_computation.2 | async-start | bytes 589824 | tf_op jit(solution)/shard_map/all_to_all | solution.py:147
  50.1 1.9 %collective-permute-start.7 = (bf16[160,2176]{1,0:T(8,128)(2,1)S(1)}, bf16[160,2176]{1,0:T(8,128)(2,1)}, u32[]{:S(2)}, u32[]{:S(2)}) collective-permute-start(bf16[160,2176]{1,0:T(8,128)(2,1)S(1)} %copy-done.5), channel_id=1, source_target_pairs={{0,32},{8,104},{32,64},{40,8},{64,96},{72,40},{96,0},{104,72},{1,3... | collective-permute-start | bytes 2088968 | tf_op jit(solution)/shard_map/ppermute | solution.py:34
  52.0 1.4 %collective-permute-start.14 = (bf16[160,2176]{1,0:T(8,128)(2,1)S(1)}, bf16[160,2176]{1,0:T(8,128)(2,1)}, u32[]{:S(2)}, u32[]{:S(2)}) collective-permute-start(bf16[160,2176]{1,0:T(8,128)(2,1)S(1)} %copy-done.5), channel_id=1, source_target_pairs={{0,96},{8,40},{32,0},{40,72},{64,32},{72,104},{96,64},{104,8},{1,9... | collective-permute-start | bytes 2088968 | tf_op jit(solution)/shard_map/ppermute | solution.py:34
  53.4 0.6 collective-permute-start.3
  54.0 4.4 %all-to-all-done.2 = bf16[8,16,1152]{2,1,0:T(8,128)(2,1)S(1)} async-done(((bf16[8,16,1152]{2,1,0:T(8,128)(2,1)}), bf16[8,16,1152]{2,1,0:T(8,128)(2,1)S(1)}, u32[]{:S(2)}, u32[]{:S(2)}) %all-to-all-start.2) | async-done | bytes 294944 | tf_op jit(solution)/shard_map/all_to_all | solution.py:147
  58.4 1.4 shard_map.274
  59.8 7.5 %all-to-all-start.3 = ((bf16[8,128,384]{2,1,0:T(8,128)(2,1)}), bf16[8,128,384]{2,1,0:T(8,128)(2,1)S(1)}, u32[]{:S(2)}, u32[]{:S(2)}) async-start(bf16[8,128,384]{2,1,0:T(8,128)(2,1)} %get-tuple-element.39), calls=%async_computation.3 | async-start | bytes 1572864 | tf_op jit(solution)/shard_map/all_to_all | solution.py:147
  67.3 0.0 collective-permute-start.12
  67.3 4.3 %collective-permute-done.7.refs_4_ = bf16[160,2176]{1,0:T(8,128)(2,1)} collective-permute-done((bf16[160,2176]{1,0:T(8,128)(2,1)S(1)}, bf16[160,2176]{1,0:T(8,128)(2,1)}, u32[]{:S(2)}, u32[]{:S(2)}) %collective-permute-start.7) | collective-permute-done | bytes 696352 | tf_op jit(solution)/shard_map/ppermute | solution.py:34
  71.6 0.0 collective-permute-start.13
  71.6 0.3 collective-permute-done.14.refs_6_
  71.9 2.0 %collective-permute-start.5 = (bf16[160,2176]{1,0:T(8,128)(2,1)}, bf16[160,2176]{1,0:T(8,128)(2,1)}, u32[]{:S(2)}, u32[]{:S(2)}) collective-permute-start(bf16[160,2176]{1,0:T(8,128)(2,1)} %collective-permute-done.2.refs_2_), channel_id=1, source_target_pairs={{0,96},{8,40},{32,0},{40,72},{64,32},{72,104},{96,64},{104,8},{1,9... | collective-permute-start | bytes 2088968 | tf_op jit(solution)/shard_map/ppermute | solution.py:34
  73.9 0.0 collective-permute-done.1
  73.9 0.1 collective-permute-start.8
  73.9 7.9 %collective-permute-done.3.refs_0_ = bf16[160,2176]{1,0:T(8,128)(2,1)} collective-permute-done((bf16[160,2176]{1,0:T(8,128)(2,1)}, bf16[160,2176]{1,0:T(8,128)(2,1)}, u32[]{:S(2)}, u32[]{:S(2)}) %collective-permute-start.3) | collective-permute-done | bytes 696352 | tf_op jit(solution)/shard_map/ppermute | solution.py:34
  81.9 0.0 collective-permute-start.10
  81.9 0.1 reshape.41.gains
  82.0 3.1 %shard_map.275 = bf16[128,3328]{1,0:T(8,128)(2,1)} custom-call(bf16[8,128,384]{2,1,0:T(8,128)(2,1)S(1)} %all-to-all-done.3.mixed, bf16[128,640]{1,0:T(8,128)(2,1)S(1)} %bitcast.16, f32[16,160]{1,0:T(8,128)S(1)} %reshape.41.gains, bf16[160,3200]{1,0:T(8,128)(2,1)S(1)} %bitcast.18, bf16[160,3200]{1,0:T(8,128)(2,1)} %bitcast.8.lm_other), custom_call_target="tpu_custom_call" | custom-call | flops 300000000 | bytes 4000000 | tf_op jit(solution)/shard_map/pallas_call | solution.py:184
  85.1 5.4 %all-to-all-start.4 = ((bf16[8,16,3328]{2,1,0:T(8,128)(2,1)}), bf16[8,16,3328]{2,1,0:T(8,128)(2,1)S(1)}, u32[]{:S(2)}, u32[]{:S(2)}) async-start(bf16[8,16,3328]{2,1,0:T(8,128)(2,1)} %bitcast.9), calls=%async_computation.4 | async-start | bytes 1703936 | tf_op jit(solution)/shard_map/all_to_all | solution.py:147
  90.5 0.0 collective-permute-done.12.refs_3_
  90.5 0.1 collective-permute-start.15
  90.6 0.0 collective-permute-done.13.refs_5_
  90.6 0.5 collective-permute-start.4
  91.1 0.2 collective-permute-start.6
  91.2 4.5 %collective-permute-done.8.refs_4_ = bf16[160,2176]{1,0:T(8,128)(2,1)} collective-permute-done((bf16[160,2176]{1,0:T(8,128)(2,1)}, bf16[160,2176]{1,0:T(8,128)(2,1)}, u32[]{:S(2)}, u32[]{:S(2)}) %collective-permute-start.8) | collective-permute-done | bytes 696352 | tf_op jit(solution)/shard_map/ppermute | solution.py:34
  95.7 10.2 %collective-permute-done.10.refs_6_ = bf16[160,2176]{1,0:T(8,128)(2,1)} collective-permute-done((bf16[160,2176]{1,0:T(8,128)(2,1)}, bf16[160,2176]{1,0:T(8,128)(2,1)}, u32[]{:S(2)}, u32[]{:S(2)}) %collective-permute-start.10) | collective-permute-done | bytes 696352 | tf_op jit(solution)/shard_map/ppermute | solution.py:34
  106.0 0.1 copy.35.tokens
  106.1 0.9 mul.25
  106.9 3.5 %all-to-all-done.4.parts = bf16[8,16,3328]{2,1,0:T(8,128)(2,1)S(1)} async-done(((bf16[8,16,3328]{2,1,0:T(8,128)(2,1)}), bf16[8,16,3328]{2,1,0:T(8,128)(2,1)S(1)}, u32[]{:S(2)}, u32[]{:S(2)}) %all-to-all-start.4) | async-done | bytes 852000 | tf_op jit(solution)/shard_map/all_to_all | solution.py:147
  110.5 1.1 shard_map.276
  111.5 7.5 %all-to-all-start.5 = ((f32[8,8,128]{2,1,0:T(8,128)}), f32[8,8,128]{2,1,0:T(8,128)S(1)}, u32[]{:S(2)}, u32[]{:S(2)}) async-start(f32[8,8,128]{2,1,0:T(8,128)} %shard_map.276), calls=%async_computation.5 | async-start | bytes 65536 | tf_op jit(solution)/shard_map/all_to_all | solution.py:147
  119.0 6.1 %multiply_add_fusion = f32[16,10,64,128]{3,2,1,0:T(8,128)} fusion(f32[16,10,64,128]{3,2,1,0:T(8,128)} %param.23, f32[16,128]{1,0:T(8,128)S(1)} %copy-done.11, f32[16,10,64]{2,1,0:T(8,128)S(1)} %mul.25, f32[16,10]{1,0:T(8,128)S(1)} %bitcast.24), kind=kLoop, calls=%fused_computation | loop fusion | flops 3932160 | bytes 10535552 | tf_op jit(solution)/shard_map/add | solution.py:499
  125.1 4.5 %shard_map.278 = (bf16[2560,640]{1,0:T(8,128)(2,1)}, bf16[2560,640]{1,0:T(8,128)(2,1)}, bf16[2560,256]{1,0:T(8,128)(2,1)}, bf16[2560,640]{1,0:T(8,128)(2,1)}) custom-call(bf16[160,2176]{1,0:T(8,128)(2,1)S(1)} %copy-done.5, bf16[160,2304]{1,0:T(8,128)(2,1)S(1)} %copy-done.1, bf16[160,2176]{1,0:T(8,128)(2,1)} %collective-permute-done.2.refs_2_, ...), custom_call_target="tpu_custom_call" | custom-call | flops 10000000 | bytes 11796480 | tf_op jit(solution)/shard_map/pallas_call | solution.py:130
  129.6 5.1 %shard_map.279 = (bf16[2560,640]{1,0:T(8,128)(2,1)}, bf16[2560,640]{1,0:T(8,128)(2,1)}, bf16[2560,256]{1,0:T(8,128)(2,1)}, bf16[2560,640]{1,0:T(8,128)(2,1)}) custom-call(bf16[160,2176]{1,0:T(8,128)(2,1)} %collective-permute-done.3.refs_0_, ...), custom_call_target="tpu_custom_call", output_to_operand_aliasing={{0}: (8, {}), {1}: (9, {}), {2}: (10, {}), {3}: (11, {})} | custom-call | flops 10000000 | bytes 11141120 | tf_op jit(solution)/shard_map/pallas_call | solution.py:130
  134.8 0.6 shard_map.277
  (37 shorter events, 0.1 us)
Async XLA Ops:
  3.0 20.3 %collective-permute-start = (bf16[160,2304]{1,0:T(8,128)(2,1)}, bf16[160,2304]{1,0:T(8,128)(2,1)S(1)}, u32[]{:S(2)}, u32[]{:S(2)}) collective-permute-start(bf16[160,2304]{1,0:T(8,128)(2,1)} %get-tuple-element.31.own), channel_id=1, source_target_pairs={{0,8},{8,0},{1,9},{9,1},{2,10},{10,2},{3,11},{11,3},{4,12},{12,4},... | collective-permute-start | bytes 2211848 | tf_op jit(solution)/shard_map/ppermute | solution.py:20
  3.0 50.4 %collective-permute-start.2 = (bf16[160,2176]{1,0:T(8,128)(2,1)}, bf16[160,2176]{1,0:T(8,128)(2,1)}, u32[]{:S(2)}, u32[]{:S(2)}) collective-permute-start(bf16[160,2176]{1,0:T(8,128)(2,1)} %get-tuple-element.42.refs_0_), channel_id=1, source_target_pairs={{0,16},{16,0},{1,17},{17,1},{2,18},{18,2},{3,19},{19,3},{4,20},{20... | collective-permute-start | bytes 2088968 | tf_op jit(solution)/shard_map/ppermute | solution.py:24
  23.3 8.3 %copy-start = (bf16[160,2304]{1,0:T(8,128)(2,1)}, bf16[160,2304]{1,0:T(8,128)(2,1)S(1)}, u32[]{:S(2)}) copy-start(bf16[160,2304]{1,0:T(8,128)(2,1)S(1)} %collective-permute-done.other.refs_1_) | copy-start | bytes 2211844
  23.3 1.4 %copy-start.4 = (bf16[160,2304]{1,0:T(8,128)(2,1)S(1)}, bf16[160,2304]{1,0:T(8,128)(2,1)}, u32[]{:S(2)}) copy-start(bf16[160,2304]{1,0:T(8,128)(2,1)} %get-tuple-element.31.own) | copy-start | bytes 2211844
  24.7 25.4 %copy-start.5 = (bf16[160,2176]{1,0:T(8,128)(2,1)S(1)}, bf16[160,2176]{1,0:T(8,128)(2,1)}, u32[]{:S(2)}) copy-start(bf16[160,2176]{1,0:T(8,128)(2,1)} %get-tuple-element.42.refs_0_) | copy-start | bytes 2088964
  24.7 33.7 %copy-start.3 = (bf16[160,640]{1,0:T(8,128)(2,1)S(1)}, bf16[160,640]{1,0:T(8,128)(2,1)}, u32[]{:S(2)}) copy-start(bf16[160,640]{1,0:T(8,128)(2,1)} %out_own.1) | copy-start | bytes 614404
  24.7 33.7 %copy-start.7 = (f32[640]{0:T(1024)S(1)}, f32[640]{0:T(1024)}, u32[]{:S(2)}) copy-start(f32[640]{0:T(1024)} %gain.3) | copy-start | bytes 7684
  26.0 55.9 %copy-start.9 = (f32[2560]{0:T(1024)S(1)}, f32[2560]{0:T(1024)}, u32[]{:S(2)}) copy-start(f32[2560]{0:T(1024)} %param.43) | copy-start | bytes 30724
  26.0 56.0 %copy-start.2 = (bf16[3200,160]{0,1:T(8,128)(2,1)S(1)}, bf16[3200,160]{0,1:T(8,128)(2,1)}, u32[]{:S(2)}) copy-start(bf16[3200,160]{0,1:T(8,128)(2,1)} %param.33) | copy-start | bytes 3072004
  26.0 14.0 %all-to-all-start.1 = ((bf16[8,16,1664]{2,1,0:T(8,128)(2,1)}), bf16[8,16,1664]{2,1,0:T(8,128)(2,1)S(1)}, u32[]{:S(2)}, u32[]{:S(2)}) async-start(bf16[8,16,1664]{2,1,0:T(8,128)(2,1)} %bitcast.2), calls=%async_computation.1 | async-start | bytes 851968 | tf_op jit(solution)/shard_map/all_to_all | solution.py:147
  31.6 42.3 %collective-permute-start.1 = (bf16[3200,160]{0,1:T(8,128)(2,1)}, bf16[3200,160]{0,1:T(8,128)(2,1)}, u32[]{:S(2)}, u32[]{:S(2)}) collective-permute-start(bf16[3200,160]{0,1:T(8,128)(2,1)} %param.33), channel_id=1, source_target_pairs={{0,8},{8,0},{1,9},{9,1},{2,10},{10,2},{3,11},{11,3},{4,12},{12,4},... | collective-permute-start | bytes 3072008 | tf_op jit(solution)/shard_map/ppermute | solution.py:20
  33.2 20.8 %copy-start.1 = (bf16[160,2304]{1,0:T(8,128)(2,1)S(1)}, bf16[160,2304]{1,0:T(8,128)(2,1)}, u32[]{:S(2)}) copy-start(bf16[160,2304]{1,0:T(8,128)(2,1)} %copy-done) | copy-start | bytes 2211844
  40.0 0.8 copy-start.8
  46.5 64.0 %copy-start.6 = (bf16[16,3200]{1,0:T(8,128)(2,1)S(1)}, bf16[16,3200]{1,0:T(8,128)(2,1)}, u32[]{:S(2)}) copy-start(bf16[16,3200]{1,0:T(8,128)(2,1)} %reference.1) | copy-start | bytes 307204
  46.5 72.5 %copy-start.10 = (f32[16,128]{1,0:T(8,128)S(1)}, f32[16,128]{1,0:T(8,128)}, u32[]{:S(2)}) copy-start(f32[16,128]{1,0:T(8,128)} %get-tuple-element.35) | copy-start | bytes 24580
  46.5 72.5 %copy-start.11 = (f32[16,128]{1,0:T(8,128)S(1)}, f32[16,128]{1,0:T(8,128)}, u32[]{:S(2)}) copy-start(f32[16,128]{1,0:T(8,128)} %get-tuple-element.37) | copy-start | bytes 24580
  46.5 11.9 %all-to-all-start.2 = ((bf16[8,16,1152]{2,1,0:T(8,128)(2,1)}), bf16[8,16,1152]{2,1,0:T(8,128)(2,1)S(1)}, u32[]{:S(2)}, u32[]{:S(2)}) async-start(bf16[8,16,1152]{2,1,0:T(8,128)(2,1)} %get-tuple-element.38), calls=%async_computation.2 | async-start | bytes 589824 | tf_op jit(solution)/shard_map/all_to_all | solution.py:147
  50.1 21.5 %collective-permute-start.7 = (bf16[160,2176]{1,0:T(8,128)(2,1)S(1)}, bf16[160,2176]{1,0:T(8,128)(2,1)}, u32[]{:S(2)}, u32[]{:S(2)}) collective-permute-start(bf16[160,2176]{1,0:T(8,128)(2,1)S(1)} %copy-done.5), channel_id=1, source_target_pairs={{0,32},{8,104},{32,64},{40,8},{64,96},{72,40},{96,0},{104,72},{1,3... | collective-permute-start | bytes 2088968 | tf_op jit(solution)/shard_map/ppermute | solution.py:34
  52.0 19.9 %collective-permute-start.14 = (bf16[160,2176]{1,0:T(8,128)(2,1)S(1)}, bf16[160,2176]{1,0:T(8,128)(2,1)}, u32[]{:S(2)}, u32[]{:S(2)}) collective-permute-start(bf16[160,2176]{1,0:T(8,128)(2,1)S(1)} %copy-done.5), channel_id=1, source_target_pairs={{0,96},{8,40},{32,0},{40,72},{64,32},{72,104},{96,64},{104,8},{1,9... | collective-permute-start | bytes 2088968 | tf_op jit(solution)/shard_map/ppermute | solution.py:34
  53.4 28.5 %collective-permute-start.3 = (bf16[160,2176]{1,0:T(8,128)(2,1)}, bf16[160,2176]{1,0:T(8,128)(2,1)}, u32[]{:S(2)}, u32[]{:S(2)}) collective-permute-start(bf16[160,2176]{1,0:T(8,128)(2,1)} %collective-permute-done.2.refs_2_), channel_id=1, source_target_pairs={{0,32},{8,104},{32,64},{40,8},{64,96},{72,40},{96,0},{104,72},{1,3... | collective-permute-start | bytes 2088968 | tf_op jit(solution)/shard_map/ppermute | solution.py:34
  59.8 22.2 %all-to-all-start.3 = ((bf16[8,128,384]{2,1,0:T(8,128)(2,1)}), bf16[8,128,384]{2,1,0:T(8,128)(2,1)S(1)}, u32[]{:S(2)}, u32[]{:S(2)}) async-start(bf16[8,128,384]{2,1,0:T(8,128)(2,1)} %get-tuple-element.39), calls=%async_computation.3 | async-start | bytes 1572864 | tf_op jit(solution)/shard_map/all_to_all | solution.py:147
  67.3 23.2 %collective-permute-start.12 = (bf16[160,2176]{1,0:T(8,128)(2,1)}, bf16[160,2176]{1,0:T(8,128)(2,1)}, u32[]{:S(2)}, u32[]{:S(2)}) collective-permute-start(bf16[160,2176]{1,0:T(8,128)(2,1)} %collective-permute-done.2.refs_2_), channel_id=1, source_target_pairs={{0,8},{8,0},{1,9},{9,1},{2,10},{10,2},{3,11},{11,3},{4,12},{12,4},... | collective-permute-start | bytes 2088968 | tf_op jit(solution)/shard_map/ppermute | solution.py:20
  71.6 19.0 %collective-permute-start.13 = (bf16[160,2176]{1,0:T(8,128)(2,1)}, bf16[160,2176]{1,0:T(8,128)(2,1)}, u32[]{:S(2)}, u32[]{:S(2)}) collective-permute-start(bf16[160,2176]{1,0:T(8,128)(2,1)} %collective-permute-done.7.refs_4_), channel_id=1, source_target_pairs={{0,8},{8,0},{1,9},{9,1},{2,10},{10,2},{3,11},{11,3},{4,12},{12,4},... | collective-permute-start | bytes 2088968 | tf_op jit(solution)/shard_map/ppermute | solution.py:20
  71.9 19.2 %collective-permute-start.5 = (bf16[160,2176]{1,0:T(8,128)(2,1)}, bf16[160,2176]{1,0:T(8,128)(2,1)}, u32[]{:S(2)}, u32[]{:S(2)}) collective-permute-start(bf16[160,2176]{1,0:T(8,128)(2,1)} %collective-permute-done.2.refs_2_), channel_id=1, source_target_pairs={{0,96},{8,40},{32,0},{40,72},{64,32},{72,104},{96,64},{104,8},{1,9... | collective-permute-start | bytes 2088968 | tf_op jit(solution)/shard_map/ppermute | solution.py:34
  73.9 21.8 %collective-permute-start.8 = (bf16[160,2176]{1,0:T(8,128)(2,1)}, bf16[160,2176]{1,0:T(8,128)(2,1)}, u32[]{:S(2)}, u32[]{:S(2)}) collective-permute-start(bf16[160,2176]{1,0:T(8,128)(2,1)} %collective-permute-done.7.refs_4_), channel_id=1, source_target_pairs={{0,32},{8,104},{32,64},{40,8},{64,96},{72,40},{96,0},{104,72},{1,3... | collective-permute-start | bytes 2088968 | tf_op jit(solution)/shard_map/ppermute | solution.py:34
  81.9 24.1 %collective-permute-start.10 = (bf16[160,2176]{1,0:T(8,128)(2,1)}, bf16[160,2176]{1,0:T(8,128)(2,1)}, u32[]{:S(2)}, u32[]{:S(2)}) collective-permute-start(bf16[160,2176]{1,0:T(8,128)(2,1)} %collective-permute-done.3.refs_0_), channel_id=1, source_target_pairs={{0,32},{8,104},{32,64},{40,8},{64,96},{72,40},{96,0},{104,72},{1,3... | collective-permute-start | bytes 2088968 | tf_op jit(solution)/shard_map/ppermute | solution.py:34
  81.9 24.0 %copy-start.12 = (s32[16]{0:T(128)S(1)}, s32[16]{0:T(128)}, u32[]{:S(2)}) copy-start(s32[16]{0:T(128)} %param.26) | copy-start | bytes 196
  85.1 25.4 %all-to-all-start.4 = ((bf16[8,16,3328]{2,1,0:T(8,128)(2,1)}), bf16[8,16,3328]{2,1,0:T(8,128)(2,1)S(1)}, u32[]{:S(2)}, u32[]{:S(2)}) async-start(bf16[8,16,3328]{2,1,0:T(8,128)(2,1)} %bitcast.9), calls=%async_computation.4 | async-start | bytes 1703936 | tf_op jit(solution)/shard_map/all_to_all | solution.py:147
  90.5 34.6 %collective-permute-start.15 = (bf16[160,2176]{1,0:T(8,128)(2,1)}, bf16[160,2176]{1,0:T(8,128)(2,1)S(1)}, u32[]{:S(2)}, u32[]{:S(2)}) collective-permute-start(bf16[160,2176]{1,0:T(8,128)(2,1)} %collective-permute-done.14.refs_6_), channel_id=1, source_target_pairs={{0,8},{8,0},{1,9},{9,1},{2,10},{10,2},{3,11},{11,3},{4,12},{12,4},... | collective-permute-start | bytes 2088968 | tf_op jit(solution)/shard_map/ppermute | solution.py:20
  90.6 39.0 %collective-permute-start.4 = (bf16[160,2176]{1,0:T(8,128)(2,1)}, bf16[160,2176]{1,0:T(8,128)(2,1)}, u32[]{:S(2)}, u32[]{:S(2)}) collective-permute-start(bf16[160,2176]{1,0:T(8,128)(2,1)} %collective-permute-done.3.refs_0_), channel_id=1, source_target_pairs={{0,8},{8,0},{1,9},{9,1},{2,10},{10,2},{3,11},{11,3},{4,12},{12,4},... | collective-permute-start | bytes 2088968 | tf_op jit(solution)/shard_map/ppermute | solution.py:20
  91.1 38.5 %collective-permute-start.6 = (bf16[160,2176]{1,0:T(8,128)(2,1)}, bf16[160,2176]{1,0:T(8,128)(2,1)}, u32[]{:S(2)}, u32[]{:S(2)}) collective-permute-start(bf16[160,2176]{1,0:T(8,128)(2,1)} %collective-permute-done.5.refs_2_), channel_id=1, source_target_pairs={{0,8},{8,0},{1,9},{9,1},{2,10},{10,2},{3,11},{11,3},{4,12},{12,4},... | collective-permute-start | bytes 2088968 | tf_op jit(solution)/shard_map/ppermute | solution.py:20
  95.7 33.9 %collective-permute-start.9 = (bf16[160,2176]{1,0:T(8,128)(2,1)}, bf16[160,2176]{1,0:T(8,128)(2,1)}, u32[]{:S(2)}, u32[]{:S(2)}) collective-permute-start(bf16[160,2176]{1,0:T(8,128)(2,1)} %collective-permute-done.8.refs_4_), channel_id=1, source_target_pairs={{0,8},{8,0},{1,9},{9,1},{2,10},{10,2},{3,11},{11,3},{4,12},{12,4},... | collective-permute-start | bytes 2088968 | tf_op jit(solution)/shard_map/ppermute | solution.py:20
  106.0 23.6 %collective-permute-start.11 = (bf16[160,2176]{1,0:T(8,128)(2,1)}, bf16[160,2176]{1,0:T(8,128)(2,1)}, u32[]{:S(2)}, u32[]{:S(2)}) collective-permute-start(bf16[160,2176]{1,0:T(8,128)(2,1)} %collective-permute-done.10.refs_6_), channel_id=1, source_target_pairs={{0,8},{8,0},{1,9},{9,1},{2,10},{10,2},{3,11},{11,3},{4,12},{12,4},... | collective-permute-start | bytes 2088968 | tf_op jit(solution)/shard_map/ppermute | solution.py:20
  111.5 23.3 %all-to-all-start.5 = ((f32[8,8,128]{2,1,0:T(8,128)}), f32[8,8,128]{2,1,0:T(8,128)S(1)}, u32[]{:S(2)}, u32[]{:S(2)}) async-start(f32[8,8,128]{2,1,0:T(8,128)} %shard_map.276), calls=%async_computation.5 | async-start | bytes 65536 | tf_op jit(solution)/shard_map/all_to_all | solution.py:147

commit v4 on v3

--- a/solution.py
+++ b/solution.py
@@ -198,7 +198,10 @@
     logits = total[:, :vocab] * lax.rsqrt(square / width + EPSILON)
     rows = reference[...].astype(F32)
     columns = lax.axis_index("head") * vocab + lax.broadcasted_iota(jnp.int32, logits.shape, 1)
-    picked = jnp.sum(jnp.where(columns == tokens[...], logits, 0.0), axis=-1, keepdims=True)
+    seqs = tokens.shape[0]
+    same = lax.broadcasted_iota(jnp.int32, (seqs, seqs), 0) == lax.broadcasted_iota(jnp.int32, (seqs, seqs), 1)
+    ids = jnp.sum(jnp.where(same, tokens[...].astype(F32)[None, :], 0.0), axis=-1, keepdims=True).astype(jnp.int32)
+    picked = jnp.sum(jnp.where(columns == ids, logits, 0.0), axis=-1, keepdims=True)
     roll_max = jnp.max(logits, axis=-1, keepdims=True)
     ref_max = jnp.max(rows, axis=-1, keepdims=True)
     roll_sum = jnp.sum(jnp.exp(logits - roll_max), axis=-1, keepdims=True)
@@ -266,7 +269,7 @@
         input_kernel,
         out_shape=jax.ShapeDtypeStruct((both.shape[0], cols), BF16),
         compiler_params=pltpu.CompilerParams(vmem_limit_bytes=12 * 2**20),
-        cost_estimate=pl.CostEstimate(flops=140000000, bytes_accessed=2000000, transcendentals=0),
+        cost_estimate=pl.CostEstimate(flops=20000000000, bytes_accessed=60000000, transcendentals=0),
     )(both, own, other)
 
 
@@ -297,36 +300,20 @@
     half = turned.shape[1] // 2
     rows = in_dt.shape[1]
     turned[:heads, :rows] = in_dt[...]
-    turned[:, half : half + rows] = other[...].astype(F32).T[:seqs].astype(turned.dtype)
-
-
-def prepared(x_state, bc_state, taps_x, off_x, taps_bc, off_bc, dt_bias, a_log, skip, in_dt, other, dt_at):
-    seqs, _, inner = x_state.shape
-    rows = in_dt.shape[0]
-    whole = pl.BlockSpec(memory_space=pltpu.VMEM)
-    return pl.pallas_call(
-        prepared_kernel,
-        out_shape=(
-            jax.ShapeDtypeStruct((seqs + 8, inner + bc_state.shape[2] + 128), F32),
-            jax.ShapeDtypeStruct((seqs, 512), BF16),
-        ),
-        grid=(1,),
-        in_specs=[whole] * 10 + [pl.BlockSpec((rows, 128), lambda i: (0, dt_at // 128))],
-        out_specs=(whole, whole),
-        cost_estimate=pl.CostEstimate(flops=1000000, bytes_accessed=300000, transcendentals=0),
-    )(
-        x_state.transpose(1, 0, 2), bc_state.transpose(1, 0, 2), taps_x, off_x, taps_bc, off_bc,
-        dt_bias, a_log, skip, in_dt.T, other,
-    )
-
-
-def mixer_kernel(heads, parts, scale, ready, steps, state, out, inflow, decays, b_out, held, turned, sems):
+    turned[:, half : half + rows] = other.astype(F32).T[:seqs].astype(turned.dtype)
+
+
+def mixer_kernel(
+    heads, dt_at, parts, scale, x_state, bc_state, taps_x, off_x, taps_bc, off_bc, dt_bias, a_log, skip, in_dt,
+    other, state, out, inflow, decays, b_out, turned, ready, steps,
+):
+    prepared_kernel(
+        x_state, bc_state, taps_x, off_x, taps_bc, off_bc, dt_bias, a_log, skip, in_dt,
+        other[:, dt_at : dt_at + 128], ready, steps,
+    )
     seqs = scale.shape[0]
     inner = heads * P_SIZE
     size = state.shape[2]
-    copies = [pltpu.make_async_copy(state.at[s], held.at[s], sems.at[s]) for s in range(seqs)]
-    for copy in copies:
-        copy.start()
     total = parts[0].astype(F32)
     for k in range(1, parts.shape[0]):
         total = total + parts[k].astype(F32)
@@ -337,8 +324,7 @@
     x_conv, b_vals, c_vals = conv[:, :inner], conv[:, inner : inner + size], conv[:, inner + size :]
     lane = lax.broadcasted_iota(jnp.int32, (inner, 128), 1)
     for s in range(seqs):
-        copies[s].wait()
-        sums = jnp.sum(held[s] * c_vals[s : s + 1, :], axis=-1, keepdims=True)
+        sums = jnp.sum(state[s] * c_vals[s : s + 1, :], axis=-1, keepdims=True)
         if s == 0:
             turned[...] = jnp.where(lane == s, sums, 0.0)
         else:
@@ -359,27 +345,26 @@
     b_out[...] = b_vals
 
 
-def mixer(parts, scale, ready, steps, state):
+def mixer(parts, scale, vectors, in_dt, other, dt_at, state):
     chips, seqs, _ = parts.shape
     _, heads, p_size, size = state.shape
     inner = heads * p_size
     return pl.pallas_call(
-        functools.partial(mixer_kernel, heads),
+        functools.partial(mixer_kernel, heads, dt_at),
         out_shape=(
-            jax.ShapeDtypeStruct((chips, seqs, inner + steps.shape[1]), BF16),
+            jax.ShapeDtypeStruct((chips, seqs, inner + 512), BF16),
             jax.ShapeDtypeStruct((seqs, inner), F32),
             jax.ShapeDtypeStruct((seqs, 128), F32),
             jax.ShapeDtypeStruct((seqs, size), F32),
         ),
-        in_specs=[pl.BlockSpec(memory_space=pltpu.VMEM)] * 4 + [pl.BlockSpec(memory_space=pl.ANY)],
         scratch_shapes=[
-            pltpu.VMEM((seqs, inner, size), F32),
             pltpu.VMEM((inner, 128), F32),
-            pltpu.SemaphoreType.DMA((seqs,)),
+            pltpu.VMEM((seqs + 8, inner + 2 * size + 128), F32),
+            pltpu.VMEM((seqs, 512), BF16),
         ],
-        compiler_params=pltpu.CompilerParams(vmem_limit_bytes=59 * 2**20),
+        compiler_params=pltpu.CompilerParams(vmem_limit_bytes=12 * 2**20),
         cost_estimate=pl.CostEstimate(flops=10000000, bytes_accessed=6000000, transcendentals=0),
-    )(parts, scale, ready, steps, state.reshape(seqs, inner, size))
+    )(parts, scale, *vectors, in_dt.T, other, state.reshape(seqs, inner, size))
 
 
 def mix_kernel(gated, gain, out_own, other, out, steps):
@@ -490,11 +475,11 @@
 
     partial_in = partial_inputs(both, full, other, in_cols).reshape(chips, seqs, in_cols)
     partial_in = exchange(partial_in, CHIPS)
-    ready, steps = prepared(
-        conv_x_state, conv_bc_state, conv_wx, conv_bx, conv_wbc, conv_bbc, dt_bias, a_log, skip_gain,
-        in_dt, other, dt_at,
-    )
-    gated, inflow, decay, b_vals = mixer(partial_in, scale, ready, steps, ssm_state)
+    vectors = (
+        conv_x_state.transpose(1, 0, 2), conv_bc_state.transpose(1, 0, 2), conv_wx, conv_bx, conv_wbc, conv_bbc,
+        dt_bias, a_log, skip_gain,
+    )
+    gated, inflow, decay, b_vals = mixer(partial_in, scale, vectors, in_dt, other, dt_at, ssm_state)
     new_state = (
         decay[:, :heads, None, None] * ssm_state
         + inflow.reshape(seqs, heads, P_SIZE)[:, :, :, None] * b_vals[:, None, None, :]
@@ -513,7 +498,7 @@
         mix, both, gains, lm_head.T, lm_other.T, inner * lax.axis_size("head")
     )
     parts = exchange(sent.reshape(chips, seqs, -1), CHIPS)
-    stats = head_stats(parts, ref_logits, token_ids[:, None], width, lax.axis_size("head"))
+    stats = head_stats(parts, ref_logits, token_ids, width, lax.axis_size("head"))
     stats = exchange(stats, "head")
     divergence, token_logprob = combined(stats, seqs)
     divergence, token_logprob = divergence[0], token_logprob[0]

time: 137 us -> 131 us (0.956)
  blocking collectives: 16.6 us -> 0 us
  waiting for transfers between devices: 41.9 us -> 51.6 us
  Pallas kernels: 28.4 us -> 23.6 us
  starting transfers between devices: 38.3 us -> 43 us
  local copies, waits for them, and re-layouts: 3.22 us -> 4.84 us
    all_to_all x1 -> x0, blocking collectives: 16.6 us -> none  [exchange(): return lax.all_to_all(blocks, axis, 0, 0, tiled=True)]
    all_to_all x5 -> x6, waiting for transfers between devices: 14.6 us -> 24.7 us  [exchange(): return lax.all_to_all(blocks, axis, 0, 0, tiled=True)]
    pallas_call x2 -> x1, Pallas kernels: 7.34 us -> 2.51 us  [mixer(): pl.pallas_call(functools.partial(mixer_kernel, heads, dt_at), out_shape=(...]
    all_to_all x5 -> x6, starting transfers between devices: 29.6 us -> 34.1 us  [exchange(): return lax.all_to_all(blocks, axis, 0, 0, tiled=True)]
    unnamed x26 -> x44, local copies, waits for them, and re-layouts: 2.18 us -> 4.66 us
  transfers between devices with their start and end apart: 21 -> 22, of which waited for: 8 -> 8; matrix products, arithmetic and copies ran while one was open for 5% -> 5% of each run, Pallas kernels for 19% -> 16%
where the time goes in v4:
time: 131 us; the launch traced here: 130 us
  waiting for transfers between devices  51.6 us (39%)
  starting transfers between devices  43 us (33%)
  Pallas kernels  23.6 us (18%)
  other arithmetic  6.01 us (5%)
  local copies, waits for them, and re-layouts  4.84 us (4%)
    all_to_all x6, starting transfers between devices, exchange(): return lax.all_to_all(blocks, axis, 0, 0, tiled=True)  34.1 us
    ppermute x6, waiting for transfers between devices, along_ring(): return lax.ppermute(array, ('x', 'core'), pairs)  26.9 us
    all_to_all x6, waiting for transfers between devices, exchange(): return lax.all_to_all(blocks, axis, 0, 0, tiled=True)  24.7 us
    pallas_call x2, Pallas kernels, placed(): pl.pallas_call(functools.partial(placed_kernel, tags, widths), out_shape=...  9.61 us
    ppermute x6, starting transfers between devices, along_ring(): return lax.ppermute(array, ('x', 'core'), pairs)  6.08 us
    add x1, other arithmetic, shards(): decay[:, :heads, None, None] * ssm_state  6.01 us
    unnamed x44, local copies, waits for them, and re-layouts  4.66 us
    pallas_call x1, Pallas kernels, partial_logits(): pl.pallas_call(functools.partial(logits_kernel, inner_total), out_shape=j...  3.1 us
  transfers between devices with their start and end apart: 22, of which 8 were waited for; matrix products, arithmetic and copies ran while one was open for 5% of the time, Pallas kernels for 16%

profile of v4, /device:TPU:0, one launch (start us, length us, event | category | flops | bytes accessed | tf_op | source)
XLA Modules:
  0.0 130.0 jit_solution(2989402534042768271)
XLA Ops:
  0.6 2.4 %shard_map.270 = (bf16[160,2304]{1,0:T(8,128)(2,1)}, bf16[160,2176]{1,0:T(8,128)(2,1)}) custom-call(bf16[160,640]{1,0:T(8,128)(2,1)} %in_z.1, bf16[160,640]{1,0:T(8,128)(2,1)} %in_x.1, bf16[160,256]{1,0:T(8,128)(2,1)} %in_bc.1, bf16[10,160]{1,0:T(8,128)(2,1)} %bitcast.20, bf16[160,640]{1,0:T(8,128)(2,1)} %out_own.1), custom_call_target="tpu_custom_call" | custom-call | flops 2000000 | bytes 1392640 | tf_op jit(solution)/shard_map/pallas_call | solution.py:57
  3.0 1.7 %shard_map.269 = (bf16[8,16,640]{2,1,0:T(8,128)(2,1)}, f32[16,128]{1,0:T(8,128)}) custom-call(bf16[16,2560]{1,0:T(8,128)(2,1)} %hidden.1, f32[2560]{0:T(1024)} %gain.2), custom_call_target="tpu_custom_call" | custom-call | flops 1000000 | bytes 300000 | tf_op jit(solution)/shard_map/pallas_call | solution.py:80
  4.7 5.8 %all-to-all-start = ((bf16[8,16,640]{2,1,0:T(8,128)(2,1)}), bf16[8,16,640]{2,1,0:T(8,128)(2,1)S(1)}, u32[]{:S(2)}, u32[]{:S(2)}) async-start(bf16[8,16,640]{2,1,0:T(8,128)(2,1)} %get-tuple-element.28), calls=%async_computation | async-start | bytes 327680 | tf_op jit(solution)/shard_map/all_to_all | solution.py:147
  10.5 2.0 %collective-permute-start.2 = (bf16[160,2176]{1,0:T(8,128)(2,1)}, bf16[160,2176]{1,0:T(8,128)(2,1)}, u32[]{:S(2)}, u32[]{:S(2)}) collective-permute-start(bf16[160,2176]{1,0:T(8,128)(2,1)} %get-tuple-element.38.refs_0_), channel_id=1, source_target_pairs={{0,16},{16,0},{1,17},{17,1},{2,18},{18,2},{3,19},{19,3},{4,20},{20... | collective-permute-start | bytes 2088968 | tf_op jit(solution)/shard_map/ppermute | solution.py:24
  12.5 4.7 %all-to-all-done = bf16[8,16,640]{2,1,0:T(8,128)(2,1)S(1)} async-done(((bf16[8,16,640]{2,1,0:T(8,128)(2,1)}), bf16[8,16,640]{2,1,0:T(8,128)(2,1)S(1)}, u32[]{:S(2)}, u32[]{:S(2)}) %all-to-all-start) | async-done | bytes 163872 | tf_op jit(solution)/shard_map/all_to_all | solution.py:147
  17.2 1.2 copy-done.20
  18.4 0.0 copy-start.10
  18.4 0.0 copy-start.11
  18.5 0.0 copy-start.13
  18.5 0.0 copy-start.14
  18.5 0.0 copy-start.15
  18.5 0.0 copy-start.17
  18.5 0.0 copy-start.18
  18.5 1.3 shard_map.271
  19.8 3.6 %all-to-all-start.1 = ((bf16[8,16,1664]{2,1,0:T(8,128)(2,1)}), bf16[8,16,1664]{2,1,0:T(8,128)(2,1)S(1)}, u32[]{:S(2)}, u32[]{:S(2)}) async-start(bf16[8,16,1664]{2,1,0:T(8,128)(2,1)} %bitcast.2), calls=%async_computation.1 | async-start | bytes 851968 | tf_op jit(solution)/shard_map/all_to_all | solution.py:147
  23.4 0.1 collective-permute-start.1
  23.5 11.2 %all-to-all-done.1.parts = bf16[8,16,1664]{2,1,0:T(8,128)(2,1)S(1)} async-done(((bf16[8,16,1664]{2,1,0:T(8,128)(2,1)}), bf16[8,16,1664]{2,1,0:T(8,128)(2,1)S(1)}, u32[]{:S(2)}, u32[]{:S(2)}) %all-to-all-start.1) | async-done | bytes 426016 | tf_op jit(solution)/shard_map/all_to_all | solution.py:147
  34.8 0.0 copy-start
  34.8 2.5 %copy-done = f32[16,10,64,128]{3,2,1,0:T(8,128)S(1)} copy-done((f32[16,10,64,128]{3,2,1,0:T(8,128)S(1)}, f32[16,10,64,128]{3,2,1,0:T(8,128)}, u32[]{:S(2)}) %copy-start) | copy-done | bytes 5242904
  37.3 2.5 %shard_map.272 = (bf16[8,16,1152]{2,1,0:T(8,128)(2,1)}, f32[16,640]{1,0:T(8,128)S(1)}, f32[16,128]{1,0:T(8,128)S(1)}, f32[16,128]{1,0:T(8,128)S(1)}) custom-call(bf16[8,16,1664]{2,1,0:T(8,128)(2,1)S(1)} %all-to-all-done.1.parts, f32[16,128]{1,0:T(8,128)S(1)} %copy-done.11, bf16[3,16,640]{2,1,0:T(8,128)(2,1)S(1)} %bitcast.19, ...), custom_call_target="tpu_custom_call" | custom-call | flops 10000000 | bytes 6000000 | tf_op jit(solution)/shard_map/pallas_call | solution.py:352
  39.8 4.4 %all-to-all-start.2 = ((bf16[8,16,1152]{2,1,0:T(8,128)(2,1)}), bf16[8,16,1152]{2,1,0:T(8,128)(2,1)S(1)}, u32[]{:S(2)}, u32[]{:S(2)}) async-start(bf16[8,16,1152]{2,1,0:T(8,128)(2,1)} %get-tuple-element.34), calls=%async_computation.2 | async-start | bytes 589824 | tf_op jit(solution)/shard_map/all_to_all | solution.py:147
  44.2 2.0 %collective-permute-start.7 = (bf16[160,2176]{1,0:T(8,128)(2,1)S(1)}, bf16[160,2176]{1,0:T(8,128)(2,1)}, u32[]{:S(2)}, u32[]{:S(2)}) collective-permute-start(bf16[160,2176]{1,0:T(8,128)(2,1)S(1)} %copy-done.3), channel_id=1, source_target_pairs={{0,32},{8,104},{32,64},{40,8},{64,96},{72,40},{96,0},{104,72},{1,3... | collective-permute-start | bytes 2088968 | tf_op jit(solution)/shard_map/ppermute | solution.py:34
  46.2 1.3 collective-permute-start.14
  47.5 0.7 collective-permute-start.3
  48.3 4.3 %all-to-all-done.2 = bf16[8,16,1152]{2,1,0:T(8,128)(2,1)S(1)} async-done(((bf16[8,16,1152]{2,1,0:T(8,128)(2,1)}), bf16[8,16,1152]{2,1,0:T(8,128)(2,1)S(1)}, u32[]{:S(2)}, u32[]{:S(2)}) %all-to-all-start.2) | async-done | bytes 294944 | tf_op jit(solution)/shard_map/all_to_all | solution.py:147
  52.7 1.4 %shard_map.273 = (bf16[8,128,384]{2,1,0:T(8,128)(2,1)}, bf16[10,2560]{1,0:T(8,128)(2,1)}) custom-call(bf16[128,1152]{1,0:T(8,128)(2,1)S(1)} %bitcast.15, f32[640]{0:T(1024)S(1)} %copy-done.12, bf16[160,640]{1,0:T(8,128)(2,1)S(1)} %copy-done.2, bf16[160,640]{1,0:T(8,128)(2,1)S(1)} %slice.8.other), custom_call_target="tpu_custom_call" | custom-call | flops 60000000 | bytes 2000000 | tf_op jit(solution)/shard_map/pallas_call | solution.py:400
  54.0 7.5 %all-to-all-start.3 = ((bf16[8,128,384]{2,1,0:T(8,128)(2,1)}), bf16[8,128,384]{2,1,0:T(8,128)(2,1)S(1)}, u32[]{:S(2)}, u32[]{:S(2)}) async-start(bf16[8,128,384]{2,1,0:T(8,128)(2,1)} %get-tuple-element.35), calls=%async_computation.3 | async-start | bytes 1572864 | tf_op jit(solution)/shard_map/all_to_all | solution.py:147
  61.5 4.7 %collective-permute-done.7.refs_4_ = bf16[160,2176]{1,0:T(8,128)(2,1)} collective-permute-done((bf16[160,2176]{1,0:T(8,128)(2,1)S(1)}, bf16[160,2176]{1,0:T(8,128)(2,1)}, u32[]{:S(2)}, u32[]{:S(2)}) %collective-permute-start.7) | collective-permute-done | bytes 696352 | tf_op jit(solution)/shard_map/ppermute | solution.py:34
  66.2 1.8 %collective-permute-start.5 = (bf16[160,2176]{1,0:T(8,128)(2,1)}, bf16[160,2176]{1,0:T(8,128)(2,1)}, u32[]{:S(2)}, u32[]{:S(2)}) collective-permute-start(bf16[160,2176]{1,0:T(8,128)(2,1)} %collective-permute-done.2.refs_2_), channel_id=1, source_target_pairs={{0,96},{8,40},{32,0},{40,72},{64,32},{72,104},{96,64},{104,8},{1,9... | collective-permute-start | bytes 2088968 | tf_op jit(solution)/shard_map/ppermute | solution.py:34
  68.1 0.2 collective-permute-start.8
  68.3 8.2 %collective-permute-done.3.refs_0_ = bf16[160,2176]{1,0:T(8,128)(2,1)} collective-permute-done((bf16[160,2176]{1,0:T(8,128)(2,1)}, bf16[160,2176]{1,0:T(8,128)(2,1)}, u32[]{:S(2)}, u32[]{:S(2)}) %collective-permute-start.3) | collective-permute-done | bytes 696352 | tf_op jit(solution)/shard_map/ppermute | solution.py:34
  76.5 0.1 reshape.41.gains
  76.6 0.9 copy-done.5
  77.5 3.1 %shard_map.274 = bf16[128,3328]{1,0:T(8,128)(2,1)} custom-call(bf16[8,128,384]{2,1,0:T(8,128)(2,1)S(1)} %all-to-all-done.3.mixed, bf16[128,640]{1,0:T(8,128)(2,1)S(1)} %bitcast.18, f32[16,160]{1,0:T(8,128)S(1)} %reshape.41.gains, bf16[160,3200]{1,0:T(8,128)(2,1)S(1)} %bitcast.16, bf16[160,3200]{1,0:T(8,128)(2,1)} %bitcast.8.lm_other), custom_call_target="tpu_custom_call" | custom-call | flops 300000000 | bytes 4000000 | tf_op jit(solution)/shard_map/pallas_call | solution.py:184
  80.6 5.4 %all-to-all-start.4 = ((bf16[8,16,3328]{2,1,0:T(8,128)(2,1)}), bf16[8,16,3328]{2,1,0:T(8,128)(2,1)S(1)}, u32[]{:S(2)}, u32[]{:S(2)}) async-start(bf16[8,16,3328]{2,1,0:T(8,128)(2,1)} %bitcast.9), calls=%async_computation.4 | async-start | bytes 1703936 | tf_op jit(solution)/shard_map/all_to_all | solution.py:147
  86.0 0.1 collective-permute-start.15
  86.1 0.5 collective-permute-start.4
  86.6 0.1 collective-permute-start.6
  86.7 2.3 %collective-permute-done.8.refs_4_ = bf16[160,2176]{1,0:T(8,128)(2,1)} collective-permute-done((bf16[160,2176]{1,0:T(8,128)(2,1)}, bf16[160,2176]{1,0:T(8,128)(2,1)}, u32[]{:S(2)}, u32[]{:S(2)}) %collective-permute-start.8) | collective-permute-done | bytes 696352 | tf_op jit(solution)/shard_map/ppermute | solution.py:34
  89.0 11.6 %collective-permute-done.10.refs_6_ = bf16[160,2176]{1,0:T(8,128)(2,1)} collective-permute-done((bf16[160,2176]{1,0:T(8,128)(2,1)}, bf16[160,2176]{1,0:T(8,128)(2,1)}, u32[]{:S(2)}, u32[]{:S(2)}) %collective-permute-start.10) | collective-permute-done | bytes 696352 | tf_op jit(solution)/shard_map/ppermute | solution.py:34
  100.6 0.1 mul.25
  100.7 4.4 %all-to-all-done.4.parts = bf16[8,16,3328]{2,1,0:T(8,128)(2,1)S(1)} async-done(((bf16[8,16,3328]{2,1,0:T(8,128)(2,1)}), bf16[8,16,3328]{2,1,0:T(8,128)(2,1)S(1)}, u32[]{:S(2)}, u32[]{:S(2)}) %all-to-all-start.4) | async-done | bytes 852000 | tf_op jit(solution)/shard_map/all_to_all | solution.py:147
  105.1 1.1 shard_map.275
  106.3 7.5 %all-to-all-start.5 = ((f32[8,8,128]{2,1,0:T(8,128)}), f32[8,8,128]{2,1,0:T(8,128)S(1)}, u32[]{:S(2)}, u32[]{:S(2)}) async-start(f32[8,8,128]{2,1,0:T(8,128)} %shard_map.275), calls=%async_computation.5 | async-start | bytes 65536 | tf_op jit(solution)/shard_map/all_to_all | solution.py:147
  113.8 6.0 %multiply_add_fusion = f32[16,10,64,128]{3,2,1,0:T(8,128)} fusion(f32[16,10,64,128]{3,2,1,0:T(8,128)} %param.23, f32[16,128]{1,0:T(8,128)S(1)} %get-tuple-element.33, f32[16,10,64]{2,1,0:T(8,128)S(1)} %mul.25, f32[16,10]{1,0:T(8,128)S(1)} %bitcast.23), kind=kLoop, calls=%fused_computation | loop fusion | flops 3932160 | bytes 10535552 | tf_op jit(solution)/shard_map/add | solution.py:484
  119.8 4.5 %shard_map.277 = (bf16[2560,640]{1,0:T(8,128)(2,1)}, bf16[2560,640]{1,0:T(8,128)(2,1)}, bf16[2560,256]{1,0:T(8,128)(2,1)}, bf16[2560,640]{1,0:T(8,128)(2,1)}) custom-call(bf16[160,2176]{1,0:T(8,128)(2,1)S(1)} %copy-done.3, bf16[160,2304]{1,0:T(8,128)(2,1)S(1)} %collective-permute-done.other.refs_1_, bf16[160,2176]{1,0:T(8,128)(2,1)} %collective-permute-done.2.refs_2_, ...), custom_call_target="tpu_custom_call" | custom-call | flops 10000000 | bytes 11796480 | tf_op jit(solution)/shard_map/pallas_call | solution.py:130
  124.3 5.1 %shard_map.278 = (bf16[2560,640]{1,0:T(8,128)(2,1)}, bf16[2560,640]{1,0:T(8,128)(2,1)}, bf16[2560,256]{1,0:T(8,128)(2,1)}, bf16[2560,640]{1,0:T(8,128)(2,1)}) custom-call(bf16[160,2176]{1,0:T(8,128)(2,1)} %collective-permute-done.3.refs_0_, ...), custom_call_target="tpu_custom_call", output_to_operand_aliasing={{0}: (8, {}), {1}: (9, {}), {2}: (10, {}), {3}: (11, {})} | custom-call | flops 10000000 | bytes 11141120 | tf_op jit(solution)/shard_map/pallas_call | solution.py:130
  129.4 0.6 shard_map.276
  (54 shorter events, 0.1 us)
Async XLA Ops:
  3.0 14.2 %collective-permute-start = (bf16[160,2304]{1,0:T(8,128)(2,1)}, bf16[160,2304]{1,0:T(8,128)(2,1)S(1)}, u32[]{:S(2)}, u32[]{:S(2)}) collective-permute-start(bf16[160,2304]{1,0:T(8,128)(2,1)} %get-tuple-element.29.own), channel_id=1, source_target_pairs={{0,8},{8,0},{1,9},{9,1},{2,10},{10,2},{3,11},{11,3},{4,12},{12,4},... | collective-permute-start | bytes 2211848 | tf_op jit(solution)/shard_map/ppermute | solution.py:20
  4.7 12.5 %all-to-all-start = ((bf16[8,16,640]{2,1,0:T(8,128)(2,1)}), bf16[8,16,640]{2,1,0:T(8,128)(2,1)S(1)}, u32[]{:S(2)}, u32[]{:S(2)}) async-start(bf16[8,16,640]{2,1,0:T(8,128)(2,1)} %get-tuple-element.28), calls=%async_computation | async-start | bytes 327680 | tf_op jit(solution)/shard_map/all_to_all | solution.py:147
  10.5 37.1 %collective-permute-start.2 = (bf16[160,2176]{1,0:T(8,128)(2,1)}, bf16[160,2176]{1,0:T(8,128)(2,1)}, u32[]{:S(2)}, u32[]{:S(2)}) collective-permute-start(bf16[160,2176]{1,0:T(8,128)(2,1)} %get-tuple-element.38.refs_0_), channel_id=1, source_target_pairs={{0,16},{16,0},{1,17},{17,1},{2,18},{18,2},{3,19},{19,3},{4,20},{20... | collective-permute-start | bytes 2088968 | tf_op jit(solution)/shard_map/ppermute | solution.py:24
  17.2 2.6 %copy-start.4 = (bf16[8,16,640]{2,1,0:T(8,128)(2,1)}, bf16[8,16,640]{2,1,0:T(8,128)(2,1)S(1)}, u32[]{:S(2)}) copy-start(bf16[8,16,640]{2,1,0:T(8,128)(2,1)S(1)} %all-to-all-done) | copy-start | bytes 491524
  17.2 1.2 copy-start.20
  18.4 5.0 %copy-start.1 = (bf16[3200,160]{0,1:T(8,128)(2,1)S(1)}, bf16[3200,160]{0,1:T(8,128)(2,1)}, u32[]{:S(2)}) copy-start(bf16[3200,160]{0,1:T(8,128)(2,1)} %param.33) | copy-start | bytes 3072004
  18.4 16.3 %copy-start.7 = (bf16[16,3,640]{2,0,1:T(8,128)(2,1)S(1)}, bf16[16,3,640]{2,0,1:T(8,128)(2,1)}, u32[]{:S(2)}) copy-start(bf16[16,3,640]{2,0,1:T(8,128)(2,1)} %param.24) | copy-start | bytes 184324
  18.4 16.3 %copy-start.8 = (bf16[160,10]{0,1:T(8,128)(2,1)S(1)}, bf16[160,10]{0,1:T(8,128)(2,1)}, u32[]{:S(2)}) copy-start(bf16[160,10]{0,1:T(8,128)(2,1)} %param.31) | copy-start | bytes 9604
  18.4 16.3 %copy-start.9 = (bf16[16,3,256]{2,0,1:T(8,128)(2,1)S(1)}, bf16[16,3,256]{2,0,1:T(8,128)(2,1)}, u32[]{:S(2)}) copy-start(bf16[16,3,256]{2,0,1:T(8,128)(2,1)} %param.25) | copy-start | bytes 73732
  18.4 16.3 %copy-start.10 = (f32[4,640]{1,0:T(4,128)S(1)}, f32[4,640]{1,0:T(4,128)}, u32[]{:S(2)}) copy-start(f32[4,640]{1,0:T(4,128)} %taps_x.1) | copy-start | bytes 30724
  18.4 16.3 %copy-start.11 = (f32[16,128]{1,0:T(8,128)S(1)}, f32[16,128]{1,0:T(8,128)}, u32[]{:S(2)}) copy-start(f32[16,128]{1,0:T(8,128)} %get-tuple-element.30.scale) | copy-start | bytes 24580
  18.5 16.3 %copy-start.13 = (f32[640]{0:T(1024)S(1)}, f32[640]{0:T(1024)}, u32[]{:S(2)}) copy-start(f32[640]{0:T(1024)} %off_x.1) | copy-start | bytes 7684
  18.5 16.3 %copy-start.14 = (f32[4,256]{1,0:T(4,128)S(1)}, f32[4,256]{1,0:T(4,128)}, u32[]{:S(2)}) copy-start(f32[4,256]{1,0:T(4,128)} %taps_bc.1) | copy-start | bytes 12292
  18.5 16.3 %copy-start.15 = (f32[256]{0:T(256)S(1)}, f32[256]{0:T(256)}, u32[]{:S(2)}) copy-start(f32[256]{0:T(256)} %off_bc.1) | copy-start | bytes 3076
  18.5 16.3 %copy-start.17 = (f32[10]{0:T(128)S(1)}, f32[10]{0:T(128)}, u32[]{:S(2)}) copy-start(f32[10]{0:T(128)} %dt_bias.1) | copy-start | bytes 124
  18.5 16.3 %copy-start.18 = (f32[10]{0:T(128)S(1)}, f32[10]{0:T(128)}, u32[]{:S(2)}) copy-start(f32[10]{0:T(128)} %a_log.1) | copy-start | bytes 124
  18.5 16.3 %copy-start.19 = (f32[10]{0:T(128)S(1)}, f32[10]{0:T(128)}, u32[]{:S(2)}) copy-start(f32[10]{0:T(128)} %skip.1) | copy-start | bytes 124
  18.5 25.7 %copy-start.3 = (bf16[160,2176]{1,0:T(8,128)(2,1)S(1)}, bf16[160,2176]{1,0:T(8,128)(2,1)}, u32[]{:S(2)}) copy-start(bf16[160,2176]{1,0:T(8,128)(2,1)} %get-tuple-element.38.refs_0_) | copy-start | bytes 2088964
  19.8 32.8 %copy-start.2 = (bf16[160,640]{1,0:T(8,128)(2,1)S(1)}, bf16[160,640]{1,0:T(8,128)(2,1)}, u32[]{:S(2)}) copy-start(bf16[160,640]{1,0:T(8,128)(2,1)} %out_own.1) | copy-start | bytes 614404
  19.8 32.8 %copy-start.12 = (f32[640]{0:T(1024)S(1)}, f32[640]{0:T(1024)}, u32[]{:S(2)}) copy-start(f32[640]{0:T(1024)} %gain.3) | copy-start | bytes 7684
  19.8 56.7 %copy-start.21 = (f32[2560]{0:T(1024)S(1)}, f32[2560]{0:T(1024)}, u32[]{:S(2)}) copy-start(f32[2560]{0:T(1024)} %param.43) | copy-start | bytes 30724
  19.8 14.9 %all-to-all-start.1 = ((bf16[8,16,1664]{2,1,0:T(8,128)(2,1)}), bf16[8,16,1664]{2,1,0:T(8,128)(2,1)S(1)}, u32[]{:S(2)}, u32[]{:S(2)}) async-start(bf16[8,16,1664]{2,1,0:T(8,128)(2,1)} %bitcast.2), calls=%async_computation.1 | async-start | bytes 851968 | tf_op jit(solution)/shard_map/all_to_all | solution.py:147
  23.4 44.6 %collective-permute-start.1 = (bf16[3200,160]{0,1:T(8,128)(2,1)S(1)}, bf16[3200,160]{0,1:T(8,128)(2,1)}, u32[]{:S(2)}, u32[]{:S(2)}) collective-permute-start(bf16[3200,160]{0,1:T(8,128)(2,1)S(1)} %copy-done.1), channel_id=1, source_target_pairs={{0,8},{8,0},{1,9},{9,1},{2,10},{10,2},{3,11},{11,3},{4,12},{12,4},... | collective-permute-start | bytes 3072008 | tf_op jit(solution)/shard_map/ppermute | solution.py:20
  34.8 2.5 %copy-start = (f32[16,10,64,128]{3,2,1,0:T(8,128)S(1)}, f32[16,10,64,128]{3,2,1,0:T(8,128)}, u32[]{:S(2)}) copy-start(f32[16,10,64,128]{3,2,1,0:T(8,128)} %param.23) | copy-start | bytes 15728644
  39.8 65.3 %copy-start.6 = (bf16[16,3200]{1,0:T(8,128)(2,1)S(1)}, bf16[16,3200]{1,0:T(8,128)(2,1)}, u32[]{:S(2)}) copy-start(bf16[16,3200]{1,0:T(8,128)(2,1)} %reference.1) | copy-start | bytes 307204
  39.8 65.3 %copy-start.16 = (s32[16]{0:T(128)S(1)}, s32[16]{0:T(128)}, u32[]{:S(2)}) copy-start(s32[16]{0:T(128)} %tokens.1) | copy-start | bytes 196
  39.8 12.8 %all-to-all-start.2 = ((bf16[8,16,1152]{2,1,0:T(8,128)(2,1)}), bf16[8,16,1152]{2,1,0:T(8,128)(2,1)S(1)}, u32[]{:S(2)}, u32[]{:S(2)}) async-start(bf16[8,16,1152]{2,1,0:T(8,128)(2,1)} %get-tuple-element.34), calls=%async_computation.2 | async-start | bytes 589824 | tf_op jit(solution)/shard_map/all_to_all | solution.py:147
  44.2 22.0 %collective-permute-start.7 = (bf16[160,2176]{1,0:T(8,128)(2,1)S(1)}, bf16[160,2176]{1,0:T(8,128)(2,1)}, u32[]{:S(2)}, u32[]{:S(2)}) collective-permute-start(bf16[160,2176]{1,0:T(8,128)(2,1)S(1)} %copy-done.3), channel_id=1, source_target_pairs={{0,32},{8,104},{32,64},{40,8},{64,96},{72,40},{96,0},{104,72},{1,3... | collective-permute-start | bytes 2088968 | tf_op jit(solution)/shard_map/ppermute | solution.py:34
  46.2 20.0 %collective-permute-start.14 = (bf16[160,2176]{1,0:T(8,128)(2,1)S(1)}, bf16[160,2176]{1,0:T(8,128)(2,1)}, u32[]{:S(2)}, u32[]{:S(2)}) collective-permute-start(bf16[160,2176]{1,0:T(8,128)(2,1)S(1)} %copy-done.3), channel_id=1, source_target_pairs={{0,96},{8,40},{32,0},{40,72},{64,32},{72,104},{96,64},{104,8},{1,9... | collective-permute-start | bytes 2088968 | tf_op jit(solution)/shard_map/ppermute | solution.py:34
  47.5 29.0 %collective-permute-start.3 = (bf16[160,2176]{1,0:T(8,128)(2,1)}, bf16[160,2176]{1,0:T(8,128)(2,1)}, u32[]{:S(2)}, u32[]{:S(2)}) collective-permute-start(bf16[160,2176]{1,0:T(8,128)(2,1)} %collective-permute-done.2.refs_2_), channel_id=1, source_target_pairs={{0,32},{8,104},{32,64},{40,8},{64,96},{72,40},{96,0},{104,72},{1,3... | collective-permute-start | bytes 2088968 | tf_op jit(solution)/shard_map/ppermute | solution.py:34
  54.0 22.6 %all-to-all-start.3 = ((bf16[8,128,384]{2,1,0:T(8,128)(2,1)}), bf16[8,128,384]{2,1,0:T(8,128)(2,1)S(1)}, u32[]{:S(2)}, u32[]{:S(2)}) async-start(bf16[8,128,384]{2,1,0:T(8,128)(2,1)} %get-tuple-element.35), calls=%async_computation.3 | async-start | bytes 1572864 | tf_op jit(solution)/shard_map/all_to_all | solution.py:147
  61.5 24.5 %collective-permute-start.12 = (bf16[160,2176]{1,0:T(8,128)(2,1)}, bf16[160,2176]{1,0:T(8,128)(2,1)}, u32[]{:S(2)}, u32[]{:S(2)}) collective-permute-start(bf16[160,2176]{1,0:T(8,128)(2,1)} %collective-permute-done.2.refs_2_), channel_id=1, source_target_pairs={{0,8},{8,0},{1,9},{9,1},{2,10},{10,2},{3,11},{11,3},{4,12},{12,4},... | collective-permute-start | bytes 2088968 | tf_op jit(solution)/shard_map/ppermute | solution.py:20
  66.2 19.9 %collective-permute-start.13 = (bf16[160,2176]{1,0:T(8,128)(2,1)}, bf16[160,2176]{1,0:T(8,128)(2,1)}, u32[]{:S(2)}, u32[]{:S(2)}) collective-permute-start(bf16[160,2176]{1,0:T(8,128)(2,1)} %collective-permute-done.7.refs_4_), channel_id=1, source_target_pairs={{0,8},{8,0},{1,9},{9,1},{2,10},{10,2},{3,11},{11,3},{4,12},{12,4},... | collective-permute-start | bytes 2088968 | tf_op jit(solution)/shard_map/ppermute | solution.py:20
  66.2 20.4 %collective-permute-start.5 = (bf16[160,2176]{1,0:T(8,128)(2,1)}, bf16[160,2176]{1,0:T(8,128)(2,1)}, u32[]{:S(2)}, u32[]{:S(2)}) collective-permute-start(bf16[160,2176]{1,0:T(8,128)(2,1)} %collective-permute-done.2.refs_2_), channel_id=1, source_target_pairs={{0,96},{8,40},{32,0},{40,72},{64,32},{72,104},{96,64},{104,8},{1,9... | collective-permute-start | bytes 2088968 | tf_op jit(solution)/shard_map/ppermute | solution.py:34
  68.1 20.9 %collective-permute-start.8 = (bf16[160,2176]{1,0:T(8,128)(2,1)}, bf16[160,2176]{1,0:T(8,128)(2,1)}, u32[]{:S(2)}, u32[]{:S(2)}) collective-permute-start(bf16[160,2176]{1,0:T(8,128)(2,1)} %collective-permute-done.7.refs_4_), channel_id=1, source_target_pairs={{0,32},{8,104},{32,64},{40,8},{64,96},{72,40},{96,0},{104,72},{1,3... | collective-permute-start | bytes 2088968 | tf_op jit(solution)/shard_map/ppermute | solution.py:34
  76.5 24.1 %collective-permute-start.10 = (bf16[160,2176]{1,0:T(8,128)(2,1)}, bf16[160,2176]{1,0:T(8,128)(2,1)}, u32[]{:S(2)}, u32[]{:S(2)}) collective-permute-start(bf16[160,2176]{1,0:T(8,128)(2,1)} %collective-permute-done.3.refs_0_), channel_id=1, source_target_pairs={{0,32},{8,104},{32,64},{40,8},{64,96},{72,40},{96,0},{104,72},{1,3... | collective-permute-start | bytes 2088968 | tf_op jit(solution)/shard_map/ppermute | solution.py:34
  76.6 0.9 copy-start.5
  80.6 24.5 %all-to-all-start.4 = ((bf16[8,16,3328]{2,1,0:T(8,128)(2,1)}), bf16[8,16,3328]{2,1,0:T(8,128)(2,1)S(1)}, u32[]{:S(2)}, u32[]{:S(2)}) async-start(bf16[8,16,3328]{2,1,0:T(8,128)(2,1)} %bitcast.9), calls=%async_computation.4 | async-start | bytes 1703936 | tf_op jit(solution)/shard_map/all_to_all | solution.py:147
  86.0 33.7 %collective-permute-start.15 = (bf16[160,2176]{1,0:T(8,128)(2,1)}, bf16[160,2176]{1,0:T(8,128)(2,1)S(1)}, u32[]{:S(2)}, u32[]{:S(2)}) collective-permute-start(bf16[160,2176]{1,0:T(8,128)(2,1)} %collective-permute-done.14.refs_6_), channel_id=1, source_target_pairs={{0,8},{8,0},{1,9},{9,1},{2,10},{10,2},{3,11},{11,3},{4,12},{12,4},... | collective-permute-start | bytes 2088968 | tf_op jit(solution)/shard_map/ppermute | solution.py:20
  86.1 38.1 %collective-permute-start.4 = (bf16[160,2176]{1,0:T(8,128)(2,1)}, bf16[160,2176]{1,0:T(8,128)(2,1)}, u32[]{:S(2)}, u32[]{:S(2)}) collective-permute-start(bf16[160,2176]{1,0:T(8,128)(2,1)} %collective-permute-done.3.refs_0_), channel_id=1, source_target_pairs={{0,8},{8,0},{1,9},{9,1},{2,10},{10,2},{3,11},{11,3},{4,12},{12,4},... | collective-permute-start | bytes 2088968 | tf_op jit(solution)/shard_map/ppermute | solution.py:20
  86.6 37.6 %collective-permute-start.6 = (bf16[160,2176]{1,0:T(8,128)(2,1)}, bf16[160,2176]{1,0:T(8,128)(2,1)}, u32[]{:S(2)}, u32[]{:S(2)}) collective-permute-start(bf16[160,2176]{1,0:T(8,128)(2,1)} %collective-permute-done.5.refs_2_), channel_id=1, source_target_pairs={{0,8},{8,0},{1,9},{9,1},{2,10},{10,2},{3,11},{11,3},{4,12},{12,4},... | collective-permute-start | bytes 2088968 | tf_op jit(solution)/shard_map/ppermute | solution.py:20
  89.0 35.2 %collective-permute-start.9 = (bf16[160,2176]{1,0:T(8,128)(2,1)}, bf16[160,2176]{1,0:T(8,128)(2,1)}, u32[]{:S(2)}, u32[]{:S(2)}) collective-permute-start(bf16[160,2176]{1,0:T(8,128)(2,1)} %collective-permute-done.8.refs_4_), channel_id=1, source_target_pairs={{0,8},{8,0},{1,9},{9,1},{2,10},{10,2},{3,11},{11,3},{4,12},{12,4},... | collective-permute-start | bytes 2088968 | tf_op jit(solution)/shard_map/ppermute | solution.py:20
  100.6 23.6 %collective-permute-start.11 = (bf16[160,2176]{1,0:T(8,128)(2,1)}, bf16[160,2176]{1,0:T(8,128)(2,1)}, u32[]{:S(2)}, u32[]{:S(2)}) collective-permute-start(bf16[160,2176]{1,0:T(8,128)(2,1)} %collective-permute-done.10.refs_6_), channel_id=1, source_target_pairs={{0,8},{8,0},{1,9},{9,1},{2,10},{10,2},{3,11},{11,3},{4,12},{12,4},... | collective-permute-start | bytes 2088968 | tf_op jit(solution)/shard_map/ppermute | solution.py:20
  106.3 23.2 %all-to-all-start.5 = ((f32[8,8,128]{2,1,0:T(8,128)}), f32[8,8,128]{2,1,0:T(8,128)S(1)}, u32[]{:S(2)}, u32[]{:S(2)}) async-start(f32[8,8,128]{2,1,0:T(8,128)} %shard_map.275), calls=%async_computation.5 | async-start | bytes 65536 | tf_op jit(solution)/shard_map/all_to_all | solution.py:147

commit v5 on v4

--- a/solution.py
+++ b/solution.py
@@ -12,6 +12,7 @@
 EPSILON = 1e-05
 CHIPS = ("x", "z")
 GROUP = ("x", "z", "core")
+HEAD = ("y", "w")
 F32 = jnp.float32
 BF16 = jnp.bfloat16
 
@@ -197,7 +198,7 @@
     square = total[:, vocab : vocab + 1] + total[:, vocab + 1 : vocab + 2]
     logits = total[:, :vocab] * lax.rsqrt(square / width + EPSILON)
     rows = reference[...].astype(F32)
-    columns = lax.axis_index("head") * vocab + lax.broadcasted_iota(jnp.int32, logits.shape, 1)
+    columns = (lax.axis_index("y") * 2 + lax.axis_index("w")) * vocab + lax.broadcasted_iota(jnp.int32, logits.shape, 1)
     seqs = tokens.shape[0]
     same = lax.broadcasted_iota(jnp.int32, (seqs, seqs), 0) == lax.broadcasted_iota(jnp.int32, (seqs, seqs), 1)
     ids = jnp.sum(jnp.where(same, tokens[...].astype(F32)[None, :], 0.0), axis=-1, keepdims=True).astype(jnp.int32)
@@ -383,24 +384,40 @@
     squares = jnp.sum(values * values, axis=-1, keepdims=True)
     gained = (values * gain[...][None, :]).astype(BF16)
     across = (((1,), (1,)), ((), ()))
-    out[0, :, :rows] = lax.dot_general(gained, out_own[...], across, preferred_element_type=F32).astype(BF16)
-    out[0, :, rows : 2 * rows] = lax.dot_general(
+    out[:, :rows] = lax.dot_general(gained, out_own[...], across, preferred_element_type=F32).astype(BF16)
+    out[:, rows : 2 * rows] = lax.dot_general(
         gained, other[...], across, preferred_element_type=F32
     ).astype(BF16)
-    spare = out.shape[2] - 2 * rows
+    spare = out.shape[1] - 2 * rows
     high = squares.astype(BF16).astype(F32)
-    out[0, :, 2 * rows :] = (column(0, high, spare) + column(1, squares - high, spare)).astype(BF16)
-    whole = out[0]
-    for k in range(1, out.shape[0]):
-        out[k] = whole
-
-
-def partial_mix(gated, gain, out_own, other, peers, heads, width):
+    out[:, 2 * rows :] = (column(0, high, spare) + column(1, squares - high, spare)).astype(BF16)
+
+
+def folded_kernel(at, mine, others, out):
+    total = mine[...].astype(F32) + others[...].astype(F32)
+    squares = total[:, at : at + 1] + total[:, at + 1 : at + 2]
+    high = squares.astype(BF16).astype(F32)
+    lane = lax.broadcasted_iota(jnp.int32, total.shape, 1)
+    total = jnp.where(lane == at, high, jnp.where(lane == at + 1, squares - high, total)).astype(BF16)
+    for k in range(out.shape[0]):
+        out[k] = total
+
+
+def folded(mine, others, at, peers):
+    return pl.pallas_call(
+        functools.partial(folded_kernel, at),
+        out_shape=jax.ShapeDtypeStruct((peers, *mine.shape), BF16),
+        compiler_params=pltpu.CompilerParams(vmem_limit_bytes=8 * 2**20),
+        cost_estimate=pl.CostEstimate(flops=1000000, bytes_accessed=600000, transcendentals=0),
+    )(mine, others)
+
+
+def partial_mix(gated, gain, out_own, other, heads, width):
     rows, _ = out_own.shape
     return pl.pallas_call(
         mix_kernel,
         out_shape=(
-            jax.ShapeDtypeStruct((peers, gated.shape[0], 2 * rows + 64), BF16),
+            jax.ShapeDtypeStruct((gated.shape[0], 2 * rows + 64), BF16),
             jax.ShapeDtypeStruct((heads, width), BF16),
         ),
         compiler_params=pltpu.CompilerParams(vmem_limit_bytes=12 * 2**20),
@@ -489,17 +506,19 @@
 
     gated = exchange(gated, CHIPS)
     mix, roll_dt = partial_mix(
-        gated.reshape(class_seqs, -1), norm_gain, out_t, other[:, in_cols:], lax.axis_size("head"), heads, width
+        gated.reshape(class_seqs, -1), norm_gain, out_t, other[:, in_cols:], heads, width
     )
     roll_dt = roll_dt.T
-    mix = exchange(mix, "head")
+    mix_pair = lax.ppermute(mix, "w", [(0, 1), (1, 0)])
+    mix = folded(mix, mix_pair, 2 * rows, lax.axis_size("y"))
+    mix = exchange(mix, "y")
 
     sent = partial_logits(
-        mix, both, gains, lm_head.T, lm_other.T, inner * lax.axis_size("head")
+        mix, both, gains, lm_head.T, lm_other.T, inner * lax.axis_size(HEAD)
     )
     parts = exchange(sent.reshape(chips, seqs, -1), CHIPS)
-    stats = head_stats(parts, ref_logits, token_ids, width, lax.axis_size("head"))
-    stats = exchange(stats, "head")
+    stats = head_stats(parts, ref_logits, token_ids, width, lax.axis_size(HEAD))
+    stats = exchange(stats, HEAD)
     divergence, token_logprob = combined(stats, seqs)
     divergence, token_logprob = divergence[0], token_logprob[0]
     return (new_state, divergence, token_logprob, roll_z, roll_x, roll_bc, roll_dt, roll_out)
@@ -507,43 +526,43 @@
 
 def solution(mesh):
     group, head = mesh.devices.shape
-    fine = Mesh(mesh.devices.reshape(group // 4, 2, 2, head), ("x", "z", "core", "head"))
+    fine = Mesh(mesh.devices.reshape(group // 4, 2, 2, head // 2, 2), ("x", "z", "core", "y", "w"))
     return jax.shard_map(
         shards,
         mesh=fine,
         in_specs=(
             P(GROUP, None),
-            P(GROUP, "head", None, None),
-            P(GROUP, None, "head"),
+            P(GROUP, HEAD, None, None),
+            P(GROUP, None, HEAD),
             P(GROUP, None, None),
             P(GROUP),
-            P(GROUP, "head"),
-            P(GROUP, "head"),
-            P(GROUP, "head"),
+            P(GROUP, HEAD),
+            P(GROUP, HEAD),
+            P(GROUP, HEAD),
             P(GROUP, None),
-            P(GROUP, "head"),
-            P(GROUP, "head"),
-            P("head", GROUP),
-            P(None, "head"),
-            P("head"),
+            P(GROUP, HEAD),
+            P(GROUP, HEAD),
+            P(HEAD, GROUP),
+            P(None, HEAD),
+            P(HEAD),
             P(),
             P(),
-            P("head"),
-            P("head"),
-            P("head"),
+            P(HEAD),
+            P(HEAD),
+            P(HEAD),
             P(),
-            P("head"),
+            P(HEAD),
             P(),
         ),
         out_specs=(
-            P(GROUP, "head", None, None),
+            P(GROUP, HEAD, None, None),
             P(GROUP),
             P(GROUP),
-            P(None, "head"),
-            P(None, "head"),
+            P(None, HEAD),
+            P(None, HEAD),
             P(),
-            P(None, "head"),
-            P(None, "head"),
+            P(None, HEAD),
+            P(None, HEAD),
         ),
         check_vma=False,
     )

time: 131 us -> 135 us (1.031)
  local copies, waits for them, and re-layouts: 4.84 us -> 15.8 us
  waiting for transfers between devices: 51.6 us -> 46.7 us
  Pallas kernels: 23.6 us -> 20.9 us
    ppermute x6, waiting for transfers between devices: 26.9 us -> 17.3 us  [along_ring(): return lax.ppermute(array, ('x', 'core'), pairs)]
    unnamed x44 -> x56, local copies, waits for them, and re-layouts: 4.66 us -> 14.2 us
    ppermute x1, waiting for transfers between devices: 0.01 us -> 7.05 us  [from_opposite(): return lax.ppermute(array, 'z', [(0, 1), (1, 0)])]
    all_to_all x6, waiting for transfers between devices: 24.7 us -> 19.8 us  [exchange(): return lax.all_to_all(blocks, axis, 0, 0, tiled=True)]
    all_to_all x6, starting transfers between devices: 34.1 us -> 29.3 us  [exchange(): return lax.all_to_all(blocks, axis, 0, 0, tiled=True)]
    ppermute x0 -> x1, starting transfers between devices: none -> 3.58 us  [shards(): mix_pair = lax.ppermute(mix, 'w', [(0, 1), (1, 0)])]
    ppermute x0 -> x1, waiting for transfers between devices: none -> 2.59 us  [shards(): mix_pair = lax.ppermute(mix, 'w', [(0, 1), (1, 0)])]
  transfers between devices with their start and end apart: 22 -> 23, of which waited for: 8 -> 9; matrix products, arithmetic and copies ran while one was open for 5% -> 6% of each run, Pallas kernels for 16% -> 10%
where the time goes in v5:
time: 135 us; the launch traced here: 134 us
  waiting for transfers between devices  46.7 us (35%)
  starting transfers between devices  43.2 us (32%)
  Pallas kernels  20.9 us (15%)
  local copies, waits for them, and re-layouts  15.8 us (12%)
  other arithmetic  6.08 us (5%)
    all_to_all x6, starting transfers between devices, exchange(): return lax.all_to_all(blocks, axis, 0, 0, tiled=True)  29.3 us
    all_to_all x6, waiting for transfers between devices, exchange(): return lax.all_to_all(blocks, axis, 0, 0, tiled=True)  19.8 us
    ppermute x6, waiting for transfers between devices, along_ring(): return lax.ppermute(array, ('x', 'core'), pairs)  17.3 us
    unnamed x56, local copies, waits for them, and re-layouts  14.2 us
    pallas_call x2, Pallas kernels, placed(): pl.pallas_call(functools.partial(placed_kernel, tags, widths), out_shape=...  9.15 us
    ppermute x6, starting transfers between devices, along_ring(): return lax.ppermute(array, ('x', 'core'), pairs)  7.15 us
    ppermute x1, waiting for transfers between devices, from_opposite(): return lax.ppermute(array, 'z', [(0, 1), (1, 0)])  7.05 us
    add x1, other arithmetic, shards(): decay[:, :heads, None, None] * ssm_state  6.08 us
  transfers between devices with their start and end apart: 23, of which 9 were waited for; matrix products, arithmetic and copies ran while one was open for 6% of the time, Pallas kernels for 10%

profile of v5, /device:TPU:0, one launch (start us, length us, event | category | flops | bytes accessed | tf_op | source)
XLA Modules:
  0.0 133.5 jit_solution(16447735376307294907)
XLA Ops:
  0.6 2.4 %shard_map.270 = (bf16[160,2304]{1,0:T(8,128)(2,1)}, bf16[160,2176]{1,0:T(8,128)(2,1)}) custom-call(bf16[160,640]{1,0:T(8,128)(2,1)} %in_z.1, bf16[160,640]{1,0:T(8,128)(2,1)} %in_x.1, bf16[160,256]{1,0:T(8,128)(2,1)} %in_bc.1, bf16[10,160]{1,0:T(8,128)(2,1)} %bitcast.22, bf16[160,640]{1,0:T(8,128)(2,1)} %out_own.1), custom_call_target="tpu_custom_call" | custom-call | flops 2000000 | bytes 1392640 | tf_op jit(solution)/shard_map/pallas_call | solution.py:58
  3.0 1.7 %shard_map.269 = (bf16[8,16,640]{2,1,0:T(8,128)(2,1)}, f32[16,128]{1,0:T(8,128)}) custom-call(bf16[16,2560]{1,0:T(8,128)(2,1)} %hidden.1, f32[2560]{0:T(1024)} %gain.2), custom_call_target="tpu_custom_call" | custom-call | flops 1000000 | bytes 300000 | tf_op jit(solution)/shard_map/pallas_call | solution.py:81
  4.7 5.8 %all-to-all-start = ((bf16[8,16,640]{2,1,0:T(8,128)(2,1)}), bf16[8,16,640]{2,1,0:T(8,128)(2,1)S(1)}, u32[]{:S(2)}, u32[]{:S(2)}) async-start(bf16[8,16,640]{2,1,0:T(8,128)(2,1)} %get-tuple-element.28), calls=%async_computation | async-start | bytes 327680 | tf_op jit(solution)/shard_map/all_to_all | solution.py:148
  10.5 2.0 %collective-permute-start.3 = (bf16[160,2176]{1,0:T(8,128)(2,1)}, bf16[160,2176]{1,0:T(8,128)(2,1)}, u32[]{:S(2)}, u32[]{:S(2)}) collective-permute-start(bf16[160,2176]{1,0:T(8,128)(2,1)} %get-tuple-element.38.refs_0_), channel_id=1, source_target_pairs={{0,16},{16,0},{1,17},{17,1},{2,18},{18,2},{3,19},{19,3},{4,20},{20... | collective-permute-start | bytes 2088968 | tf_op jit(solution)/shard_map/ppermute | solution.py:25
  12.5 4.7 %all-to-all-done = bf16[8,16,640]{2,1,0:T(8,128)(2,1)S(1)} async-done(((bf16[8,16,640]{2,1,0:T(8,128)(2,1)}), bf16[8,16,640]{2,1,0:T(8,128)(2,1)S(1)}, u32[]{:S(2)}, u32[]{:S(2)}) %all-to-all-start) | async-done | bytes 163872 | tf_op jit(solution)/shard_map/all_to_all | solution.py:148
  17.2 1.1 copy-done.27
  18.9 0.7 copy-done.5
  19.6 0.8 copy-done.7
  20.3 3.6 %all-to-all-start.1 = ((bf16[8,16,1664]{2,1,0:T(8,128)(2,1)}), bf16[8,16,1664]{2,1,0:T(8,128)(2,1)S(1)}, u32[]{:S(2)}, u32[]{:S(2)}) async-start(bf16[8,16,1664]{2,1,0:T(8,128)(2,1)} %bitcast.20), calls=%async_computation.1 | async-start | bytes 851968 | tf_op jit(solution)/shard_map/all_to_all | solution.py:148
  23.9 1.9 %collective-permute-start.8 = (bf16[160,2176]{1,0:T(8,128)(2,1)}, bf16[160,2176]{1,0:T(8,128)(2,1)}, u32[]{:S(2)}, u32[]{:S(2)}) collective-permute-start(bf16[160,2176]{1,0:T(8,128)(2,1)} %get-tuple-element.38.refs_0_), channel_id=1, source_target_pairs={{0,32},{8,104},{32,64},{40,8},{64,96},{72,40},{96,0},{104,72},{1,3... | collective-permute-start | bytes 2088968 | tf_op jit(solution)/shard_map/ppermute | solution.py:35
  25.9 1.4 %collective-permute-start.15 = (bf16[160,2176]{1,0:T(8,128)(2,1)}, bf16[160,2176]{1,0:T(8,128)(2,1)}, u32[]{:S(2)}, u32[]{:S(2)}) collective-permute-start(bf16[160,2176]{1,0:T(8,128)(2,1)} %get-tuple-element.38.refs_0_), channel_id=1, source_target_pairs={{0,96},{8,40},{32,0},{40,72},{64,32},{72,104},{96,64},{104,8},{1,9... | collective-permute-start | bytes 2088968 | tf_op jit(solution)/shard_map/ppermute | solution.py:35
  27.2 7.0 %collective-permute-done.3.refs_2_ = bf16[160,2176]{1,0:T(8,128)(2,1)} collective-permute-done((bf16[160,2176]{1,0:T(8,128)(2,1)}, bf16[160,2176]{1,0:T(8,128)(2,1)}, u32[]{:S(2)}, u32[]{:S(2)}) %collective-permute-start.3) | collective-permute-done | bytes 696352 | tf_op jit(solution)/shard_map/ppermute | solution.py:25
  34.3 1.4 %collective-permute-start.4 = (bf16[160,2176]{1,0:T(8,128)(2,1)}, bf16[160,2176]{1,0:T(8,128)(2,1)}, u32[]{:S(2)}, u32[]{:S(2)}) collective-permute-start(bf16[160,2176]{1,0:T(8,128)(2,1)} %collective-permute-done.3.refs_2_), channel_id=1, source_target_pairs={{0,32},{8,104},{32,64},{40,8},{64,96},{72,40},{96,0},{104,72},{1,3... | collective-permute-start | bytes 2088968 | tf_op jit(solution)/shard_map/ppermute | solution.py:35
  35.7 2.5 %copy-done = f32[16,10,64,128]{3,2,1,0:T(8,128)S(1)} copy-done((f32[16,10,64,128]{3,2,1,0:T(8,128)S(1)}, f32[16,10,64,128]{3,2,1,0:T(8,128)}, u32[]{:S(2)}) %copy-start) | copy-done | bytes 5242904
  38.2 0.7 copy-done.13
  38.9 0.7 copy-done.14
  39.6 0.7 copy-done.20
  40.3 0.7 copy-done.21
  41.0 0.7 copy-done.22
  41.7 0.7 copy-done.24
  42.3 0.7 copy-done.25
  43.6 1.8 %shard_map.272 = (bf16[8,16,1152]{2,1,0:T(8,128)(2,1)S(1)}, f32[16,640]{1,0:T(8,128)S(1)}, f32[16,128]{1,0:T(8,128)S(1)}, f32[16,128]{1,0:T(8,128)S(1)}) custom-call(bf16[8,16,1664]{2,1,0:T(8,128)(2,1)S(1)} %all-to-all-done.1.parts, f32[16,128]{1,0:T(8,128)S(1)} %copy-done.14, bf16[3,16,640]{2,1,0:T(8,128)(2,1)S(1)} %bitcast.21, ...), custom_call_target="tpu_custom_call" | custom-call | flops 10000000 | bytes 6000000 | tf_op jit(solution)/shard_map/pallas_call | solution.py:353
  45.4 0.7 copy-done.8
  47.4 4.1 %all-to-all-start.2 = ((bf16[8,16,1152]{2,1,0:T(8,128)(2,1)}), bf16[8,16,1152]{2,1,0:T(8,128)(2,1)S(1)}, u32[]{:S(2)}, u32[]{:S(2)}) async-start(bf16[8,16,1152]{2,1,0:T(8,128)(2,1)} %copy-done.8), calls=%async_computation.2 | async-start | bytes 589824 | tf_op jit(solution)/shard_map/all_to_all | solution.py:148
  51.5 0.7 slice.8.other
  52.2 6.6 %all-to-all-done.2 = bf16[8,16,1152]{2,1,0:T(8,128)(2,1)S(1)} async-done(((bf16[8,16,1152]{2,1,0:T(8,128)(2,1)}), bf16[8,16,1152]{2,1,0:T(8,128)(2,1)S(1)}, u32[]{:S(2)}, u32[]{:S(2)}) %all-to-all-start.2) | async-done | bytes 294944 | tf_op jit(solution)/shard_map/all_to_all | solution.py:148
  58.8 0.9 copy-done.3
  59.8 0.9 shard_map.273
  60.6 3.6 %collective-permute-start.1 = (bf16[128,384]{1,0:T(8,128)(2,1)S(1)}, bf16[128,384]{1,0:T(8,128)(2,1)S(1)}, u32[]{:S(2)}, u32[]{:S(2)}) collective-permute-start(bf16[128,384]{1,0:T(8,128)(2,1)S(1)} %get-tuple-element.35.mine), channel_id=1, source_target_pairs={{0,1},{1,0},{2,3},{3,2},{4,5},{5,4},{6,7},{7,6},{8,9},{9,8},{10,11... | collective-permute-start | bytes 294920 | tf_op jit(solution)/shard_map/ppermute | solution.py:512
  64.2 2.6 %collective-permute-done.1.others = bf16[128,384]{1,0:T(8,128)(2,1)S(1)} collective-permute-done((bf16[128,384]{1,0:T(8,128)(2,1)S(1)}, bf16[128,384]{1,0:T(8,128)(2,1)S(1)}, u32[]{:S(2)}, u32[]{:S(2)}) %collective-permute-start.1) | collective-permute-done | bytes 98336 | tf_op jit(solution)/shard_map/ppermute | solution.py:512
  66.8 0.9 shard_map.274
  67.7 4.5 %all-to-all-start.3 = ((bf16[4,128,384]{2,1,0:T(8,128)(2,1)}), bf16[4,128,384]{2,1,0:T(8,128)(2,1)S(1)}, u32[]{:S(2)}, u32[]{:S(2)}) async-start(bf16[4,128,384]{2,1,0:T(8,128)(2,1)} %shard_map.274), calls=%async_computation.3 | async-start | bytes 786432 | tf_op jit(solution)/shard_map/all_to_all | solution.py:148
  72.7 1.1 collective-permute-start.6
  73.8 0.9 collective-permute-start.9
  75.1 0.8 reshape.41.gains
  75.9 3.7 %all-to-all-done.3.mixed = bf16[4,128,384]{2,1,0:T(8,128)(2,1)S(1)} async-done(((bf16[4,128,384]{2,1,0:T(8,128)(2,1)}), bf16[4,128,384]{2,1,0:T(8,128)(2,1)S(1)}, u32[]{:S(2)}, u32[]{:S(2)}) %all-to-all-start.3) | async-done | bytes 393248 | tf_op jit(solution)/shard_map/all_to_all | solution.py:148
  79.6 0.9 copy-done.6
  80.5 1.9 %shard_map.275 = bf16[128,3328]{1,0:T(8,128)(2,1)} custom-call(bf16[4,128,384]{2,1,0:T(8,128)(2,1)S(1)} %all-to-all-done.3.mixed, bf16[128,640]{1,0:T(8,128)(2,1)S(1)} %bitcast.19, f32[16,160]{1,0:T(8,128)S(1)} %reshape.41.gains, bf16[160,3200]{1,0:T(8,128)(2,1)S(1)} %bitcast.16, bf16[160,3200]{1,0:T(8,128)(2,1)S(1)} %bitcast.17), custom_call_target="tpu_custom_call" | custom-call | flops 300000000 | bytes 4000000 | tf_op jit(solution)/shard_map/pallas_call | solution.py:185
  82.4 3.6 %all-to-all-start.4 = ((bf16[8,16,3328]{2,1,0:T(8,128)(2,1)}), bf16[8,16,3328]{2,1,0:T(8,128)(2,1)S(1)}, u32[]{:S(2)}, u32[]{:S(2)}) async-start(bf16[8,16,3328]{2,1,0:T(8,128)(2,1)} %bitcast.9), calls=%async_computation.4 | async-start | bytes 1703936 | tf_op jit(solution)/shard_map/all_to_all | solution.py:148
  86.5 5.0 %collective-permute-done.6.refs_2_ = bf16[160,2176]{1,0:T(8,128)(2,1)} collective-permute-done((bf16[160,2176]{1,0:T(8,128)(2,1)}, bf16[160,2176]{1,0:T(8,128)(2,1)}, u32[]{:S(2)}, u32[]{:S(2)}) %collective-permute-start.6) | collective-permute-done | bytes 696352 | tf_op jit(solution)/shard_map/ppermute | solution.py:35
  91.5 2.3 %collective-permute-done.9.refs_4_ = bf16[160,2176]{1,0:T(8,128)(2,1)} collective-permute-done((bf16[160,2176]{1,0:T(8,128)(2,1)}, bf16[160,2176]{1,0:T(8,128)(2,1)}, u32[]{:S(2)}, u32[]{:S(2)}) %collective-permute-start.9) | collective-permute-done | bytes 696352 | tf_op jit(solution)/shard_map/ppermute | solution.py:35
  93.8 10.0 %collective-permute-done.11.refs_6_ = bf16[160,2176]{1,0:T(8,128)(2,1)} collective-permute-done((bf16[160,2176]{1,0:T(8,128)(2,1)}, bf16[160,2176]{1,0:T(8,128)(2,1)}, u32[]{:S(2)}, u32[]{:S(2)}) %collective-permute-start.11) | collective-permute-done | bytes 696352 | tf_op jit(solution)/shard_map/ppermute | solution.py:35
  104.0 4.7 %all-to-all-done.4.parts = bf16[8,16,3328]{2,1,0:T(8,128)(2,1)S(1)} async-done(((bf16[8,16,3328]{2,1,0:T(8,128)(2,1)}), bf16[8,16,3328]{2,1,0:T(8,128)(2,1)S(1)}, u32[]{:S(2)}, u32[]{:S(2)}) %all-to-all-start.4) | async-done | bytes 852000 | tf_op jit(solution)/shard_map/all_to_all | solution.py:148
  108.7 1.1 shard_map.276
  109.8 7.8 %all-to-all-start.5 = ((f32[8,8,128]{2,1,0:T(8,128)}), f32[8,8,128]{2,1,0:T(8,128)S(1)}, u32[]{:S(2)}, u32[]{:S(2)}) async-start(f32[8,8,128]{2,1,0:T(8,128)} %shard_map.276), calls=%async_computation.5 | async-start | bytes 65536 | tf_op jit(solution)/shard_map/all_to_all | solution.py:148
  117.7 6.1 %multiply_add_fusion = f32[16,10,64,128]{3,2,1,0:T(8,128)} fusion(f32[16,10,64,128]{3,2,1,0:T(8,128)} %param.23, f32[16,128]{1,0:T(8,128)S(1)} %copy-done.18, f32[16,10,64]{2,1,0:T(8,128)S(1)} %mul.25, f32[16,10]{1,0:T(8,128)S(1)} %bitcast.25), kind=kLoop, calls=%fused_computation | loop fusion | flops 3932160 | bytes 10535552 | tf_op jit(solution)/shard_map/add | solution.py:501
  123.8 4.5 %shard_map.278 = (bf16[2560,640]{1,0:T(8,128)(2,1)}, bf16[2560,640]{1,0:T(8,128)(2,1)}, bf16[2560,256]{1,0:T(8,128)(2,1)}, bf16[2560,640]{1,0:T(8,128)(2,1)}) custom-call(bf16[160,2176]{1,0:T(8,128)(2,1)S(1)} %copy-done.4, bf16[160,2304]{1,0:T(8,128)(2,1)S(1)} %collective-permute-done.other.refs_1_, bf16[160,2176]{1,0:T(8,128)(2,1)} %collective-permute-done.3.refs_2_, ...), custom_call_target="tpu_custom_call" | custom-call | flops 10000000 | bytes 11796480 | tf_op jit(solution)/shard_map/pallas_call | solution.py:131
  128.8 4.7 %shard_map.279 = (bf16[2560,640]{1,0:T(8,128)(2,1)}, bf16[2560,640]{1,0:T(8,128)(2,1)}, bf16[2560,256]{1,0:T(8,128)(2,1)}, bf16[2560,640]{1,0:T(8,128)(2,1)}) custom-call(bf16[160,2176]{1,0:T(8,128)(2,1)} %collective-permute-done.4.refs_0_, ...), custom_call_target="tpu_custom_call", output_to_operand_aliasing={{0}: (8, {}), {1}: (9, {}), {2}: (10, {}), {3}: (11, {})} | custom-call | flops 10000000 | bytes 11141120 | tf_op jit(solution)/shard_map/pallas_call | solution.py:131
  (69 shorter events, 4.6 us)
Async XLA Ops:
  3.0 14.2 %collective-permute-start = (bf16[160,2304]{1,0:T(8,128)(2,1)}, bf16[160,2304]{1,0:T(8,128)(2,1)S(1)}, u32[]{:S(2)}, u32[]{:S(2)}) collective-permute-start(bf16[160,2304]{1,0:T(8,128)(2,1)} %get-tuple-element.29.own), channel_id=1, source_target_pairs={{0,8},{8,0},{1,9},{9,1},{2,10},{10,2},{3,11},{11,3},{4,12},{12,4},... | collective-permute-start | bytes 2211848 | tf_op jit(solution)/shard_map/ppermute | solution.py:21
  4.7 12.5 %all-to-all-start = ((bf16[8,16,640]{2,1,0:T(8,128)(2,1)}), bf16[8,16,640]{2,1,0:T(8,128)(2,1)S(1)}, u32[]{:S(2)}, u32[]{:S(2)}) async-start(bf16[8,16,640]{2,1,0:T(8,128)(2,1)} %get-tuple-element.28), calls=%async_computation | async-start | bytes 327680 | tf_op jit(solution)/shard_map/all_to_all | solution.py:148
  10.5 23.8 %collective-permute-start.3 = (bf16[160,2176]{1,0:T(8,128)(2,1)}, bf16[160,2176]{1,0:T(8,128)(2,1)}, u32[]{:S(2)}, u32[]{:S(2)}) collective-permute-start(bf16[160,2176]{1,0:T(8,128)(2,1)} %get-tuple-element.38.refs_0_), channel_id=1, source_target_pairs={{0,16},{16,0},{1,17},{17,1},{2,18},{18,2},{3,19},{19,3},{4,20},{20... | collective-permute-start | bytes 2088968 | tf_op jit(solution)/shard_map/ppermute | solution.py:25
  12.5 61.3 %collective-permute-start.2 = (bf16[3200,160]{0,1:T(8,128)(2,1)}, bf16[3200,160]{0,1:T(8,128)(2,1)S(1)}, u32[]{:S(2)}, u32[]{:S(2)}) collective-permute-start(bf16[3200,160]{0,1:T(8,128)(2,1)} %param.33), channel_id=1, source_target_pairs={{0,8},{8,0},{1,9},{9,1},{2,10},{10,2},{3,11},{11,3},{4,12},{12,4},... | collective-permute-start | bytes 3072008 | tf_op jit(solution)/shard_map/ppermute | solution.py:21
  17.2 1.1 copy-start.27
  18.4 17.4 %copy-start.10 = (bf16[16,3,640]{2,0,1:T(8,128)(2,1)S(1)}, bf16[16,3,640]{2,0,1:T(8,128)(2,1)}, u32[]{:S(2)}) copy-start(bf16[16,3,640]{2,0,1:T(8,128)(2,1)} %param.24) | copy-start | bytes 184324
  18.4 17.4 %copy-start.11 = (bf16[160,10]{0,1:T(8,128)(2,1)S(1)}, bf16[160,10]{0,1:T(8,128)(2,1)}, u32[]{:S(2)}) copy-start(bf16[160,10]{0,1:T(8,128)(2,1)} %param.31) | copy-start | bytes 9604
  18.4 17.4 %copy-start.12 = (bf16[16,3,256]{2,0,1:T(8,128)(2,1)S(1)}, bf16[16,3,256]{2,0,1:T(8,128)(2,1)}, u32[]{:S(2)}) copy-start(bf16[16,3,256]{2,0,1:T(8,128)(2,1)} %param.25) | copy-start | bytes 73732
  18.4 61.2 %copy-start.1 = (bf16[3200,160]{0,1:T(8,128)(2,1)S(1)}, bf16[3200,160]{0,1:T(8,128)(2,1)}, u32[]{:S(2)}) copy-start(bf16[3200,160]{0,1:T(8,128)(2,1)} %param.33) | copy-start | bytes 3072004
  18.9 0.7 copy-start.5
  19.6 0.8 copy-start.7
  20.3 38.5 %copy-start.2 = (bf16[160,640]{1,0:T(8,128)(2,1)S(1)}, bf16[160,640]{1,0:T(8,128)(2,1)}, u32[]{:S(2)}) copy-start(bf16[160,640]{1,0:T(8,128)(2,1)} %out_own.1) | copy-start | bytes 614404
  20.3 38.5 %copy-start.19 = (f32[640]{0:T(1024)S(1)}, f32[640]{0:T(1024)}, u32[]{:S(2)}) copy-start(f32[640]{0:T(1024)} %gain.3) | copy-start | bytes 7684
  20.3 15.4 %all-to-all-start.1 = ((bf16[8,16,1664]{2,1,0:T(8,128)(2,1)}), bf16[8,16,1664]{2,1,0:T(8,128)(2,1)S(1)}, u32[]{:S(2)}, u32[]{:S(2)}) async-start(bf16[8,16,1664]{2,1,0:T(8,128)(2,1)} %bitcast.20), calls=%async_computation.1 | async-start | bytes 851968 | tf_op jit(solution)/shard_map/all_to_all | solution.py:148
  23.9 48.3 %collective-permute-start.8 = (bf16[160,2176]{1,0:T(8,128)(2,1)}, bf16[160,2176]{1,0:T(8,128)(2,1)}, u32[]{:S(2)}, u32[]{:S(2)}) collective-permute-start(bf16[160,2176]{1,0:T(8,128)(2,1)} %get-tuple-element.38.refs_0_), channel_id=1, source_target_pairs={{0,32},{8,104},{32,64},{40,8},{64,96},{72,40},{96,0},{104,72},{1,3... | collective-permute-start | bytes 2088968 | tf_op jit(solution)/shard_map/ppermute | solution.py:35
  25.9 46.9 %collective-permute-start.15 = (bf16[160,2176]{1,0:T(8,128)(2,1)}, bf16[160,2176]{1,0:T(8,128)(2,1)}, u32[]{:S(2)}, u32[]{:S(2)}) collective-permute-start(bf16[160,2176]{1,0:T(8,128)(2,1)} %get-tuple-element.38.refs_0_), channel_id=1, source_target_pairs={{0,96},{8,40},{32,0},{40,72},{64,32},{72,104},{96,64},{104,8},{1,9... | collective-permute-start | bytes 2088968 | tf_op jit(solution)/shard_map/ppermute | solution.py:35
  34.3 40.5 %collective-permute-start.4 = (bf16[160,2176]{1,0:T(8,128)(2,1)}, bf16[160,2176]{1,0:T(8,128)(2,1)}, u32[]{:S(2)}, u32[]{:S(2)}) collective-permute-start(bf16[160,2176]{1,0:T(8,128)(2,1)} %collective-permute-done.3.refs_2_), channel_id=1, source_target_pairs={{0,32},{8,104},{32,64},{40,8},{64,96},{72,40},{96,0},{104,72},{1,3... | collective-permute-start | bytes 2088968 | tf_op jit(solution)/shard_map/ppermute | solution.py:35
  35.7 2.5 %copy-start = (f32[16,10,64,128]{3,2,1,0:T(8,128)S(1)}, f32[16,10,64,128]{3,2,1,0:T(8,128)}, u32[]{:S(2)}) copy-start(f32[16,10,64,128]{3,2,1,0:T(8,128)} %param.23) | copy-start | bytes 15728644
  38.2 0.7 copy-start.13
  38.9 0.7 copy-start.14
  39.6 0.7 copy-start.20
  40.3 0.7 copy-start.21
  41.0 0.7 copy-start.22
  41.7 0.7 copy-start.24
  42.3 0.7 copy-start.25
  45.4 0.7 copy-start.8
  47.3 61.4 %copy-start.9 = (bf16[16,3200]{1,0:T(8,128)(2,1)S(1)}, bf16[16,3200]{1,0:T(8,128)(2,1)}, u32[]{:S(2)}) copy-start(bf16[16,3200]{1,0:T(8,128)(2,1)} %reference.1) | copy-start | bytes 307204
  47.3 61.4 %copy-start.23 = (s32[16]{0:T(128)S(1)}, s32[16]{0:T(128)}, u32[]{:S(2)}) copy-start(s32[16]{0:T(128)} %tokens.1) | copy-start | bytes 196
  47.3 70.3 %copy-start.16 = (f32[16,128]{1,0:T(8,128)S(1)}, f32[16,128]{1,0:T(8,128)}, u32[]{:S(2)}) copy-start(f32[16,128]{1,0:T(8,128)} %copy-done.15) | copy-start | bytes 24580
  47.4 70.3 %copy-start.18 = (f32[16,128]{1,0:T(8,128)S(1)}, f32[16,128]{1,0:T(8,128)}, u32[]{:S(2)}) copy-start(f32[16,128]{1,0:T(8,128)} %copy-done.17) | copy-start | bytes 24580
  47.4 11.5 %all-to-all-start.2 = ((bf16[8,16,1152]{2,1,0:T(8,128)(2,1)}), bf16[8,16,1152]{2,1,0:T(8,128)(2,1)S(1)}, u32[]{:S(2)}, u32[]{:S(2)}) async-start(bf16[8,16,1152]{2,1,0:T(8,128)(2,1)} %copy-done.8), calls=%async_computation.2 | async-start | bytes 589824 | tf_op jit(solution)/shard_map/all_to_all | solution.py:148
  58.8 0.9 copy-start.3
  60.6 6.2 %collective-permute-start.1 = (bf16[128,384]{1,0:T(8,128)(2,1)S(1)}, bf16[128,384]{1,0:T(8,128)(2,1)S(1)}, u32[]{:S(2)}, u32[]{:S(2)}) collective-permute-start(bf16[128,384]{1,0:T(8,128)(2,1)S(1)} %get-tuple-element.35.mine), channel_id=1, source_target_pairs={{0,1},{1,0},{2,3},{3,2},{4,5},{5,4},{6,7},{7,6},{8,9},{9,8},{10,11... | collective-permute-start | bytes 294920 | tf_op jit(solution)/shard_map/ppermute | solution.py:512
  67.7 11.8 %all-to-all-start.3 = ((bf16[4,128,384]{2,1,0:T(8,128)(2,1)}), bf16[4,128,384]{2,1,0:T(8,128)(2,1)S(1)}, u32[]{:S(2)}, u32[]{:S(2)}) async-start(bf16[4,128,384]{2,1,0:T(8,128)(2,1)} %shard_map.274), calls=%async_computation.3 | async-start | bytes 786432 | tf_op jit(solution)/shard_map/all_to_all | solution.py:148
  72.2 13.7 %collective-permute-start.13 = (bf16[160,2176]{1,0:T(8,128)(2,1)}, bf16[160,2176]{1,0:T(8,128)(2,1)}, u32[]{:S(2)}, u32[]{:S(2)}) collective-permute-start(bf16[160,2176]{1,0:T(8,128)(2,1)} %collective-permute-done.3.refs_2_), channel_id=1, source_target_pairs={{0,8},{8,0},{1,9},{9,1},{2,10},{10,2},{3,11},{11,3},{4,12},{12,4},... | collective-permute-start | bytes 2088968 | tf_op jit(solution)/shard_map/ppermute | solution.py:21
  72.2 13.8 %collective-permute-start.14 = (bf16[160,2176]{1,0:T(8,128)(2,1)}, bf16[160,2176]{1,0:T(8,128)(2,1)}, u32[]{:S(2)}, u32[]{:S(2)}) collective-permute-start(bf16[160,2176]{1,0:T(8,128)(2,1)} %collective-permute-done.8.refs_4_), channel_id=1, source_target_pairs={{0,8},{8,0},{1,9},{9,1},{2,10},{10,2},{3,11},{11,3},{4,12},{12,4},... | collective-permute-start | bytes 2088968 | tf_op jit(solution)/shard_map/ppermute | solution.py:21
  72.7 18.8 %collective-permute-start.6 = (bf16[160,2176]{1,0:T(8,128)(2,1)}, bf16[160,2176]{1,0:T(8,128)(2,1)}, u32[]{:S(2)}, u32[]{:S(2)}) collective-permute-start(bf16[160,2176]{1,0:T(8,128)(2,1)} %collective-permute-done.3.refs_2_), channel_id=1, source_target_pairs={{0,96},{8,40},{32,0},{40,72},{64,32},{72,104},{96,64},{104,8},{1,9... | collective-permute-start | bytes 2088968 | tf_op jit(solution)/shard_map/ppermute | solution.py:35
  73.8 20.0 %collective-permute-start.9 = (bf16[160,2176]{1,0:T(8,128)(2,1)}, bf16[160,2176]{1,0:T(8,128)(2,1)}, u32[]{:S(2)}, u32[]{:S(2)}) collective-permute-start(bf16[160,2176]{1,0:T(8,128)(2,1)} %collective-permute-done.8.refs_4_), channel_id=1, source_target_pairs={{0,32},{8,104},{32,64},{40,8},{64,96},{72,40},{96,0},{104,72},{1,3... | collective-permute-start | bytes 2088968 | tf_op jit(solution)/shard_map/ppermute | solution.py:35
  74.7 29.1 %collective-permute-start.11 = (bf16[160,2176]{1,0:T(8,128)(2,1)}, bf16[160,2176]{1,0:T(8,128)(2,1)}, u32[]{:S(2)}, u32[]{:S(2)}) collective-permute-start(bf16[160,2176]{1,0:T(8,128)(2,1)} %collective-permute-done.4.refs_0_), channel_id=1, source_target_pairs={{0,32},{8,104},{32,64},{40,8},{64,96},{72,40},{96,0},{104,72},{1,3... | collective-permute-start | bytes 2088968 | tf_op jit(solution)/shard_map/ppermute | solution.py:35
  79.6 0.9 copy-start.6
  82.4 26.3 %all-to-all-start.4 = ((bf16[8,16,3328]{2,1,0:T(8,128)(2,1)}), bf16[8,16,3328]{2,1,0:T(8,128)(2,1)S(1)}, u32[]{:S(2)}, u32[]{:S(2)}) async-start(bf16[8,16,3328]{2,1,0:T(8,128)(2,1)} %bitcast.9), calls=%async_computation.4 | async-start | bytes 1703936 | tf_op jit(solution)/shard_map/all_to_all | solution.py:148
  86.0 37.8 %collective-permute-start.16 = (bf16[160,2176]{1,0:T(8,128)(2,1)}, bf16[160,2176]{1,0:T(8,128)(2,1)S(1)}, u32[]{:S(2)}, u32[]{:S(2)}) collective-permute-start(bf16[160,2176]{1,0:T(8,128)(2,1)} %collective-permute-done.15.refs_6_), channel_id=1, source_target_pairs={{0,8},{8,0},{1,9},{9,1},{2,10},{10,2},{3,11},{11,3},{4,12},{12,4},... | collective-permute-start | bytes 2088968 | tf_op jit(solution)/shard_map/ppermute | solution.py:21
  86.1 42.8 %collective-permute-start.5 = (bf16[160,2176]{1,0:T(8,128)(2,1)}, bf16[160,2176]{1,0:T(8,128)(2,1)S(1)}, u32[]{:S(2)}, u32[]{:S(2)}) collective-permute-start(bf16[160,2176]{1,0:T(8,128)(2,1)} %collective-permute-done.4.refs_0_), channel_id=1, source_target_pairs={{0,8},{8,0},{1,9},{9,1},{2,10},{10,2},{3,11},{11,3},{4,12},{12,4},... | collective-permute-start | bytes 2088968 | tf_op jit(solution)/shard_map/ppermute | solution.py:21
  91.5 37.3 %collective-permute-start.7 = (bf16[160,2176]{1,0:T(8,128)(2,1)}, bf16[160,2176]{1,0:T(8,128)(2,1)}, u32[]{:S(2)}, u32[]{:S(2)}) collective-permute-start(bf16[160,2176]{1,0:T(8,128)(2,1)} %collective-permute-done.6.refs_2_), channel_id=1, source_target_pairs={{0,8},{8,0},{1,9},{9,1},{2,10},{10,2},{3,11},{11,3},{4,12},{12,4},... | collective-permute-start | bytes 2088968 | tf_op jit(solution)/shard_map/ppermute | solution.py:21
  93.8 35.0 %collective-permute-start.10 = (bf16[160,2176]{1,0:T(8,128)(2,1)}, bf16[160,2176]{1,0:T(8,128)(2,1)}, u32[]{:S(2)}, u32[]{:S(2)}) collective-permute-start(bf16[160,2176]{1,0:T(8,128)(2,1)} %collective-permute-done.9.refs_4_), channel_id=1, source_target_pairs={{0,8},{8,0},{1,9},{9,1},{2,10},{10,2},{3,11},{11,3},{4,12},{12,4},... | collective-permute-start | bytes 2088968 | tf_op jit(solution)/shard_map/ppermute | solution.py:21
  103.9 25.0 %collective-permute-start.12 = (bf16[160,2176]{1,0:T(8,128)(2,1)}, bf16[160,2176]{1,0:T(8,128)(2,1)}, u32[]{:S(2)}, u32[]{:S(2)}) collective-permute-start(bf16[160,2176]{1,0:T(8,128)(2,1)} %collective-permute-done.11.refs_6_), channel_id=1, source_target_pairs={{0,8},{8,0},{1,9},{9,1},{2,10},{10,2},{3,11},{11,3},{4,12},{12,4},... | collective-permute-start | bytes 2088968 | tf_op jit(solution)/shard_map/ppermute | solution.py:21
  109.8 18.4 %all-to-all-start.5 = ((f32[8,8,128]{2,1,0:T(8,128)}), f32[8,8,128]{2,1,0:T(8,128)S(1)}, u32[]{:S(2)}, u32[]{:S(2)}) async-start(f32[8,8,128]{2,1,0:T(8,128)} %shard_map.276), calls=%async_computation.5 | async-start | bytes 65536 | tf_op jit(solution)/shard_map/all_to_all | solution.py:148
  117.7 6.1 %copy-start.4 = (bf16[160,2176]{1,0:T(8,128)(2,1)S(1)}, bf16[160,2176]{1,0:T(8,128)(2,1)}, u32[]{:S(2)}) copy-start(bf16[160,2176]{1,0:T(8,128)(2,1)} %get-tuple-element.38.refs_0_) | copy-start | bytes 2088964
  (3 other events, 1.8 us)
